TPU v7x, 32 devices: a whole 2x2x4 slice. The times are simulated.
32 devices in a mesh: dp: 2 (over y), row: 4 (over x, core), col: 4 (over z).
Axes of the slice: x: 2, y: 2, z: 4, core: 2. Of those that a mesh axis runs over, the one named last changes fastest.
Arguments:
- inputs: bfloat16 [2, 8192, 1024], P('dp', None, ('row', 'col')), may hold values from -6 to 6
- segments: int32 [2, 8192], P('dp'), may hold values from 0 to 7, never falling along the last dimension, each value on 1 to 2000 neighbouring positions
- cotangent: bfloat16 [2, 8192, 1024], P('dp', None, ('row', 'col')), may hold values from -6 to 6
- pregain: bfloat16 [1024], P(('row', 'col')), may hold values from 0.5 to 1.5
- innerweight: bfloat16 [1024, 32, 128], P('row', 'col'), may hold values from -0.1875 to 0.1875
- rateweight: bfloat16 [1024, 32], P('row', 'col'), may hold values from -0.1875 to 0.1875
- stateweight: bfloat16 [1024, 256], P(('row', 'col')), may hold values from -0.1875 to 0.1875
- innerconv: bfloat16 [5, 32, 64], P(None, ('col', 'row')), may hold values from -3 to 3
- stateconv: bfloat16 [5, 256], replicated, may hold values from -3 to 3
- headparams: bfloat16 [3, 32], P(None, ('col', 'row')), may hold values from -6.91 to 2.5, as said below
- postgain: bfloat16 [32, 64], P(('col', 'row')), may hold values from 0.5 to 1.5
- outweight: bfloat16 [32, 64, 1024], P('col', None, 'row'), may hold values from -0.125 to 0.125
- moment_pregain: float32 [1024], P(('row', 'col')), may hold values from -640 to 640
- square_pregain: float32 [1024], P(('row', 'col')), may hold values from 2500 to 40000
- moment_innerweight: float32 [1024, 32, 128], P('row', 'col'), may hold values from -640 to 640
- square_innerweight: float32 [1024, 32, 128], P('row', 'col'), may hold values from 2500 to 40000
- moment_rateweight: float32 [1024, 32], P('row', 'col'), may hold values from -640 to 640
- square_rateweight: float32 [1024, 32], P('row', 'col'), may hold values from 2500 to 40000
- moment_stateweight: float32 [1024, 256], P(('row', 'col')), may hold values from -640 to 640
- square_stateweight: float32 [1024, 256], P(('row', 'col')), may hold values from 2500 to 40000
- moment_innerconv: float32 [5, 32, 64], P(None, ('col', 'row')), may hold values from -640 to 640
- square_innerconv: float32 [5, 32, 64], P(None, ('col', 'row')), may hold values from 2500 to 40000
- moment_stateconv: float32 [5, 256], replicated, may hold values from -640 to 640
- square_stateconv: float32 [5, 256], replicated, may hold values from 2500 to 40000
- moment_headparams: float32 [3, 32], P(None, ('col', 'row')), may hold values from -1792 to 1792
- square_headparams: float32 [3, 32], P(None, ('col', 'row')), may hold values from 22500 to 360000
- moment_postgain: float32 [32, 64], P(('col', 'row')), may hold values from -640 to 640
- square_postgain: float32 [32, 64], P(('col', 'row')), may hold values from 2500 to 40000
- moment_outweight: float32 [32, 64, 1024], P('col', None, 'row'), may hold values from -896 to 896
- square_outweight: float32 [32, 64, 1024], P('col', None, 'row'), may hold values from 5600 to 90000
Outputs:
- result: float32 [2, 8192, 1024], P('dp', None, ('row', 'col'))
- grad_input: float32 [2, 8192, 1024], P('dp', None, ('row', 'col'))
- grad_pregain: float32 [1024], P(('row', 'col'))
- first_pregain: float32 [1024], P(('row', 'col'))
- second_pregain: float32 [1024], P(('row', 'col'))
- delta_pregain: float32 [1024], P(('row', 'col'))
- grad_innerweight: float32 [1024, 32, 128], P('row', 'col')
- first_innerweight: float32 [1024, 32, 128], P('row', 'col')
- second_innerweight: float32 [1024, 32, 128], P('row', 'col')
- delta_innerweight: float32 [1024, 32, 128], P('row', 'col')
- grad_rateweight: float32 [1024, 32], P('row', 'col')
- first_rateweight: float32 [1024, 32], P('row', 'col')
- second_rateweight: float32 [1024, 32], P('row', 'col')
- delta_rateweight: float32 [1024, 32], P('row', 'col')
- grad_stateweight: float32 [1024, 256], P(('row', 'col'))
- first_stateweight: float32 [1024, 256], P(('row', 'col'))
- second_stateweight: float32 [1024, 256], P(('row', 'col'))
- delta_stateweight: float32 [1024, 256], P(('row', 'col'))
- grad_innerconv: float32 [5, 32, 64], P(None, ('col', 'row'))
- first_innerconv: float32 [5, 32, 64], P(None, ('col', 'row'))
- second_innerconv: float32 [5, 32, 64], P(None, ('col', 'row'))
- delta_innerconv: float32 [5, 32, 64], P(None, ('col', 'row'))
- grad_stateconv: float32 [5, 256], replicated
- first_stateconv: float32 [5, 256], replicated
- second_stateconv: float32 [5, 256], replicated
- delta_stateconv: float32 [5, 256], replicated
- grad_headparams: float32 [3, 32], P(None, ('col', 'row'))
- first_headparams: float32 [3, 32], P(None, ('col', 'row'))
- second_headparams: float32 [3, 32], P(None, ('col', 'row'))
- delta_headparams: float32 [3, 32], P(None, ('col', 'row'))
- grad_postgain: float32 [32, 64], P(('col', 'row'))
- first_postgain: float32 [32, 64], P(('col', 'row'))
- second_postgain: float32 [32, 64], P(('col', 'row'))
- delta_postgain: float32 [32, 64], P(('col', 'row'))
- grad_outweight: float32 [32, 64, 1024], P('col', None, 'row')
- first_outweight: float32 [32, 64, 1024], P('col', None, 'row')
- second_outweight: float32 [32, 64, 1024], P('col', None, 'row')
- delta_outweight: float32 [32, 64, 1024], P('col', None, 'row')
Inputs may be any that keep to these rules, and one draw needn't show every extreme that they name: `segments`: in every sequence the document numbers never fall; each of the 8 documents holds 1 to 2000 tokens and one holds exactly 2000. `headparams`: row 0 lies in 0 to 2.5, row 1 in -6.91 to -2.25, row 2 in 0.5 to 1.5.
All inputs are finite; a program needn't handle non-finite values.
Results may differ from a plain program's by a relative error of at most 0.01.
Values may be sent and summed in bfloat16 or wider, within the bound.
A program may use at most 320 MiB of HBM per device.

v0:
```python
import jax
import jax.numpy as jnp
from jax import lax
from jax.sharding import PartitionSpec as P

D = 1024
HEADS = 32
HEADP = 64
GROUP = 256
STEP = 4


EXACT_PRECISION = lax.Precision.HIGHEST
NORM_EPSILON = 1e-05
ADAM_EPSILON = 1e-08
BETA_FIRST = 0.5
BETA_SECOND = 0.5
LEARN_RATE = 0.02
WEIGHT_DECAY = 0.1


def shifted(values, offset):
    padding = jnp.zeros_like(values[:, :offset])
    return jnp.concatenate([padding, values[:, :-offset]], axis=1)


def conv_mix(values, kernel, segments):
    extra = (1,) * (values.ndim - 2)
    last_row = kernel.shape[0] - 1
    total = values * kernel[0] + kernel[last_row]
    for offset in range(1, last_row):
        earlier = shifted(values, offset)
        seg_prev = jnp.concatenate(
            [jnp.full_like(segments[:, :offset], -1), segments[:, :-offset]], axis=1
        )
        same_doc = (seg_prev == segments).reshape(segments.shape + extra)
        total = total + jnp.where(same_doc, earlier, 0.0) * kernel[offset]
    return total


def scan_sequence(pieces):
    values, rates, log_decay, bvalues, cvalues, segrow = pieces
    length = values.shape[0]
    head_count = values.shape[1]
    head_width = values.shape[2]
    nstate = bvalues.shape[1]
    blocks = length // GROUP
    blocked = values.reshape(blocks, GROUP, head_count, head_width)
    rate_blocks = rates.reshape(blocks, GROUP, head_count)
    cumulative = jnp.cumsum(log_decay.reshape(blocks, GROUP, head_count), axis=1)
    bblocks = bvalues.reshape(blocks, GROUP, nstate)
    cblocks = cvalues.reshape(blocks, GROUP, nstate)
    seg_blocks = segrow.reshape(blocks, GROUP)
    rowpos = lax.broadcasted_iota(jnp.int32, (GROUP, GROUP), 0)
    colpos = lax.broadcasted_iota(jnp.int32, (GROUP, GROUP), 1)
    same_doc = (seg_blocks[:, :, None] == seg_blocks[:, None, :]) & (colpos <= rowpos)
    cum_heads = jnp.swapaxes(cumulative, 1, 2)
    differ = cum_heads[:, :, :, None] - cum_heads[:, :, None, :]
    doc_mask = same_doc[:, None]
    decays = jnp.where(doc_mask, jnp.exp(jnp.where(doc_mask, differ, 0.0)), 0.0)
    scores = jnp.einsum("btn,bsn->bts", cblocks, bblocks, precision=EXACT_PRECISION)
    weights = scores[:, None] * decays * jnp.swapaxes(rate_blocks, 1, 2)[:, :, None, :]
    inner_out = jnp.einsum("bhts,bshp->bthp", weights, blocked, precision=EXACT_PRECISION)
    last_cum = cumulative[:, -1]
    last_seg = seg_blocks[:, -1]
    to_end = (
        jnp.exp(last_cum[:, None, :] - cumulative)
        * (seg_blocks == last_seg[:, None])[:, :, None]
        * rate_blocks
    )
    local_state = jnp.einsum(
        "bsh,bsn,bshp->bhnp", to_end, bblocks, blocked, precision=EXACT_PRECISION
    )
    prev_seg = jnp.concatenate([jnp.full((1,), -1, jnp.int32), last_seg[:-1]])
    carry_gain = jnp.where((last_seg == prev_seg)[:, None], jnp.exp(last_cum), 0.0)

    def advance(carried, parts):
        gain_now, local_now = parts
        return (gain_now[:, None, None] * carried + local_now, carried)

    start = jnp.zeros((head_count, nstate, head_width), values.dtype)
    _, entering = lax.scan(advance, start, (carry_gain, local_state))
    keep_tok = seg_blocks == prev_seg[:, None]
    factor = jnp.where(keep_tok[:, :, None], jnp.exp(cumulative), 0.0)
    outer_out = (
        jnp.einsum("btn,bhnp->bthp", cblocks, entering, precision=EXACT_PRECISION)
        * factor[..., None]
    )
    return (inner_out + outer_out).reshape(length, head_count, head_width)


def mixer(innerproj, ratein, statein, innerconv, stateconv, headparams, segments):
    half = innerproj.shape[-1] // 2
    gatez = innerproj[..., :half]
    preact = innerproj[..., half:]
    values = jax.nn.silu(conv_mix(preact, innerconv, segments))
    states = jax.nn.silu(conv_mix(statein, stateconv, segments))
    nstate = states.shape[-1] // 2
    bvalues = states[..., :nstate]
    cvalues = states[..., nstate:]
    rates = jax.nn.softplus(ratein + headparams[1])
    log_decay = -jnp.exp(headparams[0]) * rates
    scanned = lax.map(
        jax.checkpoint(scan_sequence), (values, rates, log_decay, bvalues, cvalues, segments)
    )
    mixed = scanned + headparams[2][:, None] * values
    return mixed * jax.nn.silu(gatez)


def adamw_step(grad, moment, square, weight):
    first_new = BETA_FIRST * moment + (1.0 - BETA_FIRST) * grad
    second_new = BETA_SECOND * square + (1.0 - BETA_SECOND) * grad * grad
    fix_first = 1.0 - BETA_FIRST**STEP
    fix_second = 1.0 - BETA_SECOND**STEP
    delta = -LEARN_RATE * (
        first_new / fix_first / (jnp.sqrt(second_new / fix_second) + ADAM_EPSILON)
        + WEIGHT_DECAY * weight
    )
    return (first_new, second_new, delta)


def local(
    inputs,
    segments,
    cotangent,
    pregain,
    innerweight,
    rateweight,
    stateweight,
    innerconv,
    stateconv,
    headparams,
    postgain,
    outweight,
    moment_pregain,
    square_pregain,
    moment_innerweight,
    square_innerweight,
    moment_rateweight,
    square_rateweight,
    moment_stateweight,
    square_stateweight,
    moment_innerconv,
    square_innerconv,
    moment_stateconv,
    square_stateconv,
    moment_headparams,
    square_headparams,
    moment_postgain,
    square_postgain,
    moment_outweight,
    square_outweight,
):
    single_float = jnp.float32
    bf16 = jnp.bfloat16
    col_index = lax.axis_index("col")
    ownwidth = inputs.shape[2]
    count = HEADS * HEADP
    gathered, gain_rows, cotangent_row_block = (
        lax.all_gather(inputs, "col", axis=2, tiled=True),
        lax.all_gather(pregain, "col", axis=0, tiled=True),
        lax.all_gather(cotangent, "col", axis=2, tiled=True),
    )
    inputs_f = inputs.astype(single_float)
    normalized_rows = (gathered.astype(single_float) * gain_rows.astype(single_float)).astype(bf16)
    normalized_local_rows = lax.dynamic_slice_in_dim(
        normalized_rows, col_index * ownwidth, ownwidth, 2
    )
    inner_piece = jnp.einsum(
        "yjz,zxa->yjxa", normalized_rows, innerweight, preferred_element_type=single_float
    )
    rate_piece = jnp.einsum(
        "jvo,og->jvg", normalized_rows, rateweight, preferred_element_type=single_float
    )
    inner_unprocessed, rate_unprocessed = (
        lax.psum_scatter(inner_piece, "row", scatter_dimension=2, tiled=True),
        lax.psum_scatter(rate_piece, "row", scatter_dimension=2, tiled=True),
    )
    state_piece = jnp.einsum(
        "jph,hv->jpv", normalized_local_rows, stateweight, preferred_element_type=single_float
    )
    square_part = jnp.sum(inputs_f * inputs_f, axis=2)
    state_unprocessed, square_sum = lax.psum((state_piece, square_part), ("row", "col"))
    rootinv = lax.rsqrt(square_sum / D + NORM_EPSILON)
    innerproj = rootinv[..., None, None] * inner_unprocessed
    ratein = rootinv[..., None] * rate_unprocessed
    statein = (rootinv[..., None] * state_unprocessed).astype(bf16)

    def piece(inner_in, rate_in, state_in, iconv, sconv, hparams):
        return mixer(inner_in, rate_in, state_in, iconv, sconv, hparams, segments)

    gated, pullback = jax.vjp(
        piece,
        innerproj,
        ratein,
        statein.astype(single_float),
        innerconv.astype(single_float),
        stateconv.astype(single_float),
        headparams.astype(single_float),
    )
    gate_square = lax.psum(jnp.sum(gated * gated, axis=(2, 3)), ("row", "col"))
    rootgate = lax.rsqrt(gate_square / count + NORM_EPSILON)
    post_f = postgain.astype(single_float)
    norm_output_rows = (gated * rootgate[..., None, None] * post_f).astype(bf16)
    head_column_block = lax.all_gather(norm_output_rows, "row", axis=2, tiled=True)
    output_piece = jnp.einsum(
        "ktmz,mzv->ktv", head_column_block, outweight, preferred_element_type=single_float
    )
    out_sum = lax.psum_scatter(output_piece, "col", scatter_dimension=2, tiled=True)
    result = inputs_f + out_sum
    output_weight_gradient = jnp.einsum(
        "ifyb,ifr->ybr", head_column_block, cotangent_row_block, preferred_element_type=single_float
    )
    output_gradient_piece = jnp.einsum(
        "mce,tye->mcty", cotangent_row_block, outweight, preferred_element_type=single_float
    )
    dnormout = lax.psum_scatter(output_gradient_piece, "row", scatter_dimension=2, tiled=True)
    grad_post = jnp.sum(dnormout * gated * rootgate[..., None, None], axis=(0, 1))
    scaled = dnormout * post_f
    gate_dot = lax.psum(jnp.sum(scaled * gated, axis=(2, 3)), ("row", "col"))
    dgated = (
        rootgate[..., None, None] * scaled
        - gated * (rootgate * rootgate * rootgate * gate_dot / count)[..., None, None]
    )
    d_inner, d_rate, d_state, d_iconv, d_sconv, d_head = pullback(dgated)
    inner_low = (rootinv[..., None, None] * d_inner).astype(bf16)
    rate_low = (rootinv[..., None] * d_rate).astype(bf16)
    root_part = jnp.sum(d_inner * inner_unprocessed, axis=(2, 3)) + jnp.sum(
        d_rate * rate_unprocessed, axis=2
    )
    state_total, root_total, sconv_total = lax.psum((d_state, root_part, d_sconv), ("row", "col"))
    droot = root_total + jnp.sum(state_total * state_unprocessed, axis=2)
    state_lowpass = (rootinv[..., None] * state_total).astype(bf16)
    inner_gradient_list, rate_gradient_list = (
        lax.all_gather(inner_low, "row", axis=2, tiled=True),
        lax.all_gather(rate_low, "row", axis=2, tiled=True),
    )
    inner_gradient = jnp.einsum(
        "gaw,garf->wrf", normalized_rows, inner_gradient_list, preferred_element_type=single_float
    )
    rate_gradient = jnp.einsum(
        "kng,knm->gm", normalized_rows, rate_gradient_list, preferred_element_type=single_float
    )
    state_gradient = jnp.einsum(
        "pby,pbt->yt", normalized_local_rows, state_lowpass, preferred_element_type=single_float
    )
    norm_gradient_piece = jnp.einsum(
        "mxtp,rtp->mxr", inner_gradient_list, innerweight, preferred_element_type=single_float
    )
    norm_gradient_piece = norm_gradient_piece + jnp.einsum(
        "yat,ot->yao", rate_gradient_list, rateweight, preferred_element_type=single_float
    )
    dnormed = lax.psum_scatter(norm_gradient_piece, "col", scatter_dimension=2, tiled=True)
    dnormed = dnormed + jnp.einsum(
        "ufw,ow->ufo", state_lowpass, stateweight, preferred_element_type=single_float
    )
    gain_f = pregain.astype(single_float)
    grad_pre = jnp.sum(dnormed * inputs_f, axis=(0, 1))
    grad_input = (
        cotangent.astype(single_float)
        + dnormed * gain_f
        - inputs_f * (droot * rootinv * rootinv * rootinv / D)[..., None]
    )
    summed = lax.psum(
        (
            grad_pre,
            inner_gradient,
            rate_gradient,
            state_gradient,
            d_iconv,
            sconv_total,
            d_head,
            grad_post,
            output_weight_gradient,
        ),
        "dp",
    )
    params = (
        pregain,
        innerweight,
        rateweight,
        stateweight,
        innerconv,
        stateconv,
        headparams,
        postgain,
        outweight,
    )
    moments = (
        moment_pregain,
        moment_innerweight,
        moment_rateweight,
        moment_stateweight,
        moment_innerconv,
        moment_stateconv,
        moment_headparams,
        moment_postgain,
        moment_outweight,
    )
    squares = (
        square_pregain,
        square_innerweight,
        square_rateweight,
        square_stateweight,
        square_innerconv,
        square_stateconv,
        square_headparams,
        square_postgain,
        square_outweight,
    )
    outputs = [result, grad_input]
    for position in range(9):
        first_new, second_new, delta = adamw_step(
            summed[position],
            moments[position],
            squares[position],
            params[position].astype(single_float),
        )
        outputs = outputs + [summed[position], first_new, second_new, delta]
    return tuple(outputs)


def solution(mesh):
    return jax.shard_map(
        local,
        mesh=mesh,
        in_specs=(
            P("dp", None, ("row", "col")),
            P("dp", None),
            P("dp", None, ("row", "col")),
            P(("row", "col")),
            P("row", "col", None),
            P("row", "col"),
            P(("row", "col"), None),
            P(None, ("col", "row"), None),
            P(),
            P(None, ("col", "row")),
            P(("col", "row"), None),
            P("col", None, "row"),
            P(("row", "col")),
            P(("row", "col")),
            P("row", "col", None),
            P("row", "col", None),
            P("row", "col"),
            P("row", "col"),
            P(("row", "col"), None),
            P(("row", "col"), None),
            P(None, ("col", "row"), None),
            P(None, ("col", "row"), None),
            P(),
            P(),
            P(None, ("col", "row")),
            P(None, ("col", "row")),
            P(("col", "row"), None),
            P(("col", "row"), None),
            P("col", None, "row"),
            P("col", None, "row"),
        ),
        out_specs=(
            P("dp", None, ("row", "col")),
            P("dp", None, ("row", "col")),
            P(("row", "col")),
            P(("row", "col")),
            P(("row", "col")),
            P(("row", "col")),
            P("row", "col", None),
            P("row", "col", None),
            P("row", "col", None),
            P("row", "col", None),
            P("row", "col"),
            P("row", "col"),
            P("row", "col"),
            P("row", "col"),
            P(("row", "col"), None),
            P(("row", "col"), None),
            P(("row", "col"), None),
            P(("row", "col"), None),
            P(None, ("col", "row"), None),
            P(None, ("col", "row"), None),
            P(None, ("col", "row"), None),
            P(None, ("col", "row"), None),
            P(),
            P(),
            P(),
            P(),
            P(None, ("col", "row")),
            P(None, ("col", "row")),
            P(None, ("col", "row")),
            P(None, ("col", "row")),
            P(("col", "row"), None),
            P(("col", "row"), None),
            P(("col", "row"), None),
            P(("col", "row"), None),
            P("col", None, "row"),
            P("col", None, "row"),
            P("col", None, "row"),
            P("col", None, "row"),
        ),
        check_vma=False,
    )
```

profile of v0, /device:TPU:6, one launch (start us, length us, event | category | flops | bytes accessed | tf_op | source)
XLA Modules:
  0.0 2290.4 jit_solution(14536337361802927082)
XLA Ops:
  23.8 67.8 %all-gather.5.cloned.1.call-done = bf16[1,8192,256]{1,2,0:T(8,128)(2,1)} async-done(((bf16[1,8192,64]{1,2,0:T(8,128)(2,1)}), bf16[1,8192,256]{1,2,0:T(8,128)(2,1)}) %all-gather.5.cloned.1.call-update) | async-done | bytes 4194320 | tf_op jit(solution)/shard_map/all_gather | solution.py:160
  126.5 61.5 %psum.112 = f32[1,8192]{1,0:T(1,128)S(1)} all-reduce(f32[1,8192]{1,0:T(1,128)S(1)} %bitcast.420), channel_id=1, replica_groups=mesh['dp'=2,'row'=4,'col'=4] {'row','col'}, use_global_device_ids=true, to_apply=%region_1.0 | all-reduce | flops 8192 | bytes 65536 | tf_op jit(solution)/shard_map/psum | solution.py:183
  212.4 169.2 %all-reduce.46.cloned.1.call-done = f32[1,8192,256]{2,1,0:T(8,128)} async-done(((f32[1,8192,256]{2,1,0:T(8,128)}), f32[1,8192,256]{2,1,0:T(8,128)}) %all-reduce.46.cloned.1.call-update) | async-done | bytes 8388624 | tf_op jit(solution)/shard_map/psum | solution.py:183
  429.6 185.7 %reduce-scatter.4.cloned.1.call-done = f32[1,8192,2,128]{3,1,2,0:T(8,128)} async-done(((f32[1,8192,8,128]{3,1,2,0:T(8,128)}), f32[1,8192,2,128]{3,1,2,0:T(8,128)}) %reduce-scatter.4.cloned.1.call-update) | async-done | bytes 8388624 | tf_op jit(solution)/shard_map/reduce_scatter | solution.py:176
  641.1 19.2 fusion.148
  682.1 51.7 %while.83 = (s32[]{:T(128)}, f32[2,128,64]{2,1,0:T(8,128)S(1)}, f32[32,2,128,64]{2,3,1,0:T(8,128)}, f32[32,2]{1,0:T(8,128)}, f32[32,2,128,64]{2,3,1,0:T(8,128)S(1)}, /*index=5*/s32[]{:T(128)}, s32[]{:T(128)}) while((s32[]{:T(128)}, f32[2,128,64]{2,1,0:T(8,128)S(1)}, f32[32,2,128,64]{2,3,1,0:T(8,128)}, f32[32,2]{1,0:T(8,128)}, ...), condition=%wide.region_8.9_spmd.clone, body=%wide.region_7.8_spmd.clone.sunk | while | flops 49155 | bytes 786563 | solution.py:82
  741.1 24.4 %bitcast_add_fusion.8 = f32[32,256,2,64]{1,3,2,0:T(8,128)} fusion(f32[32,256,2,64]{1,3,2,0:T(8,128)S(1)} %bitcast.385, f32[32,256,2,64]{1,3,2,0:T(8,128)S(1)} %copy-done.19, f32[32,2,256]{2,1,0:T(2,128)S(1)} %bitcast.398, f32[32,2,256]{2,1,0:T(2,128)S(1)} %reshape.781, f32[32,256,256]{2,1,0:T(8,128)} %fusion.168, pred[32,256,256]{2,1,0:T(8,128)(4,1)S(1)} %copy-done.31, ...), kind=kOutput, calls=%fused_computation.145 | convolution fusion | flops 3244294144 | bytes 23265280 | tf_op jit(solution)/shard_map/jvp()/while/body/eval_jaxpr/bhts,bshp->bthp/dot_general | solution.py:63
  786.6 62.9 %psum.114 = f32[1,8192]{1,0:T(1,128)S(1)} all-reduce(f32[1,8192]{1,0:T(1,128)S(1)} %bitcast.421), channel_id=1, replica_groups=mesh['dp'=2,'row'=4,'col'=4] {'row','col'}, use_global_device_ids=true, to_apply=%region_10.11 | all-reduce | flops 8192 | bytes 65536 | tf_op jit(solution)/shard_map/psum | solution.py:201
  858.7 61.3 %psum.115 = f32[1,8192]{1,0:T(1,128)S(1)} all-reduce(f32[1,8192]{1,0:T(1,128)S(1)} %bitcast.416), channel_id=1, replica_groups=mesh['dp'=2,'row'=4,'col'=4] {'row','col'}, use_global_device_ids=true, to_apply=%region_14.15 | all-reduce | flops 8192 | bytes 65536 | tf_op jit(solution)/shard_map/psum | solution.py:220
  920.1 22.1 multiply_reduce_fusion.4
  975.9 32.5 %fusion.26 = (f32[32,2,256]{2,1,0:T(2,128)}, f32[32,2,256]{2,1,0:T(2,128)}, f32[32,2,256]{2,1,0:T(2,128)}, f32[32,256,256]{2,1,0:T(8,128)S(1)}) fusion(f32[32,2,256]{2,1,0:T(2,128)} %bitcast.399, f32[32,2,256]{2,1,0:T(2,128)} %reshape.782, f32[32,256,256]{2,1,0:T(8,128)} %fusion.170, pred[32,256,256]{2,1,0:T(8,128)(4,1)} %compare_and_fusion, ...), kind=kOutput, calls=%fused_computation.52 | convolution fusion | flops 3281993728 | bytes 27590656 | tf_op jit(solution)/shard_map/transpose(jvp())/while/body/eval_jaxpr/checkpoint/bhts,bshp->bthp/dot_general | solution.py:63
  1049.5 45.5 %while.84 = (s32[]{:T(128)}, f32[2,128,64]{2,1,0:T(8,128)S(1)}, f32[32,2,128,64]{3,2,1,0:T(8,128)}, f32[32,2,1,1]{1,3,2,0:T(1,128)}, f32[32,2]{1,0:T(8,128)S(1)}...) while((s32[]{:T(128)}, f32[2,128,64]{2,1,0:T(8,128)S(1)}, ...), condition=%wide.region_18.19_spmd.clone, body=%wide.region_17.18_spmd.clone.sunk | while | flops 65539 | bytes 656024 | solution.py:82
  1105.4 80.3 %while.85 = (s32[]{:T(128)}, f32[2,128,64]{2,1,0:T(8,128)S(1)}, f32[32,2]{1,0:T(8,128)S(1)}, f32[32,2,128,64]{3,2,1,0:T(8,128)}, f32[32,2,128,64]{2,3,1,0:T(8,12...) while((s32[]{:T(128)}, f32[2,128,64]{2,1,0:T(8,128)S(1)}, ...), condition=%wide.region_21.22_spmd.clone, body=%wide.region_19.21_spmd.clone.sunk | while | flops 98306 | bytes 721096 | solution.py:82
  1213.3 16.8 bitcast_add_fusion.6
  1261.2 17.0 bitcast_add_fusion.7
  1305.5 19.0 multiply_reduce_fusion.12
  1382.9 18.3 copy.537
  1435.3 70.8 %all-reduce.48.cloned.1.call-done = f32[1,8192,256]{2,1,0:T(8,128)} async-done(((f32[1,8192,256]{2,1,0:T(8,128)}), f32[1,8192,256]{2,1,0:T(8,128)}) %all-reduce.48.cloned.1.call-update) | async-done | bytes 8388624 | tf_op jit(solution)/shard_map/psum | solution.py:231
  1519.4 93.1 %all-gather.11.cloned.1.call-done = bf16[1,8192,8,128]{3,1,0,2:T(8,128)(2,1)} async-done(((bf16[1,8192,2,128]{3,1,0,2:T(8,128)(2,1)}), bf16[1,8192,8,128]{3,1,0,2:T(8,128)(2,1)}) %all-gather.11.cloned.1.call-update) | async-done | bytes 16777232 | tf_op jit(solution)/shard_map/all_gather | solution.py:235
  1643.7 18.0 copy.570
  1665.0 68.3 %all-reduce.36 = (f32[1,8192]{1,0:T(1,128)S(1)}, f32[5,256]{1,0:T(8,128)}) all-reduce(f32[1,8192]{1,0:T(1,128)S(1)} %bitcast.419, f32[5,256]{1,0:T(8,128)S(1)} %pad_add_fusion.1), channel_id=1, replica_groups=mesh['dp'=2,'row'=4,'col'=4] {'row','col'}, use_global_device_ids=true, to_apply=%region_34.35 | all-reduce | flops 9472 | bytes 75776 | tf_op jit(solution)/shard_map/psum | solution.py:231
  1745.6 163.5 %all-reduce.52.cloned.1.call-done = f32[1,8192,256]{1,0,2:T(1,128)} async-done(((f32[1,8192,256]{1,0,2:T(1,128)}), f32[1,8192,256]{1,0,2:T(1,128)}) %all-reduce.52.cloned.1.call-update) | async-done | bytes 8388624
  1910.9 52.9 %all-reduce.56.cloned.1.call-done = (f32[256,8,128]{2,0,1:T(8,128)}, f32[64,256]{1,0:T(8,128)}, f32[8,64,256]{2,1,0:T(8,128)}) async-done(((f32[256,8,128]{2,0,1:T(8,128)}, f32[64,256]{1,0:T(8,128)}, f32[8,64,256]{2,1,0:T(8,128)}), (f32[256,8,128]{2,0,1:T(8,128)}, f32[64,256]{1,0:T(8,128)}, f32[8,64,256]{2,1,0:T(8,128)})) %all-reduce.56.cloned.1.call-update) | async-done | bytes 1638416 | tf_op jit(solution)/shard_map/psum | solution.py:264
  1976.3 281.6 %all-reduce.54.cloned.1.call-done = f32[1,8192,256]{1,0,2:T(1,128)} async-done(((f32[1,8192,256]{1,0,2:T(1,128)}), f32[1,8192,256]{1,0,2:T(1,128)}) %all-reduce.54.cloned.1.call-update) | async-done | bytes 8388624
  (1086 shorter events, 742.8 us)
Async XLA Ops:
  7.2 84.4 %all-gather.5.cloned.1.call-start = ((), (), s32[]{:S(2)}) async-start(), calls=%async_computation.2 | async-start | bytes 5242880 | tf_op jit(solution)/shard_map/all_gather | solution.py:160
  8.0 184.0 %all-gather.9.cloned.1.call-start = ((), (), s32[]{:S(2)}) async-start(), calls=%async_computation.6 | async-start | bytes 5242880 | tf_op jit(solution)/shard_map/all_gather | solution.py:162
  8.7 199.0 %all-reduce.50.cloned.1.call-start = ((), (), s32[]{:S(2)}) async-start(), calls=%async_computation.10 | async-start | bytes 524288
  98.3 283.3 %all-reduce.46.cloned.1.call-start = ((), (), s32[]{:S(2)}) async-start(), calls=%async_computation.3 | async-start | bytes 16777216 | tf_op jit(solution)/shard_map/psum | solution.py:183
  104.4 510.9 %reduce-scatter.4.cloned.1.call-start = ((), (), s32[]{:S(2)}) async-start(), calls=%async_computation.4 | async-start | bytes 41943040 | tf_op jit(solution)/shard_map/reduce_scatter | solution.py:176
  120.1 730.6 %reduce-scatter.6.cloned.1.call-start = ((), (), s32[]{:S(2)}) async-start(), calls=%async_computation.7 | async-start | bytes 41943040 | tf_op jit(solution)/shard_map/reduce_scatter | solution.py:217
  123.3 517.7 %copy-start.53 = (pred[8192]{0:T(1024)(128)(4,1)}, pred[8192]{0:T(1024)(128)(4,1)S(1)}, u32[]{:S(2)}) copy-start(pred[8192]{0:T(1024)(128)(4,1)S(1)} %get-tuple-element.891) | copy-start | bytes 24580
  123.3 517.7 %copy-start.55 = (pred[8192]{0:T(1024)(128)(4,1)}, pred[8192]{0:T(1024)(128)(4,1)S(1)}, u32[]{:S(2)}) copy-start(pred[8192]{0:T(1024)(128)(4,1)S(1)} %get-tuple-element.892) | copy-start | bytes 24580
  188.7 452.3 %copy-start.80 = (f32[2,64]{1,0:T(2,128)}, f32[2,64]{1,0:T(2,128)S(1)}, u32[]{:S(2)}) copy-start(f32[2,64]{1,0:T(2,128)S(1)} %get-tuple-element.1009) | copy-start | bytes 1540
  188.7 452.3 %copy-start.82 = (f32[2,64]{1,0:T(2,128)}, f32[2,64]{1,0:T(2,128)S(1)}, u32[]{:S(2)}) copy-start(f32[2,64]{1,0:T(2,128)S(1)} %get-tuple-element.1010) | copy-start | bytes 1540
  188.8 452.3 %copy-start.84 = (f32[2,64]{1,0:T(2,128)}, f32[2,64]{1,0:T(2,128)S(1)}, u32[]{:S(2)}) copy-start(f32[2,64]{1,0:T(2,128)S(1)} %get-tuple-element.1011) | copy-start | bytes 1540
  188.8 452.3 %copy-start.86 = (f32[2,64]{1,0:T(2,128)}, f32[2,64]{1,0:T(2,128)S(1)}, u32[]{:S(2)}) copy-start(f32[2,64]{1,0:T(2,128)S(1)} %get-tuple-element.1012) | copy-start | bytes 1540
  188.8 197.1 %copy-start.88 = (f32[1,256]{1,0:T(1,128)}, f32[1,256]{1,0:T(1,128)S(1)}, u32[]{:S(2)}) copy-start(f32[1,256]{1,0:T(1,128)S(1)} %get-tuple-element.1014) | copy-start | bytes 3076
  188.8 197.1 %copy-start.90 = (f32[1,256]{1,0:T(1,128)}, f32[1,256]{1,0:T(1,128)S(1)}, u32[]{:S(2)}) copy-start(f32[1,256]{1,0:T(1,128)S(1)} %get-tuple-element.1018) | copy-start | bytes 3076
  188.8 197.1 %copy-start.92 = (f32[1,256]{1,0:T(1,128)}, f32[1,256]{1,0:T(1,128)S(1)}, u32[]{:S(2)}) copy-start(f32[1,256]{1,0:T(1,128)S(1)} %get-tuple-element.1017) | copy-start | bytes 3076
  191.9 423.4 %copy-start.26 = (f32[1,8192]{1,0:T(1,128)}, f32[1,8192]{1,0:T(1,128)S(1)}, u32[]{:S(2)}) copy-start(f32[1,8192]{1,0:T(1,128)S(1)} %add_rsqrt_fusion.1) | copy-start | bytes 98308
  207.4 1166.4 %all-gather.7.cloned.1.call-start = ((), (), s32[]{:S(2)}) async-start(), calls=%async_computation.5 | async-start | bytes 10485760 | tf_op jit(solution)/shard_map/all_gather | solution.py:205
  208.9 532.1 %copy-start.33 = (f32[1,8192,2]{1,2,0:T(2,128)}, f32[1,8192,2]{1,2,0:T(2,128)S(1)}, u32[]{:S(2)}) copy-start(f32[1,8192,2]{1,2,0:T(2,128)S(1)} %get-tuple-element.979) | copy-start | bytes 196612
  1038.3 467.8 %all-reduce.48.cloned.1.call-start = ((), (), s32[]{:S(2)}) async-start(), calls=%async_computation.9 | async-start | bytes 16777216 | tf_op jit(solution)/shard_map/psum | solution.py:231
  1337.7 274.8 %all-gather.11.cloned.1.call-start = ((), (), s32[]{:S(2)}) async-start(), calls=%async_computation.8 | async-start | bytes 20971520 | tf_op jit(solution)/shard_map/all_gather | solution.py:235
  1373.7 535.4 %all-reduce.52.cloned.1.call-start = ((), (), s32[]{:S(2)}) async-start(), calls=%async_computation.11 | async-start | bytes 16777216
  1401.2 562.6 %all-reduce.56.cloned.1.call-start = ((), (), s32[]{:S(2)}) async-start(), calls=%async_computation.13 | async-start | bytes 3276800 | tf_op jit(solution)/shard_map/psum | solution.py:264
  1625.0 632.9 %all-reduce.54.cloned.1.call-start = ((), (), s32[]{:S(2)}) async-start(), calls=%async_computation.12 | async-start | bytes 16777216
  1969.4 290.2 %copy-start.24 = (bf16[1,8192,64]{1,2,0:T(8,128)(2,1)S(1)}, bf16[1,8192,64]{1,2,0:T(8,128)(2,1)}, u32[]{:S(2)}) copy-start(bf16[1,8192,64]{1,2,0:T(8,128)(2,1)} %param.36) | copy-start | bytes 3145732
  (137 other events, 2360.4 us)
Sparse Core Ops, SparseCore 0:
  9.6 81.9 all-gather.4
  93.2 80.9 all-gather.8
  177.1 29.6 all-reduce.49
  210.4 171.1 all-reduce.45
  384.0 231.2 reduce-scatter.3
  617.7 232.9 reduce-scatter.5
  1038.4 55.4 all-gather.6
  1337.9 168.2 all-reduce.47
  1507.7 104.8 all-gather.10
  1614.8 294.2 all-reduce.51
  1912.7 51.0 all-reduce.55
  1966.1 291.7 all-reduce.53
where the time goes:
time: 2300 us; the launch traced here: 2290 us
  waiting for transfers between devices  1090 us (47%)
  other arithmetic  337 us (15%)
  matrix products  303 us (13%)
  blocking collectives  279 us (12%)
  local copies, waits for them, and re-layouts  262 us (11%)
    unnamed x15, waiting for transfers between devices  447 us
    reduce_scatter x1, waiting for transfers between devices, local(): lax.psum_scatter(inner_piece, 'row', scatter_dimension=2, tiled=True)  186 us
    psum x1, waiting for transfers between devices, local(): lax.psum((state_piece, square_part), ('row', 'col'))  169 us
    all_gather x1, waiting for transfers between devices, local(): lax.all_gather(inner_low, 'row', axis=2, tiled=True)  93.1 us
    dot_general x3, matrix products, scan_sequence(): jnp.einsum('bhts,bshp->bthp', weights, blocked, precision=EXACT_PRECISION)  73.9 us
    psum x1, waiting for transfers between devices, local(): lax.psum((d_state, root_part, d_sconv), ('row', 'col'))  70.8 us
    psum x1, blocking collectives, local(): lax.psum((d_state, root_part, d_sconv), ('row', 'col'))  68.3 us
    all_gather x1, waiting for transfers between devices, local(): lax.all_gather(inputs, 'col', axis=2, tiled=True)  67.8 us
  transfers between devices with their start and end apart: 12, of which 9 were waited for; matrix products, arithmetic and copies ran while one was open for 32% of the time, Pallas kernels for 0%

commit v1 on v0

v1 whole, which is shorter than its diff:
```python
import functools

import jax
import jax.numpy as jnp
from jax import lax
from jax.experimental import pallas as pl
from jax.experimental.pallas import tpu as pltpu
from jax.sharding import PartitionSpec as P

HEADP = 64
NSTATE = 128
GROUP = 256
MOST = 2000
STEP = 4
HALO = 16
NORM_EPSILON = 1e-05
ADAM_EPSILON = 1e-08
BETA_FIRST = 0.5
BETA_SECOND = 0.5
LEARN_RATE = 0.02
WEIGHT_DECAY = 0.1
FAR = -1e30

F32 = jnp.float32
BF16 = jnp.bfloat16


def dot(a, b, ca, cb):
    return lax.dot_general(a, b, (((ca,), (cb,)), ((), ())), preferred_element_type=F32)


def mm(a, b):
    return dot(a, b, 1, 0)


def mm_nt(a, b):
    return dot(a, b, 1, 1)


def mm_tn(a, b):
    return dot(a, b, 0, 0)


def sigmoid(v):
    return 0.5 * jnp.tanh(0.5 * v) + 0.5


def halves(v):
    high = v.astype(BF16)
    return high, (v - high.astype(F32)).astype(BF16)


def stack_parts(v, count):
    parts = []
    for _ in range(count):
        high = v.astype(BF16).astype(F32)
        parts.append(high)
        v = v - high
    return parts


def expand(rows, spread):
    high, low = stack_parts(rows, 2)
    return mm_tn(jnp.concatenate([high, low], 0).astype(BF16), spread)


def head_sums(v, spread):
    high, low = halves(v)
    sums = mm_nt(spread, high) + mm_nt(spread, low)
    return sums[: sums.shape[0] // 2]


def lane_sums(v):
    total = v[:, :128]
    for at in range(128, v.shape[1], 128):
        total = total + v[:, at : at + 128]
    high, low = halves(total)
    return mm_nt(jnp.ones((16, 256), BF16), jnp.concatenate([high, low], 1))[:8]


def running(rows, triangle, product=mm):
    count = rows.shape[0]
    parts = stack_parts(rows, 3) + [jnp.zeros_like(rows)]
    sums = product(jnp.concatenate(parts, 0).astype(BF16), triangle)
    return sums[:count] + sums[count : 2 * count] + sums[2 * count : 3 * count]


def softplus(v):
    return jnp.maximum(v, 0.0) + jnp.log1p(jnp.exp(-jnp.abs(v)))


def row_norm(xs, width):
    total = None
    for xf in xs:
        part = jnp.sum(xf * xf, axis=1, keepdims=True)
        total = part if total is None else total + part
    return lax.rsqrt(total / width + NORM_EPSILON)


def chunk_decay(cum, rates, tok):
    last = cum[:, GROUP - 1 : GROUP]
    tail = (tok[0:1] == tok[0:1, GROUP - 1 : GROUP]).astype(F32)
    to_end = jnp.exp(last - cum) * tail
    enter = jnp.exp(cum) * tok[7:8]
    return to_end, enter


def fwd1_kernel(
    x_ref, xh_ref, gain_ref, wmain_ref, wstate_ref, wrate_ref, tok_ref, head_ref,
    kin_ref, kst_ref, tri_ref, spread_ref,
    gate_ref, pre_ref, st_ref, uv_ref, us_ref, bc_ref, rows_ref, sent_ref, prod_ref, fin_ref, total_ref, preh_ref, sth_ref, rinvh_ref,
    ext, state, prod,
):
    k = pl.program_id(0)
    blocks, _, depth = x_ref.shape
    width = blocks * depth
    hl = gate_ref.shape[1]
    heads = hl // HEADP

    def project(xs):
        xf = [v.astype(F32) for v in xs]
        rinv = row_norm(xf, width)
        xn = [
            (v * gain_ref[:, i * depth : (i + 1) * depth]).astype(BF16)
            for i, v in enumerate(xf)
        ]
        main = state_in = None
        for i, v in enumerate(xn):
            at = pl.ds(i * depth, depth)
            a, b = mm(v, wmain_ref[at, :]), mm(v, wstate_ref[at, :])
            main = a if main is None else main + a
            state_in = b if state_in is None else state_in + b
        return xn, rinv, main * rinv, (state_in * rinv).astype(BF16)

    @pl.when(k == 0)
    def _():
        _, rinv, main, state_in = project([xh_ref[i] for i in range(blocks)])
        pre = main[:, hl:].astype(BF16)
        preh_ref[...] = pre.astype(BF16)
        sth_ref[...] = state_in
        rinvh_ref[...] = jnp.broadcast_to(rinv, (HALO, 128))
        ext[0:8, :hl] = pre.astype(F32)[HALO - 8 :]
        ext[0:8, hl:] = state_in.astype(F32)[HALO - 8 :]
        state[...] = jnp.zeros_like(state)
        prod[...] = jnp.ones_like(prod)

    xn, rinv, main, state_in = project([x_ref[i] for i in range(blocks)])
    gate_ref[...] = main[:, :hl]
    pre = main[:, hl:]
    pre_ref[...] = pre
    st_ref[...] = state_in
    ext[8:, :hl] = pre.astype(F32)
    ext[8:, hl:] = state_in.astype(F32)
    tok = tok_ref[...]
    cols = tok.T
    kernel = jnp.concatenate([kin_ref[...], kst_ref[...]], 1)
    u = ext[8:, :] * kernel[0:1] + kernel[4:5]
    for j in range(1, 4):
        u = u + ext[pl.ds(8 - j, GROUP), :] * cols[:, j : j + 1] * kernel[j : j + 1]
    ext[0:8, :] = ext[GROUP : GROUP + 8, :]
    uv_ref[...] = u[:, :hl]
    us_ref[...] = u[:, hl:]
    u = u.astype(F32)
    act = u * sigmoid(u)
    values = act[:, :hl]
    bc = act[:, hl:].astype(BF16)
    bc_ref[...] = bc
    rate = None
    for i, v in enumerate(xn):
        part = mm_nt(wrate_ref[:, i * depth : (i + 1) * depth], v)
        rate = part if rate is None else rate + part
    rinv_row = jnp.broadcast_to(rinv, (GROUP, 128)).T[0:heads]
    rin = rate[:heads] * rinv_row + head_ref[heads : 2 * heads, 0:1]
    rates = softplus(rin)
    cum = running(head_ref[0:heads, 0:1] * rates, tri_ref[...])
    rows_ref[0:heads] = rin
    rows_ref[heads : 2 * heads] = rates
    rows_ref[2 * heads : 3 * heads] = cum
    rows_ref[3 * heads :] = rinv_row
    to_end, _ = chunk_decay(cum, rates, tok)
    both = expand(to_end * rates, spread_ref[...])
    scaled = (values * both).astype(BF16)
    carry = jnp.exp(cum[:, GROUP - 1 :]) * tok[7:8, GROUP - 1 :]
    carry = expand(jnp.broadcast_to(carry, (heads, 128)), spread_ref[...])[0:8]
    sent_ref[0] = state[...].astype(BF16)
    prod_ref[0] = prod[...]
    state[...] = state[...] * carry[0:1] + mm_tn(bc[:, :NSTATE], scaled)
    prod[...] = prod[...] * carry
    fin_ref[...] = state[...]
    total_ref[...] = prod[...]


def pair_lanes(shape):
    return lax.broadcasted_iota(jnp.int32, shape, 1) < HEADP


def chunk_mask(tok, cols):
    rowpos = lax.broadcasted_iota(jnp.int32, (GROUP, GROUP), 0)
    colpos = lax.broadcasted_iota(jnp.int32, (GROUP, GROUP), 1)
    same = (cols[:, 0:1] == tok[0:1, :]) & (colpos <= rowpos)
    return jnp.where(same, 0.0, FAR)


def fwd2_kernel(
    gate_ref, uv_ref, bc_ref, rows_ref, tok_ref, sent_ref, prod_ref, sin_ref, cot_ref, post_ref, skip_ref,
    woutt_ref, spread_ref,
    scan_ref, out_ref, dn_ref, stat_ref,
):
    hl = gate_ref.shape[1]
    heads = hl // HEADP
    blocks, _, depth = cot_ref.shape
    tok = tok_ref[...]
    cum = rows_ref[2 * heads : 3 * heads]
    rates = rows_ref[heads : 2 * heads]
    _, enter = chunk_decay(cum, rates, tok)
    spread = spread_ref[...]
    cols = jnp.concatenate([tok, cum], 0).T
    mask = chunk_mask(tok, cols)
    bm, cm = bc_ref[:, :NSTATE], bc_ref[:, NSTATE:]
    scores = mm_nt(cm, bm)
    u = uv_ref[...].astype(F32)
    values = u * sigmoid(u)
    scaled = (values * expand(rates, spread)).astype(BF16)
    entering = (sent_ref[0].astype(F32) + prod_ref[0, 0:1] * sin_ref[...]).astype(BF16)
    outer = mm(cm, entering) * expand(enter, spread)
    first = pair_lanes((GROUP, 128))
    pieces = []
    for pair in range(heads // 2):
        vp = scaled[:, pair * 128 : (pair + 1) * 128]
        ys = []
        for h in (2 * pair, 2 * pair + 1):
            decay = jnp.exp(cols[:, 8 + h : 9 + h] - cum[h : h + 1, :] + mask)
            ys.append(mm((scores * decay).astype(BF16), vp))
        pieces.append(jnp.where(first, ys[0], ys[1]))
    scan = jnp.concatenate(pieces, 1) + outer
    scan_ref[...] = scan
    g = gate_ref[...].astype(F32)
    gated = (scan + skip_ref[...] * values) * (g * sigmoid(g))
    post = post_ref[...]
    dn = None
    for i in range(blocks):
        part = mm(cot_ref[i], woutt_ref[pl.ds(i * depth, depth), :])
        dn = part if dn is None else dn + part
    dn = dn.astype(BF16)
    dn_ref[...] = dn
    normed = gated * post
    stat_ref[0:8] = lane_sums(gated * gated)
    stat_ref[8:16] = lane_sums(dn.astype(F32) * normed)
    normed = normed.astype(BF16)
    for i in range(blocks):
        out_ref[i] = mm_nt(normed, woutt_ref[pl.ds(i * depth, depth), :]).astype(BF16)


def bwd1_kernel(
    gate_ref, uv_ref, bc_ref, rows_ref, tok_ref, scan_ref, dn_ref, scal_ref, cot_ref, post_ref, skip_ref, spread_ref,
    dy_ref, dg_ref, leave_ref, prodb_ref, first_ref, gout_ref, sums_ref, root_ref,
    adj, prod,
):
    step = pl.program_id(0)
    hl = gate_ref.shape[1]
    heads = hl // HEADP
    blocks, _, depth = cot_ref.shape
    tok = tok_ref[...]
    cum = rows_ref[2 * heads : 3 * heads]
    spread = spread_ref[...]

    @pl.when(step == 0)
    def _():
        adj[...] = jnp.zeros_like(adj)
        prod[...] = jnp.ones_like(prod)
        gout_ref[...] = jnp.zeros_like(gout_ref)
        sums_ref[...] = jnp.zeros_like(sums_ref)

    enter = jnp.exp(cum) * tok[7:8]
    scal = scal_ref[...]
    cols = jnp.concatenate([scal, rows_ref[3 * heads :]], 0).T
    rootgate, pull, rinv = cols[:, 0:1], cols[:, 1:2], cols[:, 8:9]
    u = uv_ref[...].astype(F32)
    values = u * sigmoid(u)
    mixed = scan_ref[...] + skip_ref[...] * values
    g = gate_ref[...].astype(F32)
    sg = sigmoid(g)
    act = g * sg
    gated = mixed * act
    post = post_ref[...]
    dn = dn_ref[...].astype(F32)
    dgated = rootgate * (dn * post) - gated * pull
    dy = dgated * act
    dyb = dy.astype(BF16)
    dy_ref[...] = dyb
    dgate = dgated * mixed * (sg + act * (1.0 - sg)) * rinv
    dg_ref[...] = dgate.astype(BF16)
    root_ref[...] = lane_sums(dgate * g)
    ng = gated * rootgate
    sums_ref[0:8] += jnp.sum((dn * ng).reshape(GROUP // 8, 8, hl), 0)
    sums_ref[8:16] += jnp.sum((dy * values).reshape(GROUP // 8, 8, hl), 0)
    normout = (ng * post).astype(BF16)
    for i in range(blocks):
        gout_ref[pl.ds(i * depth, depth), :] += mm_tn(cot_ref[i], normout)
    cm = bc_ref[:, NSTATE:]
    weighted = (dyb.astype(F32) * expand(enter, spread)).astype(BF16)
    carry = jnp.exp(cum[:, GROUP - 1 :]) * tok[7:8, GROUP - 1 :]
    carry = expand(jnp.broadcast_to(carry, (heads, 128)), spread)[0:8]
    leave_ref[0] = adj[...].astype(BF16)
    prodb_ref[0] = prod[...]
    adj[...] = adj[...] * carry[0:1] + mm_tn(cm, weighted)
    prod[...] = prod[...] * carry
    first_ref[...] = adj[...]


def bwd2_kernel(
    x_ref, xh_ref, gain_ref, wmain_ref, wstate_ref, wrate_ref, tok_ref, head_ref, hmask_ref, hrinv_ref,
    kin_ref, kst_ref, tri_ref, spread_ref, skip_ref,
    pre_ref, st_ref, preh_ref, sth_ref, uv_ref, us_ref, bc_ref, rows_ref, sent_ref, prod_ref, sin_ref,
    scan_ref, dy_ref, dg_ref, leave_ref, prodb_ref, din_ref, root_ref,
    gin_ref, ginh_ref, gw_ref, gr_ref, gk_ref, gh_ref, gp_ref,
    ext,
):
    step = pl.program_id(0)
    steps = pl.num_programs(0)
    hl = uv_ref.shape[1]
    heads = hl // HEADP
    blocks, _, depth = x_ref.shape
    tok = tok_ref[...]
    spread = spread_ref[...]
    rin = rows_ref[0:heads]
    rates = rows_ref[heads : 2 * heads]
    cum = rows_ref[2 * heads : 3 * heads]
    rinv_row = rows_ref[3 * heads :]
    cols = jnp.concatenate([tok, cum, rinv_row], 0).T
    rinv = cols[:, 16:17]

    @pl.when(step == 0)
    def _():
        ext[GROUP:, :] = jnp.zeros_like(ext[GROUP:, :])
        gw_ref[...] = jnp.zeros_like(gw_ref)
        gr_ref[...] = jnp.zeros_like(gr_ref)
        gk_ref[...] = jnp.zeros_like(gk_ref)
        gh_ref[...] = jnp.zeros_like(gh_ref)
        gp_ref[...] = jnp.zeros_like(gp_ref)

    to_end, enter = chunk_decay(cum, rates, tok)
    mask = chunk_mask(tok, cols)
    bm, cm = bc_ref[:, :NSTATE], bc_ref[:, NSTATE:]
    scores = mm_nt(cm, bm)
    u = uv_ref[...].astype(F32)
    sg = sigmoid(u)
    values = u * sg
    rexp = expand(rates, spread)
    scaled = (values * rexp).astype(BF16)
    dyb = dy_ref[...]
    entering = (sent_ref[0].astype(F32) + prod_ref[0, 0:1] * sin_ref[...]).astype(BF16)
    leaving = (leave_ref[0].astype(F32) + prodb_ref[0, 0:1] * din_ref[...]).astype(BF16)

    first = pair_lanes((GROUP, 128))
    dscores = jnp.zeros((GROUP, GROUP), F32)
    pieces = []
    for pair in range(heads // 2):
        vp = scaled[:, pair * 128 : (pair + 1) * 128]
        dp = dyb[:, pair * 128 : (pair + 1) * 128]
        dvs = []
        for h in (2 * pair, 2 * pair + 1):
            decay = jnp.exp(cols[:, 8 + h : 9 + h] - cum[h : h + 1, :] + mask)
            weight = (scores * decay).astype(BF16)
            own = first if h % 2 == 0 else ~first
            dh = jnp.where(own, dp, jnp.zeros_like(dp))
            dscores = dscores + mm_nt(dh, vp) * decay
            dvs.append(mm_tn(weight, dp))
        pieces.append(jnp.where(first, dvs[0], dvs[1]))
    tend = expand(to_end, spread)
    inside = jnp.concatenate(pieces, 1)
    onward = mm(bm, leaving) * tend
    dscaled = inside + onward
    dsb = dscores.astype(BF16)
    dyf = dyb.astype(F32)
    weighted = (dyf * expand(enter, spread)).astype(BF16)
    ended = (values * (tend * rexp)).astype(BF16)
    dcm = mm(dsb, bm) + mm_nt(weighted, entering)
    dbm = mm_tn(dsb, cm) + mm_nt(ended, leaving)
    dvalues = dscaled * rexp + skip_ref[...] * dyf

    kept = scaled.astype(F32)
    dcum = head_sums(dyf * scan_ref[...] - kept * inside, spread)
    dend = head_sums(kept * onward, spread)
    drates = head_sums(values * dscaled, spread)
    through = leaving.astype(F32) * entering.astype(F32)
    through = head_sums(jnp.sum(through.reshape(NSTATE // 8, 8, hl), 0), spread)
    through = jnp.sum(through, axis=1, keepdims=True) * (
        jnp.exp(cum[:, GROUP - 1 :]) * tok[7:8, GROUP - 1 :]
    )
    ddec = running(dcum, tri_ref[...], mm_nt) + running(dend, tri_ref[...]) - dend + through
    drates = drates + head_ref[0:heads, 0:1] * ddec
    drin = drates * sigmoid(rin)
    gh_ref[0:heads] += ddec * (head_ref[0:heads, 0:1] * rates)
    gh_ref[heads : 2 * heads] += drin

    us = us_ref[...].astype(F32)
    ss = sigmoid(us)
    dstates = jnp.concatenate([dbm, dcm], 1)
    ext[0:GROUP, :hl] = dvalues * (sg + values * (1.0 - sg))
    ext[0:GROUP, hl:] = dstates * (ss + us * ss * (1.0 - ss))
    kernel = jnp.concatenate([kin_ref[...], kst_ref[...]], 1)
    source = jnp.concatenate([pre_ref[...], st_ref[...]], 1).astype(F32)
    du = ext[0:GROUP, :]
    gk_ref[32:40] += jnp.sum(du.reshape(GROUP // 8, 8, du.shape[1]), 0)
    gk_ref[0:8] += jnp.sum((du * source).reshape(GROUP // 8, 8, du.shape[1]), 0)
    dsource = du * kernel[0:1]
    for j in range(1, 4):
        moved = ext[pl.ds(j, GROUP), :] * cols[:, 3 + j : 4 + j]
        gk_ref[8 * j : 8 * j + 8] += jnp.sum(
            (moved * source).reshape(GROUP // 8, 8, du.shape[1]), 0
        )
        dsource = dsource + moved * kernel[j : j + 1]
    low = dsource * rinv
    lowb = low.astype(BF16)
    root = lane_sums(low * source) + root_ref[...] + jnp.sum(
        drin * (rin - head_ref[heads : 2 * heads, 0:1]), 0, keepdims=True
    ) * rinv_row[0:1]
    root = (root * rinv_row[0:1]).T[:, 0:1] / (blocks * depth)
    ratelow = (drin * rinv_row).astype(F32)
    ratelow = jnp.concatenate([ratelow, jnp.zeros_like(ratelow)], 0).astype(BF16)
    gates = dg_ref[...]
    for i in range(blocks):
        at = pl.ds(i * depth, depth)
        xf = x_ref[i].astype(F32)
        gain = gain_ref[:, i * depth : (i + 1) * depth]
        xn = (xf * gain).astype(BF16)
        gw_ref[at, 0:hl] += mm_tn(xn, gates)
        gw_ref[at, hl:] += mm_tn(xn, lowb)
        gr_ref[:, i * depth : (i + 1) * depth] += mm(ratelow, xn)
        dn = (
            mm_nt(gates, wmain_ref[at, 0:hl])
            + mm_nt(lowb[:, :hl], wmain_ref[at, hl:])
            + mm_nt(lowb[:, hl:], wstate_ref[at, :])
            + mm_tn(ratelow, wrate_ref[:, i * depth : (i + 1) * depth])
        )
        gp_ref[:, i * depth : (i + 1) * depth] += jnp.sum(
            (dn * xf).reshape(GROUP // 8, 8, depth), 0
        )
        gin_ref[i] = (dn * gain - xf * root).astype(BF16)

    ext[GROUP : GROUP + 8, :] = ext[0:8, :]

    @pl.when(step == steps - 1)
    def _():
        wide = ext.shape[1]
        source_h = jnp.concatenate([preh_ref[...], sth_ref[...]], 1).astype(F32)
        head8 = ext[GROUP : GROUP + 8, :]
        ext[0:HALO, :] = jnp.zeros((HALO, wide), F32)
        ext[HALO : HALO + 8, :] = head8
        dsource_h = jnp.zeros((HALO, wide), F32)
        for j in range(1, 4):
            moved = ext[pl.ds(j, HALO), :] * hmask_ref[:, j : j + 1]
            gk_ref[8 * j : 8 * j + 8] += jnp.sum(
                (moved * source_h).reshape(HALO // 8, 8, wide), 0
            )
            dsource_h = dsource_h + moved * kernel[j : j + 1]
        rinv_h = hrinv_ref[:, 0:1]
        low_h = dsource_h * rinv_h
        lowb_h = low_h.astype(BF16)
        root_h = jnp.sum(low_h * source_h, axis=1, keepdims=True) * rinv_h / (blocks * depth)
        for i in range(blocks):
            at = pl.ds(i * depth, depth)
            xf = xh_ref[i].astype(F32)
            gain = gain_ref[:, i * depth : (i + 1) * depth]
            xn = (xf * gain).astype(BF16)
            gw_ref[at, hl:] += mm_tn(xn, lowb_h)
            dn = mm_nt(lowb_h[:, :hl], wmain_ref[at, hl:]) + mm_nt(
                lowb_h[:, hl:], wstate_ref[at, :]
            )
            gp_ref[:, i * depth : (i + 1) * depth] += jnp.sum(
                (dn * xf).reshape(HALO // 8, 8, depth), 0
            )
            ginh_ref[i] = (dn * gain - xf * root_h).astype(BF16)


def call(kernel, steps, ins, outs, scratch, reverse, name):
    def spec(block, axis):
        def index(step):
            at = steps - 1 - step if reverse else step
            return tuple(at if a == axis else 0 for a in range(len(block)))

        return pl.BlockSpec(block, index)

    return pl.pallas_call(
        kernel,
        grid=(steps,),
        in_specs=[spec(block, axis) for _, block, axis in ins],
        out_specs=[spec(block, axis) for _, _, block, axis in outs],
        out_shape=[jax.ShapeDtypeStruct(shape, dtype) for shape, dtype, _, _ in outs],
        scratch_shapes=scratch,
        compiler_params=pltpu.CompilerParams(
            dimension_semantics=("arbitrary",), vmem_limit_bytes=60 * 1024 * 1024
        ),
        name=name,
    )(*[array for array, _, _ in ins])


def whole(array):
    return (array, array.shape, None)


def lanes(array):
    return (array, array.shape[:-1] + (GROUP,), array.ndim - 1)


def sublanes(array):
    return (array, array.shape[:-2] + (GROUP,) + array.shape[-1:], array.ndim - 2)


def each(array):
    return (array, (1,) + array.shape[1:], 0)


def out_whole(shape, dtype):
    return (shape, dtype, shape, None)


def out_sub(shape, dtype):
    return (shape, dtype, shape[:-2] + (GROUP,) + shape[-1:], len(shape) - 2)


def out_lanes(shape, dtype):
    return (shape, dtype, shape[:-1] + (GROUP,), len(shape) - 1)


def out_each(shape, dtype):
    return (shape, dtype, (1,) + shape[1:], 0)


def adamw_step(grad, moment, square, weight):
    first_new = BETA_FIRST * moment + (1.0 - BETA_FIRST) * grad
    second_new = BETA_SECOND * square + (1.0 - BETA_SECOND) * grad * grad
    fix_first = 1.0 - BETA_FIRST**STEP
    fix_second = 1.0 - BETA_SECOND**STEP
    delta = -LEARN_RATE * (
        first_new / fix_first / (jnp.sqrt(second_new / fix_second) + ADAM_EPSILON)
        + WEIGHT_DECAY * weight
    )
    return (first_new, second_new, delta)


def local(
    inputs, segments, cotangent, pregain, innerweight, rateweight, stateweight, innerconv, stateconv, headparams,
    postgain, outweight, *moments,
):
    nrow, ncol = lax.axis_size("row"), lax.axis_size("col")
    row, col = lax.axis_index("row"), lax.axis_index("col")
    length, own = inputs.shape[1], inputs.shape[2]
    width = own * nrow * ncol
    stored = innerweight.shape[1]
    total_heads = stored * ncol
    heads = total_heads // nrow
    hl = heads * HEADP
    count = total_heads * HEADP
    tokens = length // ncol
    steps = tokens // GROUP
    depth = width // nrow
    fold = ncol // nrow
    hops = (MOST - 2) // tokens + 1

    window = jnp.pad(segments[0], (HALO, HALO), constant_values=-1)
    window = lax.dynamic_slice_in_dim(window, col * tokens, tokens + 2 * HALO, 0)
    mine = window[HALO : HALO + tokens]
    flags = [mine]
    for j in (-1, -2, -3, 1, 2, 3):
        flags.append(window[HALO + j : HALO + j + tokens] == mine)
    before = window[HALO - 1 : HALO - 1 + tokens : GROUP]
    flags.append((mine.reshape(steps, GROUP) == before[:, None]).reshape(tokens))
    tok = jnp.stack([f.astype(F32) for f in flags])
    hmask = jnp.stack([(window[j : j + HALO] == window[:HALO]).astype(F32) for j in range(8)], 1)
    hmask = jnp.pad(hmask, ((0, 0), (0, 120)))

    block_heads = headparams.shape[1]
    smalls = [pregain, innerconv, headparams, postgain, rateweight, stateweight]
    flat = jnp.concatenate([a.reshape(-1) for a in smalls])
    sizes = [a.size for a in smalls]
    pad = -flat.size % 2048
    packed = jnp.pad(flat, (0, pad)).reshape(-1, 128)
    gathered = lax.all_gather(packed, ("row", "col"), axis=0).reshape(nrow, ncol, -1)
    parts, at = [], 0
    for size in sizes:
        parts.append(gathered[:, :, at : at + size])
        at += size
    gain = parts[0].reshape(1, width).astype(F32)
    iconv = parts[1].reshape(nrow, ncol, 5, block_heads, HEADP).transpose(2, 1, 0, 3, 4)
    iconv = lax.dynamic_slice_in_dim(iconv.reshape(5, count), row * hl, hl, 1).astype(F32)
    hp = parts[2].reshape(nrow, ncol, 3, block_heads).transpose(2, 1, 0, 3)
    hp = lax.dynamic_slice_in_dim(hp.reshape(3, total_heads), row * heads, heads, 1).astype(F32)
    post = parts[3].reshape(nrow, ncol, block_heads * HEADP).transpose(1, 0, 2)
    post = lax.dynamic_slice_in_dim(post.reshape(1, count), row * hl, hl, 1).astype(F32)
    wrate = parts[4].reshape(nrow, ncol, depth, stored).transpose(1, 3, 0, 2)
    wrate = lax.dynamic_slice_in_dim(wrate.reshape(total_heads, width), row * heads, heads, 0)
    wrate = jnp.pad(wrate, ((0, 16 - heads), (0, 0)))
    wstate = parts[5].reshape(width, 2 * NSTATE)
    sconv = stateconv.astype(F32)
    head = jnp.broadcast_to(
        jnp.concatenate([-jnp.exp(hp[0]), hp[1]])[:, None], (2 * heads, 128)
    )
    skip = jnp.repeat(hp[2], HEADP)[None]

    split = innerweight.reshape(depth, stored, 2, HEADP)
    sent = jnp.concatenate(
        [
            split[:, :, 0].reshape(depth, -1),
            split[:, :, 1].reshape(depth, -1),
            outweight.reshape(stored * HEADP, depth).T,
        ],
        1,
    )
    sub = depth // fold
    sent = sent.reshape(fold, sub, -1)
    came = []
    for m in range(fold):
        perm = []
        for r in range(nrow):
            for c in range(ncol):
                perm.append((r * ncol + c, (c // fold) * ncol + r * fold + (m + c) % fold))
        piece = lax.dynamic_index_in_dim(sent, (m + col) % fold, 0, False)
        came.append(lax.ppermute(piece, ("row", "col"), perm))
    came = jnp.stack(came)
    came = jnp.stack(
        [lax.dynamic_index_in_dim(came, (col - i) % fold, 0, False) for i in range(fold)]
    )
    came = came.reshape(fold, sub, 3, stored * HEADP).transpose(1, 2, 0, 3).reshape(sub, 3 * hl)
    weights = lax.all_gather(came, "col", axis=0, tiled=True)
    wmain, woutt = weights[:, : 2 * hl], weights[:, 2 * hl :]

    padded = jnp.pad(inputs[0], ((HALO, 0), (0, 0)))
    pieces = jnp.stack([padded[i * tokens : (i + 1) * tokens + HALO] for i in range(ncol)])
    pieces = lax.all_to_all(pieces, "col", 0, 0).transpose(1, 0, 2).reshape(tokens + HALO, depth)
    xall = lax.all_gather(pieces, "row", axis=0)
    xh, x = xall[:, :HALO], xall[:, HALO:]
    pieces = lax.all_to_all(cotangent[0].reshape(ncol, tokens, own), "col", 0, 0)
    cot = lax.all_gather(pieces.transpose(1, 0, 2).reshape(tokens, depth), "row", axis=0)

    spread = jnp.repeat(jnp.eye(heads, dtype=BF16), HEADP, 1)
    spread = jnp.concatenate([spread, spread], 0)
    triangle = jnp.triu(jnp.ones((GROUP, GROUP), BF16))
    ns2 = 2 * NSTATE

    gate, pre, st, uv, us, bc, rows, states, prod, fin, total, preh, sth, rinvh = call(
        fwd1_kernel,
        steps,
        [sublanes(x), whole(xh), whole(gain), whole(wmain), whole(wstate), whole(wrate), lanes(tok), whole(head),
         whole(iconv), whole(sconv), whole(triangle), whole(spread)],
        [out_sub((tokens, hl), F32), out_sub((tokens, hl), F32), out_sub((tokens, ns2), BF16),
         out_sub((tokens, hl), F32), out_sub((tokens, ns2), F32), out_sub((tokens, ns2), BF16),
         out_lanes((4 * heads, tokens), F32),
         out_each((steps, NSTATE, hl), BF16), out_each((steps, 8, hl), F32),
         out_whole((NSTATE, hl), F32), out_whole((8, hl), F32), out_whole((HALO, hl), BF16), out_whole((HALO, ns2), BF16),
         out_whole((HALO, 128), F32)],
        [pltpu.VMEM((GROUP + 8, hl + ns2), F32), pltpu.VMEM((NSTATE, hl), F32), pltpu.VMEM((8, hl), F32)],
        False,
        "fwd1",
    )
    total = total[0:1]
    ahead = [(i, i + 1) for i in range(ncol - 1)]
    back = [(i + 1, i) for i in range(ncol - 1)]
    sin = lax.ppermute(fin, "col", ahead)
    for _ in range(hops - 1):
        sin = lax.ppermute(fin + total * sin, "col", ahead)

    scan, out, dn, stat = call(
        fwd2_kernel,
        steps,
        [sublanes(gate), sublanes(uv), sublanes(bc), lanes(rows), lanes(tok), each(states), each(prod), whole(sin),
         sublanes(cot), whole(post), whole(skip), whole(woutt), whole(spread)],
        [out_sub((tokens, hl), F32), out_sub((nrow, tokens, depth), BF16), out_sub((tokens, hl), BF16),
         out_lanes((16, tokens), F32)],
        [],
        False,
        "fwd2",
    )
    stat = lax.psum(jnp.stack([stat[0], stat[8]]), "row")
    rootgate = lax.rsqrt(stat[0] / count + NORM_EPSILON)
    pull = rootgate * rootgate * rootgate * stat[1] / count
    scal = jnp.pad(jnp.stack([rootgate, pull]), ((0, 6), (0, 0)))

    mixed = lax.psum_scatter(out, "row", scatter_dimension=0, tiled=False)
    mixed = (mixed.astype(F32) * rootgate[:, None]).astype(BF16)
    mixed = lax.all_to_all(mixed.reshape(tokens, ncol, own).transpose(1, 0, 2), "col", 0, 0)
    result = inputs.astype(F32) + mixed.reshape(1, length, own).astype(F32)

    dy, dg, leave, prodb, first, gout, sums, root = call(
        bwd1_kernel,
        steps,
        [sublanes(gate), sublanes(uv), sublanes(bc), lanes(rows), lanes(tok), sublanes(scan), sublanes(dn),
         lanes(scal), sublanes(cot), whole(post), whole(skip), whole(spread)],
        [out_sub((tokens, hl), BF16), out_sub((tokens, hl), BF16), out_each((steps, NSTATE, hl), BF16),
         out_each((steps, 8, hl), F32), out_whole((NSTATE, hl), F32), out_whole((width, hl), F32),
         out_whole((16, hl), F32), out_lanes((8, tokens), F32)],
        [pltpu.VMEM((NSTATE, hl), F32), pltpu.VMEM((8, hl), F32)],
        True,
        "bwd1",
    )
    din = lax.ppermute(first, "col", back)
    for _ in range(hops - 1):
        din = lax.ppermute(first + total * din, "col", back)

    gin, ginh, gw, gr, gk, gh, gp = call(
        bwd2_kernel,
        steps,
        [sublanes(x), whole(xh), whole(gain), whole(wmain), whole(wstate), whole(wrate), lanes(tok), whole(head),
         whole(hmask), whole(rinvh), whole(iconv), whole(sconv), whole(triangle), whole(spread), whole(skip),
         sublanes(pre), sublanes(st), whole(preh), whole(sth), sublanes(uv), sublanes(us), sublanes(bc), lanes(rows),
         each(states), each(prod), whole(sin), sublanes(scan), sublanes(dy), sublanes(dg),
         each(leave), each(prodb), whole(din), lanes(root)],
        [out_sub((nrow, tokens, depth), BF16), out_whole((nrow, HALO, depth), BF16),
         out_whole((width, 2 * hl + ns2), F32), out_whole((16, width), F32), out_whole((40, hl + ns2), F32),
         out_whole((2 * heads, GROUP), F32), out_whole((8, width), F32)],
        [pltpu.VMEM((GROUP + 8, hl + ns2), F32)],
        True,
        "bwd2",
    )

    gin = lax.psum_scatter(jnp.concatenate([gin, ginh], 1), "row", scatter_dimension=0, tiled=False)
    gin = gin.reshape(tokens + HALO, ncol, own).transpose(1, 0, 2)
    gin = lax.all_to_all(gin, "col", 0, 0).astype(F32)
    body, halo = gin[:, :tokens], gin[:, tokens:]
    halo = jnp.concatenate([halo[1:], jnp.zeros_like(halo[:1])], 0)
    body = jnp.concatenate([body[:, : tokens - HALO], body[:, tokens - HALO :] + halo], 1)
    grad_input = cotangent.astype(F32) + body.reshape(1, length, own)

    def home(grad):
        grad = lax.psum_scatter(grad.astype(BF16), "col", scatter_dimension=0, tiled=True)
        grad = lax.psum(grad.astype(F32), "dp").astype(BF16)
        per = grad.shape[1] // hl
        grad = grad.reshape(sub, per, fold, stored * HEADP).transpose(2, 0, 1, 3).reshape(fold, sub, -1)
        got = []
        for m in range(fold):
            perm = []
            for r in range(nrow):
                for c in range(ncol):
                    perm.append(((c // fold) * ncol + r * fold + (m + c) % fold, r * ncol + c))
            piece = lax.dynamic_index_in_dim(grad, (col - m) % fold, 0, False)
            got.append(lax.ppermute(piece, ("row", "col"), perm))
        got = jnp.stack(got)
        got = jnp.stack(
            [lax.dynamic_index_in_dim(got, (j - col) % fold, 0, False) for j in range(fold)]
        )
        return got.reshape(depth, per, stored, HEADP).astype(F32)

    gout = home(gout)[:, 0].transpose(1, 2, 0)
    ginner = home(gw[:, : 2 * hl]).transpose(0, 2, 1, 3).reshape(depth, stored, 2 * HEADP)
    gstate = lax.psum_scatter(gw[:, 2 * hl :], ("row", "col"), scatter_dimension=0, tiled=True)
    gstate = lax.psum(gstate, "dp")

    def place(part, size):
        blank = jnp.zeros((part.shape[0], size), F32)
        return lax.dynamic_update_slice(blank, part, (0, row * part.shape[1]))

    gk = jnp.sum(gk.reshape(5, 8, -1), 1)
    gh = jnp.sum(gh, 1).reshape(2, heads)
    sums = jnp.sum(sums.reshape(2, 8, hl), 1)
    gskip = jnp.sum(sums[1].reshape(1, heads, HEADP), 2)
    small = [
        jnp.sum(gp, 0),
        place(gr[:heads].T, total_heads),
        place(gk[:, :hl], count),
        gk[:, hl:],
        place(jnp.concatenate([gh, gskip]), total_heads),
        place(sums[0:1], count),
    ]
    flat = jnp.concatenate([a.reshape(-1) for a in small])
    pad = -flat.size % 1024
    flat = lax.psum(jnp.pad(flat, (0, pad)).reshape(-1, 128), ("dp", "row", "col")).reshape(-1)
    back_parts, at = [], 0
    for a in small:
        back_parts.append(flat[at : at + a.size].reshape(a.shape))
        at += a.size
    feature = (row * ncol + col) * own
    block = col * nrow + row
    gpre = lax.dynamic_slice_in_dim(back_parts[0], feature, own, 0)
    grate = lax.dynamic_slice(back_parts[1], (row * depth, col * stored), (depth, stored))
    giconv = lax.dynamic_slice_in_dim(back_parts[2], block * block_heads * HEADP, block_heads * HEADP, 1)
    giconv = giconv.reshape(5, block_heads, HEADP)
    gsconv = back_parts[3]
    ghead = lax.dynamic_slice_in_dim(back_parts[4], block * block_heads, block_heads, 1)
    gpost = lax.dynamic_slice_in_dim(back_parts[5], block * block_heads * HEADP, block_heads * HEADP, 1)
    gpost = gpost.reshape(block_heads, HEADP)

    grads = (gpre, ginner, grate, gstate, giconv, gsconv, ghead, gpost, gout)
    params = (
        pregain, innerweight, rateweight, stateweight, innerconv, stateconv, headparams, postgain, outweight,
    )
    outputs = [result, grad_input]
    for i, (grad, param) in enumerate(zip(grads, params)):
        outputs.append(grad)
        outputs.extend(adamw_step(grad, moments[2 * i], moments[2 * i + 1], param.astype(F32)))
    return tuple(outputs)


def solution(mesh):
    tokens = P("dp", None, ("row", "col"))
    weights = (
        P(("row", "col")),
        P("row", "col", None),
        P("row", "col"),
        P(("row", "col"), None),
        P(None, ("col", "row"), None),
        P(),
        P(None, ("col", "row")),
        P(("col", "row"), None),
        P("col", None, "row"),
    )
    return jax.shard_map(
        local,
        mesh=mesh,
        in_specs=(tokens, P("dp", None), tokens)
        + weights
        + tuple(w for w in weights for _ in range(2)),
        out_specs=(tokens, tokens) + tuple(w for w in weights for _ in range(4)),
        check_vma=False,
    )
```

time: 2300 us -> 806 us (0.35)
  waiting for transfers between devices: 1090 us -> 359 us
  other arithmetic: 337 us -> 30 us
  matrix products: 303 us -> 0 us
  local copies, waits for them, and re-layouts: 262 us -> 80.7 us
  Pallas kernels: 0 us -> 107 us
  blocking collectives: 279 us -> 187 us
    unnamed x15 -> x9, waiting for transfers between devices: 447 us -> 0.66 us
    dot_general x25 -> x0, matrix products: 288 us -> none  [the longest x3 73.9 us: scan_sequence(): jnp.einsum('bhts,bshp->bthp', weights, blocked, precision=EXACT_PRECISION)]
    psum x5 -> x2, blocking collectives: 261 us -> 52 us  [the longest x1 41.9 us: home(): grad = lax.psum(grad.astype(F32), 'dp').astype(BF16)]
    psum x3 -> x1, waiting for transfers between devices: 293 us -> 106 us  [local(): lax.psum(jnp.pad(flat, (0, pad)).reshape(-1, 128), ('dp', 'row', 'col'))]
    all_gather x4 -> x3, waiting for transfers between devices: 161 us -> 0.01 us  [the longest x1 0.01 us: local(): weights = lax.all_gather(came, 'col', axis=0, tiled=True)]
    reduce_sum x42 -> x5, other arithmetic: 134 us -> 1.85 us  [the longest x1 0.8 us: local(): jnp.sum(gp, 0)]
    pallas_call x0 -> x4, Pallas kernels: none -> 107 us  [call(): pl.pallas_call(kernel, grid=(steps,), in_specs=[spec(block, axis) for _,...]
    all_to_all x0 -> x2, blocking collectives: none -> 96.4 us  [the longest x1 55.1 us: local(): lax.all_to_all(pieces, 'col', 0, 0).transpose(1, 0, 2)]
  transfers between devices with their start and end apart: 12 -> 16, of which waited for: 9 -> 10; matrix products, arithmetic and copies ran while one was open for 32% -> 11% of each run, Pallas kernels for 0% -> 3%
where the time goes in v1:
time: 806 us; the launch traced here: 802 us
  waiting for transfers between devices  359 us (45%)
  blocking collectives  187 us (23%)
  Pallas kernels  107 us (13%)
  local copies, waits for them, and re-layouts  80.7 us (10%)
  other arithmetic  30 us (4%)
  starting transfers between devices  23.5 us (3%)
  between operations  14.7 us (2%)
    pallas_call x4, Pallas kernels, call(): pl.pallas_call(kernel, grid=(steps,), in_specs=[spec(block, axis) for _,...  107 us
    psum x1, waiting for transfers between devices, local(): lax.psum(jnp.pad(flat, (0, pad)).reshape(-1, 128), ('dp', 'row', 'col'))  106 us
    reduce_scatter x2, waiting for transfers between devices, home(): lax.psum_scatter(grad.astype(BF16), 'col', scatter_dimension=0, tiled=True)  74.4 us
    all_to_all x1, blocking collectives, local(): lax.all_to_all(pieces, 'col', 0, 0).transpose(1, 0, 2)  55.1 us
    reduce_scatter x1, waiting for transfers between devices, local(): lax.psum_scatter(gw[:, 2 * hl:], ('row', 'col'), scatter_dimension=0, til...  54.4 us
    psum x1, blocking collectives, home(): grad = lax.psum(grad.astype(F32), 'dp').astype(BF16)  41.9 us
    all_to_all x1, blocking collectives, local(): lax.all_to_all(cotangent[0].reshape(ncol, tokens, own), 'col', 0, 0)  41.3 us
    reduce_scatter x1, waiting for transfers between devices, local(): mixed = lax.psum_scatter(out, 'row', scatter_dimension=0, tiled=False)  39.9 us
  transfers between devices with their start and end apart: 16, of which 10 were waited for; matrix products, arithmetic and copies ran while one was open for 11% of the time, Pallas kernels for 3%

profile of v1, /device:TPU:6, one launch (start us, length us, event | category | flops | bytes accessed | tf_op | source)
XLA Modules:
  0.0 801.8 jit_solution(13820416847098505733)
XLA Ops:
  10.1 4.5 collective-permute-start
  14.6 36.0 %collective-permute-done = bf16[256,1536]{1,0:T(8,128)(2,1)S(1)} collective-permute-done((bf16[256,1536]{1,0:T(8,128)(2,1)S(1)}, bf16[256,1536]{1,0:T(8,128)(2,1)S(1)}, u32[]{:S(2)}, u32[]{:S(2)}) %collective-permute-start) | collective-permute-done | bytes 786464 | tf_op jit(solution)/shard_map/ppermute | solution.py:620
  52.2 55.1 %all_to_all.20 = bf16[4,2064,64]{1,2,0:T(8,128)(2,1)S(1)} all-to-all(bf16[4,2064,64]{1,2,0:T(8,128)(2,1)S(1)} %pad_maximum_fusion.2), channel_id=1, replica_groups=mesh['dp'=2,'row'=4,'col'=4] {'col'}, dimensions={0} | all-to-all | bytes 2113536 | tf_op jit(solution)/shard_map/all_to_all | solution.py:631
  111.1 41.3 %all_to_all.21 = bf16[4,2048,64]{1,2,0:T(8,128)(2,1)S(1)} all-to-all(bf16[4,2048,64]{1,2,0:T(8,128)(2,1)S(1)} %copy.319), channel_id=1, replica_groups=mesh['dp'=2,'row'=4,'col'=4] {'col'}, dimensions={0} | all-to-all | bytes 2097152 | tf_op jit(solution)/shard_map/all_to_all | solution.py:634
  154.7 38.8 %all_gather.13 = bf16[16,160,128]{2,1,0:T(8,128)(2,1)S(1)} all-gather(bf16[1,160,128]{2,1,0:T(8,128)(2,1)S(1)} %pad_bitcast_fusion.1), channel_id=1, replica_groups=mesh['dp'=2,'row'=4,'col'=4] {'row','col'}, dimensions={0}, use_global_device_ids=true | all-gather | bytes 696320 | tf_op jit(solution)/shard_map/all_gather | solution.py:580
  206.5 4.5 slice.251.x_ref
  213.1 21.5 %fwd1.1 = (f32[2048,512]{1,0:T(8,128)}, f32[2048,512]{1,0:T(8,128)}, bf16[2048,256]{1,0:T(8,128)(2,1)}, f32[2048,512]{1,0:T(8,128)}, f32[2048,256]{1,0:T(8,128)}...) custom-call(bf16[4,2048,256]{2,1,0:T(8,128)(2,1)} %slice.251.x_ref, ...), custom_call_target="tpu_custom_call" | custom-call | tf_op jit(solution)/shard_map/fwd1/pallas_call | solution.py:485
  241.1 17.7 %fwd2.1 = (f32[2048,512]{1,0:T(8,128)}, bf16[4,2048,256]{2,1,0:T(8,128)(2,1)}, bf16[2048,512]{1,0:T(8,128)(2,1)}, f32[16,2048]{1,0:T(8,128)}) custom-call(f32[2048,512]{1,0:T(8,128)} %get-tuple-element.70.gate_ref, f32[2048,512]{1,0:T(8,128)} %get-tuple-element.71.uv_ref, bf16[2048,256]{1,0:T(8,128)(2,1)} %get-tuple-element.72.bc_ref, ...), custom_call_target="tpu_custom_call" | custom-call | tf_op jit(solution)/shard_map/fwd2/pallas_call | solution.py:485
  259.7 10.1 %psum.35 = f32[2,2048]{1,0:T(2,128)S(1)} all-reduce(f32[2,2048]{1,0:T(2,128)S(1)} %pad_maximum_fusion.4), channel_id=1, replica_groups=mesh['dp'=2,'row'=4,'col'=4] {'row'}, use_global_device_ids=true, to_apply=%region_1.2 | all-reduce | flops 4096 | bytes 32768 | tf_op jit(solution)/shard_map/psum | solution.py:675
  270.5 15.0 %bwd1.1 = (bf16[2048,512]{1,0:T(8,128)(2,1)}, bf16[2048,512]{1,0:T(8,128)(2,1)}, bf16[8,128,512]{2,1,0:T(8,128)(2,1)}, f32[8,8,512]{2,1,0:T(8,128)}, f32[128,512...) custom-call(f32[2048,512]{1,0:T(8,128)} %get-tuple-element.70.gate_ref, ...), custom_call_target="tpu_custom_call" | custom-call | tf_op jit(solution)/shard_map/bwd1/pallas_call | solution.py:485
  288.1 6.9 collective-permute-done.2.din_ref
  295.7 52.7 %bwd2.1 = (bf16[4,2048,256]{2,1,0:T(8,128)(2,1)}, bf16[4,16,256]{2,1,0:T(8,128)(2,1)}, f32[1024,1280]{1,0:T(8,128)}, f32[16,1024]{1,0:T(8,128)}, f32[40,768]{1,0...) custom-call(bf16[4,2048,256]{2,1,0:T(8,128)(2,1)} %slice.251.x_ref, bf16[4,16,256]{2,1,0:T(8,128)(2,1)} %slice.252.xh_ref, ...), custom_call_target="tpu_custom_call" | custom-call | tf_op jit(solution)/shard_map/bwd2/pallas_call | solution.py:485
  363.9 4.5 pad_maximum_fusion
  372.7 106.0 %all-reduce.12.cloned.1.call-done = f32[376,128]{1,0:T(8,128)} async-done(((f32[376,128]{1,0:T(8,128)}), f32[376,128]{1,0:T(8,128)}) %all-reduce.12.cloned.1.call-update) | async-done | bytes 192528 | tf_op jit(solution)/shard_map/psum | solution.py:767
  486.3 39.9 %reduce-scatter.6.cloned.1.call-done = bf16[1,2048,256]{2,1,0:T(8,128)(2,1)} async-done(((bf16[4,2048,256]{2,1,0:T(8,128)(2,1)}), bf16[1,2048,256]{2,1,0:T(8,128)(2,1)}) %reduce-scatter.6.cloned.1.call-update) | async-done | bytes 1048592 | tf_op jit(solution)/shard_map/reduce_scatter | solution.py:680
  528.9 4.8 all-to-all-start.2
  534.3 54.4 %reduce-scatter.12.cloned.1.call-done = f32[64,256]{1,0:T(8,128)} async-done(((f32[1024,256]{1,0:T(8,128)}), f32[64,256]{1,0:T(8,128)}) %reduce-scatter.12.cloned.1.call-update) | async-done | bytes 65552 | tf_op jit(solution)/shard_map/reduce_scatter | solution.py:746
  588.7 29.3 %reduce-scatter.14.cloned.1.call-done = bf16[256,512]{1,0:T(8,128)(2,1)} async-done(((bf16[1024,512]{1,0:T(8,128)(2,1)}), bf16[256,512]{1,0:T(8,128)(2,1)}) %reduce-scatter.14.cloned.1.call-update) | async-done | bytes 262160 | tf_op jit(solution)/shard_map/reduce_scatter | solution.py:726
  618.0 45.0 %reduce-scatter.10.cloned.1.call-done = bf16[256,1024]{1,0:T(8,128)(2,1)} async-done(((bf16[1024,1024]{1,0:T(8,128)(2,1)}), bf16[256,1024]{1,0:T(8,128)(2,1)}) %reduce-scatter.10.cloned.1.call-update) | async-done | bytes 524304 | tf_op jit(solution)/shard_map/reduce_scatter | solution.py:726
  663.1 41.9 %all-reduce.13 = (bf16[256,512]{1,0:T(8,128)(2,1)S(1)}, bf16[256,1024]{1,0:T(8,128)(2,1)}, f32[64,256]{1,0:T(8,128)S(1)}) all-reduce(bf16[256,512]{1,0:T(8,128)(2,1)} %reduce-scatter.14.cloned.1.call-done, bf16[256,1024]{1,0:T(8,128)(2,1)} %reduce-scatter.10.cloned.1.call-done, ...), channel_id=1, replica_groups=mesh['dp'=2,'row'=4,'col'=4] {'dp'}, use_global_device_ids=true, to_apply=%region_14.15 | all-reduce | flops 409600 | bytes 1703936 | tf_op jit(solution)/shard_map/psum | solution.py:727
  705.0 4.2 collective-permute-start.4
  716.5 15.2 %collective-permute-done.4 = bf16[256,512]{1,0:T(8,128)(2,1)S(1)} collective-permute-done((bf16[256,512]{1,0:T(8,128)(2,1)S(1)}, bf16[256,512]{1,0:T(8,128)(2,1)S(1)}, u32[]{:S(2)}, u32[]{:S(2)}) %collective-permute-start.4) | collective-permute-done | bytes 262176 | tf_op jit(solution)/shard_map/ppermute | solution.py:737
  734.7 8.2 %collective-permute-done.3 = bf16[256,1024]{1,0:T(8,128)(2,1)S(1)} collective-permute-done((bf16[256,1024]{1,0:T(8,128)(2,1)}, bf16[256,1024]{1,0:T(8,128)(2,1)S(1)}, u32[]{:S(2)}, u32[]{:S(2)}) %collective-permute-start.3) | collective-permute-done | bytes 524320 | tf_op jit(solution)/shard_map/ppermute | solution.py:737
  770.5 17.1 %all-to-all-done.3 = bf16[4,2064,64]{1,2,0:T(8,128)(2,1)S(1)} async-done(((bf16[4,2064,64]{1,2,0:T(8,128)(2,1)}), bf16[4,2064,64]{1,2,0:T(8,128)(2,1)S(1)}, u32[]{:S(2)}, u32[]{:S(2)}) %all-to-all-start.3) | async-done | bytes 1056800 | tf_op jit(solution)/shard_map/all_to_all | solution.py:719
  (284 shorter events, 112.5 us)
Async XLA Ops:
  7.2 196.2 %all-gather.6.cloned.1.call-start = ((), (), s32[]{:S(2)}) async-start(), calls=%async_computation.10 | async-start | bytes 3932160 | tf_op jit(solution)/shard_map/all_gather | solution.py:626
  10.1 40.5 %collective-permute-start = (bf16[256,1536]{1,0:T(8,128)(2,1)S(1)}, bf16[256,1536]{1,0:T(8,128)(2,1)S(1)}, u32[]{:S(2)}, u32[]{:S(2)}) collective-permute-start(bf16[256,1536]{1,0:T(8,128)(2,1)S(1)} %pad_maximum_fusion.3), channel_id=1, source_target_pairs={{0,0},{1,4},{2,8},{3,12},{4,1},{5,5},{6,9},{7,13},{8,2},{9,6},{10,... | collective-permute-start | bytes 2359304 | tf_op jit(solution)/shard_map/ppermute | solution.py:620
  51.5 155.0 %all-gather.4.cloned.1.call-start = ((), (), s32[]{:S(2)}) async-start(), calls=%async_computation.9 | async-start | bytes 5283840 | tf_op jit(solution)/shard_map/all_gather | solution.py:632
  108.7 131.7 %all-gather.8.cloned.1.call-start = ((), (), s32[]{:S(2)}) async-start(), calls=%async_computation.11 | async-start | bytes 5242880 | tf_op jit(solution)/shard_map/all_gather | solution.py:635
  153.8 324.8 %all-reduce.12.cloned.1.call-start = ((), (), s32[]{:S(2)}) async-start(), calls=%async_computation.14 | async-start | bytes 385024 | tf_op jit(solution)/shard_map/psum | solution.py:767
  234.6 5.8 collective-permute-start.1
  285.6 9.4 %collective-permute-start.2 = (f32[128,512]{1,0:T(8,128)}, f32[128,512]{1,0:T(8,128)S(1)}, u32[]{:S(2)}, u32[]{:S(2)}) collective-permute-start(f32[128,512]{1,0:T(8,128)} %get-tuple-element.91), channel_id=1, source_target_pairs={{1,0},{2,1},{3,2},{5,4},{6,5},{7,6},{9,8},{10,9},{11,10},{13,12},{... | collective-permute-start | bytes 786440 | tf_op jit(solution)/shard_map/ppermute | solution.py:697
  355.0 171.3 %reduce-scatter.6.cloned.1.call-start = ((), (), s32[]{:S(2)}) async-start(), calls=%async_computation.12 | async-start | bytes 5242880 | tf_op jit(solution)/shard_map/reduce_scatter | solution.py:680
  355.6 233.1 %reduce-scatter.12.cloned.1.call-start = ((), (), s32[]{:S(2)}) async-start(), calls=%async_computation.16 | async-start | bytes 1114112 | tf_op jit(solution)/shard_map/reduce_scatter | solution.py:746
  358.0 260.0 %reduce-scatter.14.cloned.1.call-start = ((), (), s32[]{:S(2)}) async-start(), calls=%async_computation.17 | async-start | bytes 1310720 | tf_op jit(solution)/shard_map/reduce_scatter | solution.py:726
  359.2 303.8 %reduce-scatter.10.cloned.1.call-start = ((), (), s32[]{:S(2)}) async-start(), calls=%async_computation.15 | async-start | bytes 2621440 | tf_op jit(solution)/shard_map/reduce_scatter | solution.py:726
  363.2 392.7 %reduce-scatter.8.cloned.1.call-start = ((), (), s32[]{:S(2)}) async-start(), calls=%async_computation.13 | async-start | bytes 5283840 | tf_op jit(solution)/shard_map/reduce_scatter | solution.py:717
  371.0 114.0 %copy-start.28 = (f32[256,8]{0,1:T(8,128)S(1)}, f32[256,8]{0,1:T(8,128)}, u32[]{:S(2)}) copy-start(f32[256,8]{0,1:T(8,128)} %param.47) | copy-start | bytes 24580
  371.0 114.6 %copy-start.30 = (f32[5,256]{1,0:T(8,128)S(1)}, f32[5,256]{1,0:T(8,128)}, u32[]{:S(2)}) copy-start(f32[5,256]{1,0:T(8,128)} %param.53) | copy-start | bytes 15364
  371.0 114.6 %copy-start.31 = (f32[5,256]{1,0:T(8,128)S(1)}, f32[5,256]{1,0:T(8,128)}, u32[]{:S(2)}) copy-start(f32[5,256]{1,0:T(8,128)} %param.52) | copy-start | bytes 15364
  528.9 180.2 %copy-start.40 = (f32[64]{0:T(128)S(1)}, f32[64]{0:T(128)}, u32[]{:S(2)}) copy-start(f32[64]{0:T(128)} %param.43) | copy-start | bytes 772
  528.9 180.2 %copy-start.41 = (f32[64]{0:T(128)S(1)}, f32[64]{0:T(128)}, u32[]{:S(2)}) copy-start(f32[64]{0:T(128)} %param.42) | copy-start | bytes 772
  528.9 186.9 %copy-start.17 = (f32[64,256]{1,0:T(8,128)S(1)}, f32[64,256]{1,0:T(8,128)}, u32[]{:S(2)}) copy-start(f32[64,256]{1,0:T(8,128)} %param.49) | copy-start | bytes 196612
  528.9 186.9 %copy-start.18 = (f32[64,256]{1,0:T(8,128)S(1)}, f32[64,256]{1,0:T(8,128)}, u32[]{:S(2)}) copy-start(f32[64,256]{1,0:T(8,128)} %param.48) | copy-start | bytes 196612
  528.9 202.9 %copy-start.10 = (bf16[8,64,256]{2,1,0:T(8,128)(2,1)S(1)}, bf16[8,64,256]{2,1,0:T(8,128)(2,1)}, u32[]{:S(2)}) copy-start(bf16[8,64,256]{2,1,0:T(8,128)(2,1)} %param.41) | copy-start | bytes 786436
  528.9 229.2 %all-to-all-start.2 = ((bf16[4,2048,64]{1,2,0:T(8,128)(2,1)}), bf16[4,2048,64]{1,2,0:T(8,128)(2,1)S(1)}, u32[]{:S(2)}, u32[]{:S(2)}) async-start(bf16[4,2048,64]{1,2,0:T(8,128)(2,1)} %fusion.1), calls=%async_computation.3 | async-start | bytes 2097152 | tf_op jit(solution)/shard_map/all_to_all | solution.py:682
  705.0 26.7 %collective-permute-start.4 = (bf16[256,512]{1,0:T(8,128)(2,1)S(1)}, bf16[256,512]{1,0:T(8,128)(2,1)S(1)}, u32[]{:S(2)}, u32[]{:S(2)}) collective-permute-start(bf16[256,512]{1,0:T(8,128)(2,1)S(1)} %get-tuple-element.292), channel_id=1, source_target_pairs={{0,0},{4,1},{8,2},{12,3},{1,4},{5,5},{9,6},{13,7},{2,8},{6,9},{10,... | collective-permute-start | bytes 786440 | tf_op jit(solution)/shard_map/ppermute | solution.py:737
  712.4 30.5 %collective-permute-start.3 = (bf16[256,1024]{1,0:T(8,128)(2,1)}, bf16[256,1024]{1,0:T(8,128)(2,1)S(1)}, u32[]{:S(2)}, u32[]{:S(2)}) collective-permute-start(bf16[256,1024]{1,0:T(8,128)(2,1)} %get-tuple-element.293), channel_id=1, source_target_pairs={{0,0},{4,1},{8,2},{12,3},{1,4},{5,5},{9,6},{13,7},{2,8},{6,9},{10,... | collective-permute-start | bytes 1572872 | tf_op jit(solution)/shard_map/ppermute | solution.py:737
  759.1 28.5 %all-to-all-start.3 = ((bf16[4,2064,64]{1,2,0:T(8,128)(2,1)}), bf16[4,2064,64]{1,2,0:T(8,128)(2,1)S(1)}, u32[]{:S(2)}, u32[]{:S(2)}) async-start(bf16[4,2064,64]{1,2,0:T(8,128)(2,1)} %bitcast.41), calls=%async_computation.5 | async-start | bytes 2228224 | tf_op jit(solution)/shard_map/all_to_all | solution.py:719
  (36 other events, 686.7 us)
Sparse Core Ops, SparseCore 0:
  51.6 100.2 all-gather.5
  154.1 35.4 all-gather.3
  191.7 34.5 all-gather.7
  355.1 123.5 all-reduce.11
  481.0 45.1 reduce-scatter.5
  530.3 58.3 reduce-scatter.11
  591.5 26.4 reduce-scatter.13
  620.9 42.1 reduce-scatter.9
  665.6 43.0 reduce-scatter.7

commit v2 on v1

v2 whole, which is shorter than its diff:
```python
import functools

import jax
import jax.numpy as jnp
from jax import lax
from jax.experimental import pallas as pl
from jax.experimental.pallas import tpu as pltpu
from jax.sharding import PartitionSpec as P

HEADP = 64
NSTATE = 128
GROUP = 256
MOST = 2000
STEP = 4
HALO = 16
NORM_EPSILON = 1e-05
ADAM_EPSILON = 1e-08
BETA_FIRST = 0.5
BETA_SECOND = 0.5
LEARN_RATE = 0.02
WEIGHT_DECAY = 0.1
FAR = -1e30

F32 = jnp.float32
BF16 = jnp.bfloat16


def dot(a, b, ca, cb):
    return lax.dot_general(a, b, (((ca,), (cb,)), ((), ())), preferred_element_type=F32)


def mm(a, b):
    return dot(a, b, 1, 0)


def mm_nt(a, b):
    return dot(a, b, 1, 1)


def mm_tn(a, b):
    return dot(a, b, 0, 0)


def sigmoid(v):
    return 0.5 * jnp.tanh(0.5 * v) + 0.5


def halves(v):
    high = v.astype(BF16)
    return high, (v - high.astype(F32)).astype(BF16)


def stack_parts(v, count):
    parts = []
    for _ in range(count):
        high = v.astype(BF16).astype(F32)
        parts.append(high)
        v = v - high
    return parts


def expand(rows, spread):
    high, low = stack_parts(rows, 2)
    return mm_tn(jnp.concatenate([high, low], 0).astype(BF16), spread)


def head_sums(v, spread):
    high, low = halves(v)
    sums = mm_nt(spread, high) + mm_nt(spread, low)
    return sums[: sums.shape[0] // 2]


def lane_sums(v):
    total = v[:, :128]
    for at in range(128, v.shape[1], 128):
        total = total + v[:, at : at + 128]
    high, low = halves(total)
    return mm_nt(jnp.ones((16, 256), BF16), jnp.concatenate([high, low], 1))[:8]


def running(rows, triangle, product=mm):
    count = rows.shape[0]
    parts = stack_parts(rows, 3) + [jnp.zeros_like(rows)]
    sums = product(jnp.concatenate(parts, 0).astype(BF16), triangle)
    return sums[:count] + sums[count : 2 * count] + sums[2 * count : 3 * count]


def softplus(v):
    return jnp.maximum(v, 0.0) + jnp.log1p(jnp.exp(-jnp.abs(v)))


def turned(row, count):
    return jnp.broadcast_to(row, (8, count)).T[:, 0:1]


def chunk_decay(cum, rates, tok):
    last = cum[:, GROUP - 1 : GROUP]
    tail = (tok[0:1] == tok[0:1, GROUP - 1 : GROUP]).astype(F32)
    to_end = jnp.exp(last - cum) * tail
    enter = jnp.exp(cum) * tok[7:8]
    return to_end, enter


def fwd1_kernel(
    x_ref, xh_ref, gain_ref, wmain_ref, wstate_ref, wrate_ref, tok_ref, head_ref,
    kin_ref, kst_ref, tri_ref, spread_ref,
    gate_ref, pre_ref, st_ref, uv_ref, us_ref, bc_ref, rows_ref, sent_ref, prod_ref, fin_ref, total_ref, preh_ref, sth_ref, rinvh_ref,
    ext, state, prod,
):
    k = pl.program_id(0)
    width = x_ref.shape[0]
    hl = gate_ref.shape[1]
    heads = hl // HEADP

    def project(x):
        xf = x.astype(F32)
        rinv = lax.rsqrt(jnp.sum(xf * xf, axis=0, keepdims=True) / width + NORM_EPSILON)
        gain = gain_ref[...]
        if x.shape[1] > 128:
            gain = jnp.concatenate([gain] * (x.shape[1] // 128), 1)
        xn = (xf * gain).astype(BF16)
        col = turned(rinv, x.shape[1])
        return xn, rinv, col, mm_tn(xn, wmain_ref[...]) * col, (mm_tn(xn, wstate_ref[...]) * col).astype(BF16)

    @pl.when(k == 0)
    def _():
        _, _, rinv, main, state_in = project(xh_ref[...])
        at = slice(128 - HALO, 128)
        pre = main[at, hl:]
        preh_ref[...] = pre.astype(BF16)
        sth_ref[...] = state_in[at]
        rinvh_ref[...] = jnp.broadcast_to(rinv[at], (HALO, 128))
        ext[0:8, :hl] = pre[HALO - 8 :]
        ext[0:8, hl:] = state_in.astype(F32)[128 - 8 :]
        state[...] = jnp.zeros_like(state)
        prod[...] = jnp.ones_like(prod)

    xn, rinv, _, main, state_in = project(x_ref[...])
    gate_ref[...] = main[:, :hl]
    pre = main[:, hl:]
    pre_ref[...] = pre
    st_ref[...] = state_in
    ext[8:, :hl] = pre.astype(F32)
    ext[8:, hl:] = state_in.astype(F32)
    tok = tok_ref[...]
    cols = tok.T
    kernel = jnp.concatenate([kin_ref[...], kst_ref[...]], 1)
    u = ext[8:, :] * kernel[0:1] + kernel[4:5]
    for j in range(1, 4):
        u = u + ext[pl.ds(8 - j, GROUP), :] * cols[:, j : j + 1] * kernel[j : j + 1]
    ext[0:8, :] = ext[GROUP : GROUP + 8, :]
    uv_ref[...] = u[:, :hl]
    us_ref[...] = u[:, hl:]
    u = u.astype(F32)
    act = u * sigmoid(u)
    values = act[:, :hl]
    bc = act[:, hl:].astype(BF16)
    bc_ref[...] = bc
    rate = mm(wrate_ref[...], xn)
    rinv_row = jnp.broadcast_to(rinv, (heads, GROUP))
    rin = rate[:heads] * rinv_row + head_ref[heads : 2 * heads, 0:1]
    rates = softplus(rin)
    cum = running(head_ref[0:heads, 0:1] * rates, tri_ref[...])
    rows_ref[0:heads] = rin
    rows_ref[heads : 2 * heads] = rates
    rows_ref[2 * heads : 3 * heads] = cum
    rows_ref[3 * heads :] = rinv_row
    to_end, _ = chunk_decay(cum, rates, tok)
    both = expand(to_end * rates, spread_ref[...])
    scaled = (values * both).astype(BF16)
    carry = jnp.exp(cum[:, GROUP - 1 :]) * tok[7:8, GROUP - 1 :]
    carry = expand(jnp.broadcast_to(carry, (heads, 128)), spread_ref[...])[0:8]
    sent_ref[0] = state[...].astype(BF16)
    prod_ref[0] = prod[...]
    state[...] = state[...] * carry[0:1] + mm_tn(bc[:, :NSTATE], scaled)
    prod[...] = prod[...] * carry
    fin_ref[...] = state[...]
    total_ref[...] = prod[...]


def pair_lanes(shape):
    return lax.broadcasted_iota(jnp.int32, shape, 1) < HEADP


def chunk_mask(tok, cols):
    rowpos = lax.broadcasted_iota(jnp.int32, (GROUP, GROUP), 0)
    colpos = lax.broadcasted_iota(jnp.int32, (GROUP, GROUP), 1)
    same = (cols[:, 0:1] == tok[0:1, :]) & (colpos <= rowpos)
    return jnp.where(same, 0.0, FAR)


def fwd2_kernel(
    gate_ref, uv_ref, bc_ref, rows_ref, tok_ref, sent_ref, prod_ref, sin_ref, cot_ref, post_ref, skip_ref,
    woutt_ref, spread_ref,
    scan_ref, out_ref, dn_ref, stat_ref,
):
    row = lax.axis_index("row")
    hl = gate_ref.shape[1]
    heads = hl // HEADP
    blocks, depth, _ = out_ref.shape
    tok = tok_ref[...]
    cum = rows_ref[2 * heads : 3 * heads]
    rates = rows_ref[heads : 2 * heads]
    _, enter = chunk_decay(cum, rates, tok)
    spread = spread_ref[...]
    cols = jnp.concatenate([tok, cum], 0).T
    mask = chunk_mask(tok, cols)
    bm, cm = bc_ref[:, :NSTATE], bc_ref[:, NSTATE:]
    scores = mm_nt(cm, bm)
    u = uv_ref[...].astype(F32)
    values = u * sigmoid(u)
    scaled = (values * expand(rates, spread)).astype(BF16)
    entering = (sent_ref[0].astype(F32) + prod_ref[0, 0:1] * sin_ref[...]).astype(BF16)
    outer = mm(cm, entering) * expand(enter, spread)
    first = pair_lanes((GROUP, 128))
    pieces = []
    for pair in range(heads // 2):
        vp = scaled[:, pair * 128 : (pair + 1) * 128]
        ys = []
        for h in (2 * pair, 2 * pair + 1):
            decay = jnp.exp(cols[:, 8 + h : 9 + h] - cum[h : h + 1, :] + mask)
            ys.append(mm((scores * decay).astype(BF16), vp))
        pieces.append(jnp.where(first, ys[0], ys[1]))
    scan = jnp.concatenate(pieces, 1) + outer
    scan_ref[...] = scan
    g = gate_ref[...].astype(F32)
    gated = (scan + skip_ref[...] * values) * (g * sigmoid(g))
    post = post_ref[...]
    dn = mm_tn(cot_ref[...], woutt_ref[...])
    dn = dn.astype(BF16)
    dn_ref[...] = dn
    normed = gated * post
    squares, inner = lane_sums(gated * gated), lane_sums(dn.astype(F32) * normed)
    stat_ref[...] = jnp.where(
        lax.broadcasted_iota(jnp.int32, squares.shape, 0) == 0, squares, inner
    )
    normed = normed.astype(BF16)
    for i in range(blocks):
        block = mm_nt(woutt_ref[pl.ds(i * depth, depth), :], normed)
        out_ref[jnp.bitwise_xor(row, i)] = block.astype(BF16)


def bwd1_kernel(
    gate_ref, uv_ref, bc_ref, rows_ref, tok_ref, scan_ref, dn_ref, scal_ref, cot_ref, post_ref, skip_ref, spread_ref,
    dy_ref, dg_ref, leave_ref, prodb_ref, first_ref, gout_ref, sums_ref, root_ref,
    adj, prod, gacc,
):
    step = pl.program_id(0)
    hl = gate_ref.shape[1]
    heads = hl // HEADP
    tok = tok_ref[...]
    cum = rows_ref[2 * heads : 3 * heads]
    spread = spread_ref[...]

    @pl.when(step == 0)
    def _():
        adj[...] = jnp.zeros_like(adj)
        prod[...] = jnp.ones_like(prod)
        gacc[...] = jnp.zeros_like(gacc)
        sums_ref[...] = jnp.zeros_like(sums_ref)

    enter = jnp.exp(cum) * tok[7:8]
    scal = scal_ref[...]
    cols = jnp.concatenate([scal, rows_ref[3 * heads :]], 0).T
    rootgate, pull, rinv = cols[:, 0:1], cols[:, 1:2], cols[:, 8:9]
    u = uv_ref[...].astype(F32)
    values = u * sigmoid(u)
    mixed = scan_ref[...] + skip_ref[...] * values
    g = gate_ref[...].astype(F32)
    sg = sigmoid(g)
    act = g * sg
    gated = mixed * act
    post = post_ref[...]
    dn = dn_ref[...].astype(F32)
    dgated = rootgate * (dn * post) - gated * pull
    dy = dgated * act
    dyb = dy.astype(BF16)
    dy_ref[...] = dyb
    dgate = dgated * mixed * (sg + act * (1.0 - sg)) * rinv
    dg_ref[...] = dgate.astype(BF16)
    root_ref[...] = lane_sums(dgate * g)
    ng = gated * rootgate
    sums_ref[0:8] += jnp.sum((dn * ng).reshape(GROUP // 8, 8, hl), 0)
    sums_ref[8:16] += jnp.sum((dy * values).reshape(GROUP // 8, 8, hl), 0)
    normout = (ng * post).astype(BF16)
    gacc[...] += mm(cot_ref[...], normout)

    @pl.when(step == pl.num_programs(0) - 1)
    def _():
        gout_ref[...] = gacc[...].astype(BF16)

    cm = bc_ref[:, NSTATE:]
    weighted = (dyb.astype(F32) * expand(enter, spread)).astype(BF16)
    carry = jnp.exp(cum[:, GROUP - 1 :]) * tok[7:8, GROUP - 1 :]
    carry = expand(jnp.broadcast_to(carry, (heads, 128)), spread)[0:8]
    leave_ref[0] = adj[...].astype(BF16)
    prodb_ref[0] = prod[...]
    adj[...] = adj[...] * carry[0:1] + mm_tn(cm, weighted)
    prod[...] = prod[...] * carry
    first_ref[...] = adj[...]


class Delivery:
    def __init__(self, dims, refs, scal):
        nrow, ncol, ndp, fold = self.dims = dims
        (
            self.out, self.gout, self.home, self.hout,
            self.own, self.ra, self.rb, self.sb, self.sc, self.gv, self.ry, self.sy, self.rz, self.fin, self.rdp,
            send, recv, self.local,
        ) = refs
        self.scal = scal
        self.step, self.last = pl.program_id(0), pl.num_programs(0) - 1
        row, col, dp = (lax.axis_index(a) for a in ("row", "col", "dp"))
        w = self.w = Wires(send, recv)
        near, far, other, half = flip(row, 1), flip(row, 2), flip(dp, 1), lax.rem(dp, 2)
        self.plan = plan = order(ncol)[::-1]
        cols = [lax.rem(col + d, ncol) for d in range(ncol)]
        back = [lax.rem(col - d + ncol, ncol) for d in range(ncol)]
        tokens = self.out.shape[3]
        hs, sh = self.fin.shape[0], self.hout.shape[2]
        places = [pl.ds(pl.multiple_of(c * tokens, 128), tokens) for c in back]
        rows = [pl.ds(half * hs, hs), pl.ds((1 - half) * hs, hs)]
        self.starts = {name: [] for name in ("a", "y", "b", "c", "z", "h")}
        self.takes = {name: [] for name in ("a0", "a1", "y", "b", "c", "z", "h")}

        def wire(kind, at, src, dst, to, when=None):
            slot = w.slot()
            self.starts[kind].append((at, w.copy(slot, src, dst, to), when))
            w.sent.append(None)
            return slot

        def take(kind, at, slot, ref, to, when=None):
            self.takes[kind].append((at, w.copy(slot, ref, ref, to), when))

        for d in plan:
            take("a1", d, wire("a", d, self.out.at[3, cols[d]], self.ra.at[1, d], {"row": near}), self.ra.at[1, d], {"row": near})
            take("a0", d, wire("a", d, self.out.at[1, cols[d]], self.ra.at[0, d], {"row": near}), self.ra.at[0, d], {"row": near})
            take("y", d, wire("y", d, self.gout.at[cols[d], 1 - half], self.ry.at[d], {"dp": other}), self.ry.at[d], {"dp": other})
            take("b", d, wire("b", d, self.sb.at[d], self.rb.at[d], {"row": far}), self.rb.at[d], {"row": far})
            if d:
                to, come = {"col": cols[d]}, {"col": back[d]}
                slot = wire("c", d, self.sc.at[d], self.home.at[:, places[0]], to)
                take("c", d, slot, self.home.at[:, places[d]], come)
                take("z", d, wire("z", d, self.sy.at[d], self.rz.at[d], to), self.rz.at[d], come)
        self.cols = cols
        self.stays = pltpu.make_async_copy(self.sc.at[0], self.home.at[:, places[0]], self.local.at[3])
        self.loads = [
            pltpu.make_async_copy(self.out.at[0], self.own.at[0], self.local.at[0]),
            pltpu.make_async_copy(self.out.at[2], self.own.at[1], self.local.at[1]),
            pltpu.make_async_copy(self.gout.at[:, half], self.gv, self.local.at[2]),
        ]
        self.hops = []
        for i, bit in enumerate(bits(ndp)[1:]):
            to = {"dp": flip(dp, bit)}
            self.hops.append(w.copy(w.slot(), self.rdp.at[2 * i], self.rdp.at[2 * i + 1], to))
            w.sent.append(None)
        self.keeps = []
        for i in range(fold):
            orow, ocol = col // fold, row * fold + i
            away = (orow != row) | (ocol != col)
            src = self.fin.at[:, pl.ds(i * sh, sh)]
            for j in range(fold):
                this = lax.rem(col, fold) == j
                dst = self.hout.at[j, rows[0]]
                near_slot, far_slot = w.slot(), w.slot()
                if i == 0:
                    self.slots = getattr(self, "slots", []) + [(near_slot, far_slot)]
                near_slot, far_slot = self.slots[j]
                to = {"row": orow, "col": ocol}
                self.starts["h"].append((j, w.copy(near_slot, src, dst, to), away & this))
                w.sent.append(None)
                self.starts["h"].append((j, w.copy(far_slot, src, dst, to | {"dp": other}), this))
                w.sent.append(None)
                keep = pltpu.make_async_copy(src, dst, self.local.at[4])
                self.keeps.append((keep, ~away & this))
        for j in range(fold):
            srow, scol = col // fold, row * fold + j
            to = {"row": srow, "col": scol}
            take("h", j, self.slots[j][0], self.hout.at[j, rows[0]], to, (srow != row) | (scol != col))
            take("h", j, self.slots[j][1], self.hout.at[j, rows[1]], to | {"dp": other})

    def go(self, kind, at=None):
        for d, copy, when in self.starts[kind]:
            if at is None or d == at:
                copy.start() if when is None else pl.when(when)(copy.start)

    def come(self, kind, at=None):
        for d, copy, when in self.takes[kind]:
            if at is None or d == at:
                copy.wait_recv() if when is None else pl.when(when)(copy.wait_recv)

    def before(self):
        nrow, ncol, ndp, fold = self.dims
        step, last, plan = self.step, self.last, self.plan

        @pl.when(step == 0)
        def _():
            greet(nrow, ncol, ndp)
            self.go("a")
            self.go("y")
            for load in self.loads:
                load.start()

        @pl.when(step == 1)
        def _():
            for load in self.loads:
                load.wait()
            for d in plan:
                self.come("a1", d)
                self.sb[d] = (self.own[1, self.cols[d]].astype(F32) + self.ra[1, d].astype(F32)).astype(BF16)
                self.go("b", d)

        for i, d in enumerate(plan):

            @pl.when(step == jnp.minimum(2 + i, last - 1))
            def _():
                self.come("a0", d)
                self.come("b", d)
                total = self.own[0, self.cols[d]].astype(F32) + self.ra[0, d].astype(F32) + self.rb[d].astype(F32)
                self.sc[d] = (total * self.scal[0:1]).astype(BF16)
                if d:
                    self.go("c", d)
                else:
                    self.stays.start()

        @pl.when(step == jnp.minimum(3, last - 1))
        def _():
            for d in plan:
                self.come("y", d)
                self.sy[d] = (self.gv[self.cols[d]].astype(F32) + self.ry[d].astype(F32)).astype(BF16)
                if d:
                    self.go("z", d)

        @pl.when(step == last)
        def _():
            total = self.sy[0].astype(F32)
            for d in range(1, ncol):
                self.come("z", d)
                total = total + self.rz[d].astype(F32)
            for i, hop in enumerate(self.hops):
                self.rdp[2 * i] = total
                hop.start()
                hop.wait_recv()
                total = total + self.rdp[2 * i + 1]
            self.fin[...] = total.astype(BF16)
            self.go("h")
            for keep, when in self.keeps:
                pl.when(when)(keep.start)

    def after(self):
        @pl.when(self.step == self.last)
        def _():
            for keep, when in self.keeps:
                pl.when(when)(keep.wait)
            self.come("h")
            self.come("c")
            self.stays.wait()
            for hop in self.hops:
                hop.wait_send()
            for copies in self.starts.values():
                for _, copy, when in copies:
                    copy.wait_send() if when is None else pl.when(when)(copy.wait_send)


def delivery_scratch(nrow, ncol, ndp, fold, own, tokens, hs, hl):
    nb = len(bits(ndp))
    slots = 8 * ncol + nb + 2 * fold * fold + 4
    return [
        pltpu.VMEM((2, ncol, own, tokens), BF16),
        pltpu.VMEM((2, ncol, own, tokens), BF16),
        pltpu.VMEM((ncol, own, tokens), BF16),
        pltpu.VMEM((ncol, own, tokens), BF16),
        pltpu.VMEM((ncol, own, tokens), BF16),
        pltpu.VMEM((ncol, hs, hl), BF16),
        pltpu.VMEM((ncol, hs, hl), BF16),
        pltpu.VMEM((ncol, hs, hl), BF16),
        pltpu.VMEM((ncol, hs, hl), BF16),
        pltpu.VMEM((hs, hl), BF16),
        pltpu.VMEM((max(2 * nb - 2, 1), hs if ndp > 2 else 8, hl), F32),
        pltpu.SemaphoreType.DMA((slots,)),
        pltpu.SemaphoreType.DMA((slots,)),
        pltpu.SemaphoreType.DMA((5,)),
    ]


def bwd2_kernel(
    dims,
    x_ref, xh_ref, gain_ref, wmain_ref, wstate_ref, wrate_ref, tok_ref, head_ref, hmask_ref, hrinv_ref,
    kin_ref, kst_ref, tri_ref, spread_ref, skip_ref,
    pre_ref, st_ref, preh_ref, sth_ref, uv_ref, us_ref, bc_ref, rows_ref, sent_ref, prod_ref, sin_ref,
    scan_ref, dy_ref, dg_ref, leave_ref, prodb_ref, din_ref, root_ref, scal_ref, outs_ref, gout_ref,
    home_ref, hout_ref, gin_ref, ginh_ref, gw_ref, gs_ref, gr_ref, gk_ref, gh_ref, gp_ref,
    ext, gacc, *more,
):
    delivery = Delivery(dims, (outs_ref, gout_ref, home_ref, hout_ref) + more, scal_ref)
    delivery.before()
    step = pl.program_id(0)
    steps = pl.num_programs(0)
    row = lax.axis_index("row")
    hl = uv_ref.shape[1]
    heads = hl // HEADP
    width = x_ref.shape[0]
    blocks, depth, _ = gin_ref.shape
    tok = tok_ref[...]
    spread = spread_ref[...]
    rin = rows_ref[0:heads]
    rates = rows_ref[heads : 2 * heads]
    cum = rows_ref[2 * heads : 3 * heads]
    rinv_row = rows_ref[3 * heads :]
    cols = jnp.concatenate([tok, cum, rinv_row], 0).T
    rinv = cols[:, 16:17]

    @pl.when(step == 0)
    def _():
        ext[GROUP:, :] = jnp.zeros_like(ext[GROUP:, :])
        gacc[...] = jnp.zeros_like(gacc)
        gr_ref[...] = jnp.zeros_like(gr_ref)
        gk_ref[...] = jnp.zeros_like(gk_ref)
        gh_ref[...] = jnp.zeros_like(gh_ref)
        gp_ref[...] = jnp.zeros_like(gp_ref)

    to_end, enter = chunk_decay(cum, rates, tok)
    mask = chunk_mask(tok, cols)
    bm, cm = bc_ref[:, :NSTATE], bc_ref[:, NSTATE:]
    scores = mm_nt(cm, bm)
    u = uv_ref[...].astype(F32)
    sg = sigmoid(u)
    values = u * sg
    rexp = expand(rates, spread)
    scaled = (values * rexp).astype(BF16)
    dyb = dy_ref[...]
    entering = (sent_ref[0].astype(F32) + prod_ref[0, 0:1] * sin_ref[...]).astype(BF16)
    leaving = (leave_ref[0].astype(F32) + prodb_ref[0, 0:1] * din_ref[...]).astype(BF16)

    first = pair_lanes((GROUP, 128))
    dscores = jnp.zeros((GROUP, GROUP), F32)
    pieces = []
    for pair in range(heads // 2):
        vp = scaled[:, pair * 128 : (pair + 1) * 128]
        dp = dyb[:, pair * 128 : (pair + 1) * 128]
        dvs = []
        for h in (2 * pair, 2 * pair + 1):
            decay = jnp.exp(cols[:, 8 + h : 9 + h] - cum[h : h + 1, :] + mask)
            weight = (scores * decay).astype(BF16)
            own = first if h % 2 == 0 else ~first
            dh = jnp.where(own, dp, jnp.zeros_like(dp))
            dscores = dscores + mm_nt(dh, vp) * decay
            dvs.append(mm_tn(weight, dp))
        pieces.append(jnp.where(first, dvs[0], dvs[1]))
    tend = expand(to_end, spread)
    inside = jnp.concatenate(pieces, 1)
    onward = mm(bm, leaving) * tend
    dscaled = inside + onward
    dsb = dscores.astype(BF16)
    dyf = dyb.astype(F32)
    weighted = (dyf * expand(enter, spread)).astype(BF16)
    ended = (values * (tend * rexp)).astype(BF16)
    dcm = mm(dsb, bm) + mm_nt(weighted, entering)
    dbm = mm_tn(dsb, cm) + mm_nt(ended, leaving)
    dvalues = dscaled * rexp + skip_ref[...] * dyf

    kept = scaled.astype(F32)
    dcum = head_sums(dyf * scan_ref[...] - kept * inside, spread)
    dend = head_sums(kept * onward, spread)
    drates = head_sums(values * dscaled, spread)
    through = leaving.astype(F32) * entering.astype(F32)
    through = head_sums(jnp.sum(through.reshape(NSTATE // 8, 8, hl), 0), spread)
    through = jnp.sum(through, axis=1, keepdims=True) * (
        jnp.exp(cum[:, GROUP - 1 :]) * tok[7:8, GROUP - 1 :]
    )
    ddec = running(dcum, tri_ref[...], mm_nt) + running(dend, tri_ref[...]) - dend + through
    drates = drates + head_ref[0:heads, 0:1] * ddec
    drin = drates * sigmoid(rin)
    gh_ref[0:heads] += ddec * (head_ref[0:heads, 0:1] * rates)
    gh_ref[heads : 2 * heads] += drin

    us = us_ref[...].astype(F32)
    ss = sigmoid(us)
    dstates = jnp.concatenate([dbm, dcm], 1)
    ext[0:GROUP, :hl] = dvalues * (sg + values * (1.0 - sg))
    ext[0:GROUP, hl:] = dstates * (ss + us * ss * (1.0 - ss))
    kernel = jnp.concatenate([kin_ref[...], kst_ref[...]], 1)
    source = jnp.concatenate([pre_ref[...], st_ref[...]], 1).astype(F32)
    du = ext[0:GROUP, :]
    gk_ref[32:40] += jnp.sum(du.reshape(GROUP // 8, 8, du.shape[1]), 0)
    gk_ref[0:8] += jnp.sum((du * source).reshape(GROUP // 8, 8, du.shape[1]), 0)
    dsource = du * kernel[0:1]
    for j in range(1, 4):
        moved = ext[pl.ds(j, GROUP), :] * cols[:, 3 + j : 4 + j]
        gk_ref[8 * j : 8 * j + 8] += jnp.sum(
            (moved * source).reshape(GROUP // 8, 8, du.shape[1]), 0
        )
        dsource = dsource + moved * kernel[j : j + 1]
    low = dsource * rinv
    lowb = low.astype(BF16)
    root = lane_sums(low * source) + root_ref[...] + jnp.sum(
        drin * (rin - head_ref[heads : 2 * heads, 0:1]), 0, keepdims=True
    ) * rinv_row[0:1]
    root = root[0:1] * rinv_row[0:1] / width
    ratelow = (drin * rinv_row).astype(F32)
    ratelow = jnp.concatenate([ratelow, jnp.zeros_like(ratelow)], 0).astype(BF16)
    gates = dg_ref[...]
    xf = x_ref[...].astype(F32)
    gain = jnp.concatenate([gain_ref[...]] * (GROUP // 128), 1)
    xn = (xf * gain).astype(BF16)
    gacc[:, 0:hl] += mm(xn, gates)
    gacc[:, hl:] += mm(xn, lowb)
    gr_ref[...] += mm_nt(ratelow, xn)
    dn = (
        mm_nt(wmain_ref[:, 0:hl], gates)
        + mm_nt(wmain_ref[:, hl:], lowb[:, :hl])
        + mm_nt(wstate_ref[...], lowb[:, hl:])
        + mm_tn(wrate_ref[...], ratelow)
    )
    both = dn * xf
    for at in range(0, GROUP, 128):
        gp_ref[...] += both[:, at : at + 128]
    grad = (dn * gain - xf * root).astype(BF16)
    for i in range(blocks):
        gin_ref[jnp.bitwise_xor(row, i)] = grad[i * depth : (i + 1) * depth]

    ext[GROUP : GROUP + 8, :] = ext[0:8, :]

    @pl.when(step == steps - 1)
    def _():
        wide = ext.shape[1]
        source_h = jnp.concatenate([preh_ref[...], sth_ref[...]], 1).astype(F32)
        head8 = ext[GROUP : GROUP + 8, :]
        ext[0:HALO, :] = jnp.zeros((HALO, wide), F32)
        ext[HALO : HALO + 8, :] = head8
        dsource_h = jnp.zeros((HALO, wide), F32)
        for j in range(1, 4):
            moved = ext[pl.ds(j, HALO), :] * hmask_ref[:, j : j + 1]
            gk_ref[8 * j : 8 * j + 8] += jnp.sum(
                (moved * source_h).reshape(HALO // 8, 8, wide), 0
            )
            dsource_h = dsource_h + moved * kernel[j : j + 1]
        rinv_h = hrinv_ref[:, 0:1]
        low_h = dsource_h * rinv_h
        root_h = jnp.sum(low_h * source_h, axis=1, keepdims=True) * rinv_h / width
        fill = jnp.zeros((128 - HALO, wide), F32)
        lowb_h = jnp.concatenate([fill, low_h], 0).astype(BF16)
        root_h = jnp.concatenate([jnp.zeros((128 - HALO, 1), F32), root_h], 0)
        root_h = jnp.broadcast_to(root_h, (128, 128)).T[0:1]
        xf = xh_ref[...].astype(F32)
        gain = gain_ref[...]
        gacc[:, hl:] += mm((xf * gain).astype(BF16), lowb_h)
        dn = mm_nt(wmain_ref[:, hl:], lowb_h[:, :hl]) + mm_nt(wstate_ref[...], lowb_h[:, hl:])
        gp_ref[...] += dn * xf
        grad = (dn * gain - xf * root_h).astype(BF16)
        for i in range(blocks):
            ginh_ref[jnp.bitwise_xor(row, i)] = grad[i * depth : (i + 1) * depth]
        gw_ref[...] = gacc[:, 0 : 2 * hl].astype(BF16)
        gs_ref[...] = gacc[:, 2 * hl :].astype(BF16)

    delivery.after()


MESH = pl.DeviceIdType.MESH


class Wires:
    def __init__(self, send, recv):
        self.sends, self.recv, self.used, self.sent = send, recv, 0, []

    def slot(self):
        self.used += 1
        return self.used - 1

    def copy(self, slot, src, dst, to):
        return pltpu.make_async_remote_copy(
            src_ref=src,
            dst_ref=dst,
            send_sem=self.sends.at[len(self.sent)],
            recv_sem=self.recv.at[slot],
            device_id=to,
            device_id_type=MESH,
        )

    def start(self, slot, src, dst, to, when=None):
        copy = self.copy(slot, src, dst, to)
        if when is None:
            copy.start()
        else:
            pl.when(when)(copy.start)
        self.sent.append((copy, when))

    def arrived(self, slot, ref, to):
        pltpu.make_async_remote_copy(
            src_ref=ref,
            dst_ref=ref,
            send_sem=self.sends.at[0],
            recv_sem=self.recv.at[slot],
            device_id=to,
            device_id_type=MESH,
        ).wait_recv()

    def finish(self):
        for copy, when in self.sent:
            if when is None:
                copy.wait_send()
            else:
                pl.when(when)(copy.wait_send)


def greet(nrow, ncol, ndp):
    row, col, dp = (lax.axis_index(a) for a in ("row", "col", "dp"))
    sem = pltpu.get_barrier_semaphore()
    total = 0
    for i in range(nrow):
        for j in range(ncol):
            if i or j:
                to = {"row": lax.rem(row + i, nrow), "col": lax.rem(col + j, ncol)}
                pl.semaphore_signal(sem, 1, device_id=to, device_id_type=MESH)
                total += 1
    for bit in bits(ndp):
        pl.semaphore_signal(sem, 1, device_id={"dp": flip(dp, bit)}, device_id_type=MESH)
        total += 1
    pl.semaphore_wait(sem, total)


def bits(size):
    found, bit = [], 1
    while bit < size:
        found.append(bit)
        bit *= 2
    return found


def flip(index, bit):
    return index + bit - 2 * bit * lax.rem(index // bit, 2)


def order(ncol):
    near = [0]
    for d in range(1, ncol // 2 + 1):
        near.extend([d, ncol - d] if ncol - d != d else [d])
    return near


class Spread:
    def __init__(self, wires, ncol, source, out):
        self.w, self.ncol, self.source, self.out = wires, ncol, source, out
        self.row, self.col = lax.axis_index("row"), lax.axis_index("col")
        self.far, self.near = flip(self.row, 2), flip(self.row, 1)
        self.a = [wires.slot() for _ in range(ncol)]
        self.b = [wires.slot() for _ in range(ncol)]
        self.e = [wires.slot() for _ in range(ncol)]
        self.f = [wires.slot() for _ in range(ncol)]

    def begin(self):
        for d in order(self.ncol)[:0:-1]:
            to = lax.rem(self.col + d, self.ncol)
            self.w.start(self.a[d], self.source(to), self.out.at[self.row, self.col], {"col": to})

    def forward(self, d):
        at = lax.rem(self.col - d + self.ncol, self.ncol)
        place = self.out.at[self.row, at]
        src = place
        if d:
            self.w.arrived(self.a[d], place, {"col": at})
        else:
            src = self.source(self.col)
        self.w.start(self.b[d], src, place, {"row": self.far})
        self.w.start(self.e[d], src, place, {"row": self.near})

    def relay(self, d):
        at = lax.rem(self.col - d + self.ncol, self.ncol)
        place = self.out.at[self.far, at]
        self.w.arrived(self.b[d], place, {"row": self.far})
        self.w.start(self.f[d], place, place, {"row": self.near})

    def end(self):
        for d in range(self.ncol):
            at = lax.rem(self.col - d + self.ncol, self.ncol)
            self.w.arrived(self.e[d], self.out.at[self.near, at], {"row": self.near})
            self.w.arrived(self.f[d], self.out.at[flip(self.near, 2), at], {"row": self.near})


def moved(src, mid, dst, sem):
    pltpu.make_async_copy(src, mid, sem).start()
    pltpu.make_async_copy(src, mid, sem).wait()
    pltpu.make_async_copy(mid, dst, sem).start()


def enter_kernel(nrow, ncol, ndp, fold, xs, cs, ws, ss, xo, ho, co, wo, so, xv, hv, cv, wv, sv, send, recv, local):
    row, col, dp = (lax.axis_index(a) for a in ("row", "col", "dp"))
    w = Wires(send, recv)
    greet(nrow, ncol, ndp)
    tokens = xo.shape[3]

    def tokens_of(ref, to):
        return ref.at[:, pl.ds(pl.multiple_of(to * tokens, 128), tokens)]

    def before(ref, to):
        at = jnp.maximum(to * tokens - 128, 0)
        return ref.at[:, pl.ds(pl.multiple_of(at, 128), 128)]

    spreads = [
        Spread(w, ncol, lambda to: ss, so),
        Spread(w, ncol, lambda to: before(xs, to), ho),
        Spread(w, ncol, lambda to: tokens_of(xs, to), xo),
        Spread(w, ncol, lambda to: tokens_of(cs, to), co),
    ]
    half, other = lax.rem(dp, 2), flip(dp, 1)
    hs = ws.shape[1] // 2
    mine, theirs = pl.ds(half * hs, hs), pl.ds((1 - half) * hs, hs)
    w1 = [w.slot() for _ in range(fold)]
    left = [w.slot() for _ in range(ncol)]
    right = [w.slot() for _ in range(ncol)]
    cross = [w.slot() for _ in range(2 * ncol)]

    for j in range(fold):
        tr, tc = col // fold, row * fold + j
        away = (tr != row) | (tc != col)
        for i in range(fold):
            w.start(
                w1[i], ws.at[j, mine], wo.at[tc, i, mine], {"row": tr, "col": tc},
                away & (lax.rem(col, fold) == i),
            )

        @pl.when(~away)
        def _():
            i = lax.rem(col, fold)
            moved(ws.at[j, mine], wv, wo.at[col, i, mine], local.at[0])
            pltpu.make_async_copy(wv, wo.at[col, i, mine], local.at[0]).wait()

    for s in spreads:
        s.begin()
    moved(ss, sv, so.at[row, col], local.at[1])
    moved(tokens_of(xs, col), xv, xo.at[row, col], local.at[2])
    moved(tokens_of(cs, col), cv, co.at[row, col], local.at[3])
    moved(before(xs, col), hv, ho.at[row, col], local.at[4])
    for s in spreads:
        s.forward(0)
    for i in range(fold):
        sr, sc = col // fold, row * fold + i

        @pl.when((sr != row) | (sc != col))
        def _():
            w.arrived(w1[i], wo.at[col, i, mine], {"row": sr, "col": sc})

    def unit(c, rows):
        return wo.at[c, :, rows]

    own = unit(col, mine)
    w.start(left[1], own, own, {"col": col + 1}, col + 1 < ncol)
    w.start(right[1], own, own, {"col": col - 1}, col >= 1)
    w.start(cross[0], own, own, {"dp": other})
    steps = order(ncol)
    for at in range(1, ncol):
        d = steps[at]
        for s in spreads:
            s.forward(d)
        for s in spreads:
            s.relay(steps[at - 1])

        @pl.when(col >= at)
        def _():
            w.arrived(left[at], unit(col - at, mine), {"col": col - 1})

        got = unit(col - at, mine)
        w.start(left[min(at + 1, ncol - 1)], got, got, {"col": col + 1}, (col >= at) & (col + 1 < ncol))
        w.start(cross[at], got, got, {"dp": other}, col >= at)

        @pl.when(col + at < ncol)
        def _():
            w.arrived(right[at], unit(col + at, mine), {"col": col + 1})

        got = unit(col + at, mine)
        w.start(right[min(at + 1, ncol - 1)], got, got, {"col": col - 1}, (col + at < ncol) & (col >= 1))
        w.start(cross[ncol + at], got, got, {"dp": other}, col + at < ncol)
    for s in spreads:
        s.relay(steps[-1])
    w.arrived(cross[0], unit(col, theirs), {"dp": other})
    for at in range(1, ncol):

        @pl.when(col >= at)
        def _():
            w.arrived(cross[at], unit(col - at, theirs), {"dp": other})

        @pl.when(col + at < ncol)
        def _():
            w.arrived(cross[ncol + at], unit(col + at, theirs), {"dp": other})

    for s in spreads:
        s.end()
    pltpu.make_async_copy(sv, so.at[row, col], local.at[1]).wait()
    pltpu.make_async_copy(xv, xo.at[row, col], local.at[2]).wait()
    pltpu.make_async_copy(cv, co.at[row, col], local.at[3]).wait()
    pltpu.make_async_copy(hv, ho.at[row, col], local.at[4]).wait()
    w.finish()


ANYWHERE = pl.BlockSpec(memory_space=pl.ANY)
ONCHIP = pl.BlockSpec(memory_space=pltpu.VMEM)


def enter(nrow, ncol, ndp, fold, xs, cs, ws, ss):
    own, tokens = xs.shape[0], xs.shape[1] // ncol
    slots = 16 * ncol + fold + 4 * ncol
    return pl.pallas_call(
        functools.partial(enter_kernel, nrow, ncol, ndp, fold),
        out_shape=[
            jax.ShapeDtypeStruct((nrow, ncol, own, tokens), BF16),
            jax.ShapeDtypeStruct((nrow, ncol, own, 128), BF16),
            jax.ShapeDtypeStruct((nrow, ncol, own, tokens), BF16),
            jax.ShapeDtypeStruct((ncol,) + ws.shape, BF16),
            jax.ShapeDtypeStruct((nrow, ncol) + ss.shape, BF16),
        ],
        in_specs=[ANYWHERE] * 4,
        out_specs=[ANYWHERE] * 5,
        scratch_shapes=[
            pltpu.VMEM((own, tokens), BF16),
            pltpu.VMEM((own, 128), BF16),
            pltpu.VMEM((own, tokens), BF16),
            pltpu.VMEM((ws.shape[1] // 2, ws.shape[2]), BF16),
            pltpu.VMEM(ss.shape, BF16),
            pltpu.SemaphoreType.DMA((20 * ncol + 8 + fold * fold,)),
            pltpu.SemaphoreType.DMA((slots,)),
            pltpu.SemaphoreType.DMA((5,)),
        ],
        compiler_params=pltpu.CompilerParams(collective_id=0, has_side_effects=True),
        name="enter",
    )(xs, cs, ws, ss)


def shift_kernel(ncol, by, src, dst, buf, send, recv, local):
    col = lax.axis_index("col")
    to, back = col + by, col - by
    sends = (to >= 0) & (to < ncol)
    takes = (back >= 0) & (back < ncol)
    sem = pltpu.get_barrier_semaphore()

    @pl.when(takes)
    def _():
        pl.semaphore_signal(sem, 1, device_id={"col": back}, device_id_type=MESH)

    def wire():
        return pltpu.make_async_remote_copy(
            src_ref=src, dst_ref=buf, send_sem=send, recv_sem=recv,
            device_id={"col": to}, device_id_type=MESH,
        )

    @pl.when(sends)
    def _():
        pl.semaphore_wait(sem, 1)
        wire().start()

    @pl.when(~takes)
    def _():
        buf[...] = jnp.zeros_like(buf)

    @pl.when(takes)
    def _():
        wire().wait_recv()

    @pl.when(sends)
    def _():
        wire().wait_send()

    dst[...] = buf[...]


def shift(ncol, by, block, ident):
    return pl.pallas_call(
        functools.partial(shift_kernel, ncol, by),
        out_shape=jax.ShapeDtypeStruct(block.shape, block.dtype),
        in_specs=[ONCHIP],
        out_specs=ONCHIP,
        scratch_shapes=[
            pltpu.VMEM(block.shape, block.dtype),
            pltpu.SemaphoreType.DMA(()),
            pltpu.SemaphoreType.DMA(()),
            pltpu.SemaphoreType.DMA(()),
        ],
        compiler_params=pltpu.CompilerParams(collective_id=ident, has_side_effects=True),
        name=f"shift{ident}",
    )(block)


def gather_kernel(nrow, count, stat, scal, buf, send, recv):
    row = lax.axis_index("row")
    sem = pltpu.get_barrier_semaphore()
    for d in range(1, nrow):
        pl.semaphore_signal(sem, 1, device_id={"row": lax.rem(row + d, nrow)}, device_id_type=MESH)
    pl.semaphore_wait(sem, nrow - 1)
    w = Wires(send, recv)
    for d in range(1, nrow):
        w.start(d, stat, buf.at[d], {"row": lax.rem(row + d, nrow)})
    total = stat[...]
    for d in range(1, nrow):
        w.arrived(d, buf.at[d], {"row": lax.rem(row + d, nrow)})
        total = total + buf[d]
    w.finish()
    rootgate = lax.rsqrt(total[0:1] / count + NORM_EPSILON)
    pull = rootgate * rootgate * rootgate * total[1:2] / count
    first = lax.broadcasted_iota(jnp.int32, total.shape, 0) == 0
    scal[...] = jnp.where(first, rootgate, pull)


def gather_stat(nrow, count, stat):
    return pl.pallas_call(
        functools.partial(gather_kernel, nrow, count),
        out_shape=jax.ShapeDtypeStruct(stat.shape, F32),
        in_specs=[ONCHIP],
        out_specs=ONCHIP,
        scratch_shapes=[
            pltpu.VMEM((nrow,) + stat.shape, F32),
            pltpu.SemaphoreType.DMA((nrow,)),
            pltpu.SemaphoreType.DMA((nrow,)),
        ],
        compiler_params=pltpu.CompilerParams(collective_id=1, has_side_effects=True),
        name="stat",
    )(stat)


def leave_kernel(
    nrow, ncol, ndp, fold,
    gin, ginh, gw, gs, sm,
    go, gho, ho, so, smo,
    own, ra, rb, sb, sc, hown, hra, hrb, hsb, hsc, gwv, ry, sy, rz, fin, rdp, gsv, rs1, ss1, rs2, rs3, smb, smr, send, recv, local,
):
    row, col, dp = (lax.axis_index(a) for a in ("row", "col", "dp"))
    w = Wires(send, recv)
    greet(nrow, ncol, ndp)
    near, far, other, half = flip(row, 1), flip(row, 2), flip(dp, 1), lax.rem(dp, 2)
    cols = [lax.rem(col + d, ncol) for d in range(ncol)]
    from_col = [lax.rem(col - d + ncol, ncol) for d in range(ncol)]
    plan = order(ncol)[::-1]

    loads = {}

    def load(name, src, dst, at):
        loads[name] = pltpu.make_async_copy(src, dst, local.at[at])
        loads[name].start()

    a0 = [w.slot() for _ in range(ncol)]
    a1 = [w.slot() for _ in range(ncol)]
    b = [w.slot() for _ in range(ncol)]
    c_ = [w.slot() for _ in range(ncol)]
    y = [w.slot() for _ in range(ncol)]
    z = [w.slot() for _ in range(ncol)]
    tokens = gin.shape[3]
    ha, hb = [w.slot() for _ in range(2)], w.slot()
    hc = [w.slot() for _ in range(ncol)]
    w.start(ha[1], ginh.at[3], hra.at[1], {"row": near})
    w.start(ha[0], ginh.at[1], hra.at[0], {"row": near})
    load("h0", ginh.at[0], hown.at[0], 8)
    load("h1", ginh.at[2], hown.at[1], 9)
    place = pl.ds(pl.multiple_of(col * tokens, 128), tokens)
    for d in plan:
        w.start(a1[d], gin.at[3, cols[d]], ra.at[1, d], {"row": near})
        w.start(a0[d], gin.at[1, cols[d]], ra.at[0, d], {"row": near})
    for d in plan:
        w.start(y[d], gw.at[cols[d], 1 - half], ry.at[d], {"dp": other})
    load("own0", gin.at[0], own.at[0], 0)
    load("own1", gin.at[2], own.at[1], 1)
    load("gw", gw.at[:, half], gwv, 2)
    load("gs", gs.at[row], gsv, 3)
    load("sm", sm, smb.at[0], 4)
    s1 = [w.slot() for _ in range(nrow)]
    for d in range(1, nrow):
        to = lax.rem(row + d, nrow)
        w.start(s1[d], gs.at[to], rs1.at[d], {"row": to})

    loads["sm"].wait()
    hops = [("dp", bit) for bit in bits(ndp)] + [("col", bit) for bit in bits(ncol)]
    sms = [w.slot() for _ in hops]
    at = {"dp": dp, "col": col}

    def small_send(i):
        axis, bit = hops[i]
        w.start(sms[i], smb.at[i], smr.at[i], {axis: flip(at[axis], bit)})

    def small_take(i):
        axis, bit = hops[i]
        w.arrived(sms[i], smr.at[i], {axis: flip(at[axis], bit)})
        smb[i + 1] = smb[i] + smr[i]

    small_send(0)

    loads["own0"].wait()
    loads["own1"].wait()
    loads["h0"].wait()
    loads["h1"].wait()
    w.arrived(ha[1], hra.at[1], {"row": near})
    hsb[...] = (hown[1].astype(F32) + hra[1].astype(F32)).astype(BF16)
    w.start(hb, hsb, hrb, {"row": far})
    for d in plan:
        w.arrived(a1[d], ra.at[1, d], {"row": near})
        sb[d] = (own[1, cols[d]].astype(F32) + ra[1, d].astype(F32)).astype(BF16)
        w.start(b[d], sb.at[d], rb.at[d], {"row": far})
    small_take(0)
    if len(hops) > 1:
        small_send(1)

    loads["gw"].wait()

    def features(d):
        w.arrived(a0[d], ra.at[0, d], {"row": near})
        w.arrived(b[d], rb.at[d], {"row": far})
        total = own[0, cols[d]].astype(F32) + ra[0, d].astype(F32) + rb[d].astype(F32)
        sc[d] = total.astype(BF16)
        if d:
            w.start(c_[d], sc.at[d], go.at[:, place], {"col": cols[d]})
            w.start(hc[d], hsc.at[cols[d]], gho.at[col], {"col": cols[d]})
        else:
            pltpu.make_async_copy(sc.at[0], go.at[:, place], local.at[5]).start()
            pltpu.make_async_copy(hsc.at[col], gho.at[col], local.at[10]).start()

    def weights(d):
        w.arrived(y[d], ry.at[d], {"dp": other})
        sy[d] = (gwv[cols[d]].astype(F32) + ry[d].astype(F32)).astype(BF16)
        if d:
            w.start(z[d], sy.at[d], rz.at[d], {"col": cols[d]})

    w.arrived(ha[0], hra.at[0], {"row": near})
    w.arrived(hb, hrb, {"row": far})
    hsc[...] = (hown[0].astype(F32) + hra[0].astype(F32) + hrb[...].astype(F32)).astype(BF16)
    for d in plan:
        features(d)
        weights(d)

    loads["gs"].wait()
    total = gsv[...].astype(F32)
    for d in range(1, nrow):
        w.arrived(s1[d], rs1.at[d], {"row": lax.rem(row - d + nrow, nrow)})
        total = total + rs1[d].astype(F32)
    ss1[...] = total.astype(BF16)
    part = so.shape[0]
    s2 = [w.slot() for _ in range(ncol)]
    for d in plan[:-1]:
        w.start(s2[d], ss1.at[pl.ds(cols[d] * part, part)], rs2.at[d], {"col": cols[d]})
    for i in range(1, len(hops)):
        small_take(i)
        if i + 1 < len(hops):
            small_send(i + 1)
    last = len(hops)
    s4 = [w.slot() for _ in range(nrow)]
    for d in range(1, nrow):
        w.start(s4[d], smb.at[last], smo.at[row], {"row": lax.rem(row + d, nrow)})
    pltpu.make_async_copy(smb.at[last], smo.at[row], local.at[6]).start()

    total = ss1[pl.ds(pl.multiple_of(col * part, part), part), :].astype(F32)
    for d in range(1, ncol):
        w.arrived(s2[d], rs2.at[d], {"col": from_col[d]})
        total = total + rs2[d].astype(F32)
    rs3[0] = total
    s3 = [w.slot() for _ in bits(ndp)]
    for i, bit in enumerate(bits(ndp)):
        w.start(s3[i], rs3.at[2 * i], rs3.at[2 * i + 1], {"dp": flip(dp, bit)})
        w.arrived(s3[i], rs3.at[2 * i + 1], {"dp": flip(dp, bit)})
        total = total + rs3[2 * i + 1]
        rs3[2 * i + 2] = total
    so[...] = total

    total = sy[0].astype(F32)
    for d in range(1, ncol):
        w.arrived(z[d], rz.at[d], {"col": from_col[d]})
        total = total + rz[d].astype(F32)
    if ndp > 2:
        fin[...] = total.astype(BF16)
        for i, bit in enumerate(bits(ndp)[1:]):
            slot = w.slot()
            rdp[2 * i] = total
            w.start(slot, rdp.at[2 * i], rdp.at[2 * i + 1], {"dp": flip(dp, bit)})
            w.arrived(slot, rdp.at[2 * i + 1], {"dp": flip(dp, bit)})
            total = total + rdp[2 * i + 1]
    fin[...] = total.astype(BF16)
    hs = fin.shape[0]
    sh = ho.shape[3]
    mine, theirs = pl.ds(half * hs, hs), pl.ds((1 - half) * hs, hs)
    count = ho.shape[0]
    h1 = [[w.slot() for _ in range(fold)] for _ in range(count)]
    h2 = [[w.slot() for _ in range(fold)] for _ in range(count)]
    for i in range(fold):
        orow, ocol = col // fold, row * fold + i
        away = (orow != row) | (ocol != col)
        for p in range(count):
            src = fin.at[:, pl.ds((p * fold + i) * sh, sh)]
            for j in range(fold):
                this = lax.rem(col, fold) == j
                dst = ho.at[p, j, mine]
                w.start(h1[p][j], src, dst, {"row": orow, "col": ocol}, away & this)
                w.start(h2[p][j], src, dst, {"row": orow, "col": ocol, "dp": other}, this)

                @pl.when(~away & this)
                def _():
                    copy = pltpu.make_async_copy(src, dst, local.at[7])
                    copy.start()
                    copy.wait()

    for j in range(fold):
        srow, scol = col // fold, row * fold + j
        for p in range(count):

            @pl.when((srow != row) | (scol != col))
            def _():
                w.arrived(h1[p][j], ho.at[p, j, mine], {"row": srow, "col": scol})

            w.arrived(h2[p][j], ho.at[p, j, theirs], {"row": srow, "col": scol, "dp": other})
    for d in range(1, ncol):
        came = pl.ds(pl.multiple_of(from_col[d] * tokens, 128), tokens)
        w.arrived(c_[d], go.at[:, came], {"col": from_col[d]})
        w.arrived(hc[d], gho.at[from_col[d]], {"col": from_col[d]})
    for d in range(1, nrow):
        w.arrived(s4[d], smo.at[lax.rem(row - d + nrow, nrow)], {"row": lax.rem(row - d + nrow, nrow)})
    pltpu.make_async_copy(sc.at[0], go.at[:, place], local.at[5]).wait()
    pltpu.make_async_copy(hsc.at[col], gho.at[col], local.at[10]).wait()
    pltpu.make_async_copy(smb.at[last], smo.at[row], local.at[6]).wait()
    w.finish()


def leave(nrow, ncol, ndp, fold, gin, ginh, gw, gs, sm):
    unit = gin.shape[2:]
    hs, wide = gw.shape[2:]
    sh = wide // 2 // fold
    part = gs.shape[1] // ncol
    nb, nd = len(bits(ndp)), len(bits(ndp)) + len(bits(ncol))
    slots = 8 * ncol + 2 * nrow + nd + 2 * nb + 6 * fold + 12
    edge = ginh.shape[1:]
    return pl.pallas_call(
        functools.partial(leave_kernel, nrow, ncol, ndp, fold),
        out_shape=[
            jax.ShapeDtypeStruct((unit[0], ncol * unit[1]), BF16),
            jax.ShapeDtypeStruct(edge, BF16),
            jax.ShapeDtypeStruct((2, fold, 2 * hs, sh), BF16),
            jax.ShapeDtypeStruct((part, gs.shape[2]), F32),
            jax.ShapeDtypeStruct((nrow,) + sm.shape, F32),
        ],
        in_specs=[ANYWHERE] * 5,
        out_specs=[ANYWHERE, ANYWHERE, ANYWHERE, ONCHIP, ANYWHERE],
        scratch_shapes=[
            pltpu.VMEM((2, ncol) + unit, BF16),
            pltpu.VMEM((2, ncol) + unit, BF16),
            pltpu.VMEM((ncol,) + unit, BF16),
            pltpu.VMEM((ncol,) + unit, BF16),
            pltpu.VMEM((ncol,) + unit, BF16),
            pltpu.VMEM((2,) + edge, BF16),
            pltpu.VMEM((2,) + edge, BF16),
            pltpu.VMEM(edge, BF16),
            pltpu.VMEM(edge, BF16),
            pltpu.VMEM(edge, BF16),
            pltpu.VMEM((ncol, hs, wide), BF16),
            pltpu.VMEM((ncol, hs, wide), BF16),
            pltpu.VMEM((ncol, hs, wide), BF16),
            pltpu.VMEM((ncol, hs, wide), BF16),
            pltpu.VMEM((hs, wide), BF16),
            pltpu.VMEM((max(2 * nb - 2, 1), hs if ndp > 2 else 8, wide), F32),
            pltpu.VMEM(gs.shape[1:], BF16),
            pltpu.VMEM((nrow,) + gs.shape[1:], BF16),
            pltpu.VMEM(gs.shape[1:], BF16),
            pltpu.VMEM((ncol, part, gs.shape[2]), BF16),
            pltpu.VMEM((2 * nb + 1, part, gs.shape[2]), F32),
            pltpu.VMEM((nd + 1,) + sm.shape, F32),
            pltpu.VMEM((nd,) + sm.shape, F32),
            pltpu.SemaphoreType.DMA((9 * ncol + 20 + nd + 2 * nb + 6 * fold * fold,)),
            pltpu.SemaphoreType.DMA((slots,)),
            pltpu.SemaphoreType.DMA((11,)),
        ],
        compiler_params=pltpu.CompilerParams(
            collective_id=2, has_side_effects=True, vmem_limit_bytes=60 * 1024 * 1024
        ),
        name="leave",
    )(gin, ginh, gw, gs, sm)


def finish_kernel(x_ref, c_ref, r_ref, g_ref, h_ref, res_ref, gin_ref):
    step, steps = pl.program_id(0), pl.num_programs(0)
    tokens = x_ref.shape[1]
    res_ref[...] = x_ref[...].astype(F32) + r_ref[...].astype(F32)
    gin_ref[...] = c_ref[...].astype(F32) + g_ref[...].astype(F32)
    at = slice(tokens - 128, tokens)

    @pl.when(step < steps - 1)
    def _():
        gin_ref[:, at] += h_ref[0].astype(F32)


def adam_kernel(*refs):
    for i in range(len(refs) // 8):
        grad_ref, moment_ref, square_ref, weight_ref = refs[4 * i : 4 * i + 4]
        outs = refs[len(refs) // 2 + 4 * i : len(refs) // 2 + 4 * i + 4]
        grad = grad_ref[...].astype(F32)
        outs[0][...] = grad
        for out, value in zip(
            outs[1:], adamw_step(grad, moment_ref[...], square_ref[...], weight_ref[...].astype(F32))
        ):
            out[...] = value


def adam(sets, steps):
    ins, outs = [], []
    for arrays in sets:
        shape = arrays[1].shape
        block = (shape[0] // steps,) + shape[1:]
        ins += [(array, block, 0) for array in arrays]
        outs += [(shape, F32, block, 0)] * 4
    return call(adam_kernel, steps, ins, outs, [], False, "adam", 5)


def call(kernel, steps, ins, outs, scratch, reverse, name, cost, ident=None):
    def spec(block, axis, base=None):
        def index(step):
            at = steps - 1 - step if reverse else step
            return tuple(
                at if a == axis else (base[a] if base else 0) for a in range(len(block))
            )

        return pl.BlockSpec(block, index) if block is not None else ANYWHERE

    return pl.pallas_call(
        kernel,
        grid=(steps,),
        in_specs=[spec(*item[1:]) for item in ins],
        out_specs=[spec(block, axis) for _, _, block, axis in outs],
        out_shape=[jax.ShapeDtypeStruct(shape, dtype) for shape, dtype, _, _ in outs],
        scratch_shapes=scratch,
        compiler_params=pltpu.CompilerParams(
            dimension_semantics=("arbitrary",),
            vmem_limit_bytes=60 * 1024 * 1024,
            collective_id=ident,
            has_side_effects=ident is not None,
        ),
        cost_estimate=pl.CostEstimate(
            flops=int(cost * 1e9), bytes_accessed=int(cost * 1e6), transcendentals=0
        ),
        name=name,
    )(*[item[0] for item in ins])


def whole(array):
    return (array, array.shape, None)


def raw(array):
    return (array, None, None)


def part(array, block, base):
    return (array, block, None, base)


def lanes(array):
    return (array, array.shape[:-1] + (GROUP,), array.ndim - 1)


def sublanes(array, rows=GROUP):
    return (array, array.shape[:-2] + (rows,) + array.shape[-1:], array.ndim - 2)


def each(array):
    return (array, (1,) + array.shape[1:], 0)


def out_whole(shape, dtype):
    return (shape, dtype, shape, None)


def out_sub(shape, dtype, rows=GROUP):
    return (shape, dtype, shape[:-2] + (rows,) + shape[-1:], len(shape) - 2)


def out_lanes(shape, dtype):
    return (shape, dtype, shape[:-1] + (GROUP,), len(shape) - 1)


def out_each(shape, dtype):
    return (shape, dtype, (1,) + shape[1:], 0)


def adamw_step(grad, moment, square, weight):
    first_new = BETA_FIRST * moment + (1.0 - BETA_FIRST) * grad
    second_new = BETA_SECOND * square + (1.0 - BETA_SECOND) * grad * grad
    fix_first = 1.0 - BETA_FIRST**STEP
    fix_second = 1.0 - BETA_SECOND**STEP
    delta = -LEARN_RATE * (
        first_new / fix_first / (jnp.sqrt(second_new / fix_second) + ADAM_EPSILON)
        + WEIGHT_DECAY * weight
    )
    return (first_new, second_new, delta)


def local(
    inputs, segments, cotangent, pregain, innerweight, rateweight, stateweight, innerconv, stateconv, headparams,
    postgain, outweight, *moments,
):
    nrow, ncol, ndp = (lax.axis_size(a) for a in ("row", "col", "dp"))
    row, col = lax.axis_index("row"), lax.axis_index("col")
    length, own = inputs.shape[1], inputs.shape[2]
    width = own * nrow * ncol
    stored = innerweight.shape[1]
    total_heads = stored * ncol
    heads = total_heads // nrow
    hl = heads * HEADP
    count = total_heads * HEADP
    tokens = length // ncol
    steps = tokens // GROUP
    depth = width // nrow
    fold = ncol // nrow
    hops = (MOST - 2) // tokens + 1

    window = jnp.pad(segments[0], (HALO, HALO), constant_values=-1)
    window = lax.dynamic_slice_in_dim(window, col * tokens, tokens + 2 * HALO, 0)
    mine = window[HALO : HALO + tokens]
    flags = [mine]
    for j in (-1, -2, -3, 1, 2, 3):
        flags.append(window[HALO + j : HALO + j + tokens] == mine)
    before = window[HALO - 1 : HALO - 1 + tokens : GROUP]
    flags.append((mine.reshape(steps, GROUP) == before[:, None]).reshape(tokens))
    tok = jnp.stack([f.astype(F32) for f in flags])
    hmask = jnp.stack([(window[j : j + HALO] == window[:HALO]).astype(F32) for j in range(8)], 1)
    hmask = jnp.pad(hmask, ((0, 0), (0, 120)))

    block_heads = headparams.shape[1]
    xs, cs = inputs[0].T, cotangent[0].T
    smalls = [pregain, innerconv, headparams, postgain, rateweight, stateweight]
    flat = jnp.concatenate([a.reshape(-1) for a in smalls])
    ss = jnp.pad(flat, (0, -flat.size % 2048)).reshape(-1, 128)
    sub = depth // fold
    sh = stored * HEADP
    split = innerweight.reshape(depth, stored, 2, HEADP)
    ws = jnp.concatenate(
        [
            split[:, :, 0].reshape(depth, sh),
            split[:, :, 1].reshape(depth, sh),
            outweight.reshape(sh, depth).T,
        ],
        1,
    ).reshape(fold, sub, 3 * sh)

    x, xh, cot, weights, gathered = enter(nrow, ncol, ndp, fold, xs, cs, ws, ss)

    if fold > 1:
        weights = weights.reshape(ncol, fold, sub, 3, sh).transpose(0, 2, 3, 1, 4)
    weights = weights.reshape(width, 3 * hl)
    x, xh, cot = (a.reshape(width, a.shape[3]) for a in (x, xh, cot))
    gathered = gathered.reshape(nrow, ncol, -1)
    parts, at = [], 0
    for array in smalls:
        parts.append(gathered[:, :, at : at + array.size])
        at += array.size
    gain = jnp.broadcast_to(parts[0].reshape(width, 1).astype(F32), (width, 128))
    iconv = parts[1].reshape(nrow, ncol, 5, block_heads, HEADP).transpose(2, 1, 0, 3, 4)
    iconv = lax.dynamic_slice_in_dim(iconv.reshape(5, count), row * hl, hl, 1).astype(F32)
    hp = parts[2].reshape(nrow, ncol, 3, block_heads).transpose(2, 1, 0, 3)
    hp = lax.dynamic_slice_in_dim(hp.reshape(3, total_heads), row * heads, heads, 1).astype(F32)
    post = parts[3].reshape(nrow, ncol, block_heads * HEADP).transpose(1, 0, 2)
    post = lax.dynamic_slice_in_dim(post.reshape(1, count), row * hl, hl, 1).astype(F32)
    wrate = parts[4].reshape(nrow, ncol, depth, stored)
    wrate = wrate.transpose(1, 3, 0, 2).reshape(total_heads, width)
    wrate = lax.dynamic_slice_in_dim(wrate, row * heads, heads, 0)
    wrate = jnp.pad(wrate, ((0, 16 - heads), (0, 0)))
    wstate = parts[5].reshape(width, 2 * NSTATE)
    sconv = stateconv.astype(F32)
    head = jnp.broadcast_to(
        jnp.concatenate([-jnp.exp(hp[0]), hp[1]])[:, None], (2 * heads, 128)
    )
    skip = jnp.repeat(hp[2], HEADP)[None]

    spread = jnp.repeat(jnp.eye(heads, dtype=BF16), HEADP, 1)
    spread = jnp.concatenate([spread, spread], 0)
    triangle = jnp.triu(jnp.ones((GROUP, GROUP), BF16))
    ns2 = 2 * NSTATE
    x_in, xh_in, cot_in = lanes(x), whole(xh), lanes(cot)
    wmain = part(weights, (width, 2 * hl), (0, 0))
    woutt = part(weights, (width, hl), (0, 2))

    gate, pre, st, uv, us, bc, rows, states, prod, fin, total, preh, sth, rinvh = call(
        fwd1_kernel,
        steps,
        [x_in, xh_in, whole(gain), wmain, whole(wstate), whole(wrate), lanes(tok), whole(head),
         whole(iconv), whole(sconv), whole(triangle), whole(spread)],
        [out_sub((tokens, hl), F32), out_sub((tokens, hl), F32), out_sub((tokens, ns2), BF16),
         out_sub((tokens, hl), F32), out_sub((tokens, ns2), F32), out_sub((tokens, ns2), BF16),
         out_lanes((4 * heads, tokens), F32),
         out_each((steps, NSTATE, hl), BF16), out_each((steps, 8, hl), F32),
         out_whole((NSTATE, hl), F32), out_whole((8, hl), F32), out_whole((HALO, hl), BF16),
         out_whole((HALO, ns2), BF16), out_whole((HALO, 128), F32)],
        [pltpu.VMEM((GROUP + 8, hl + ns2), F32), pltpu.VMEM((NSTATE, hl), F32), pltpu.VMEM((8, hl), F32)],
        False,
        "fwd1",
        22,
    )
    total = total[0:1]
    sin = shift(ncol, 1, fin.astype(BF16), 3).astype(F32)
    for _ in range(hops - 1):
        sin = shift(ncol, 1, (fin + total * sin).astype(BF16), 3).astype(F32)

    scan, out, dn, stat = call(
        fwd2_kernel,
        steps,
        [sublanes(gate), sublanes(uv), sublanes(bc), lanes(rows), lanes(tok), each(states), each(prod), whole(sin),
         cot_in, whole(post), whole(skip), woutt, whole(spread)],
        [out_sub((tokens, hl), F32), out_lanes((nrow, depth, tokens), BF16), out_sub((tokens, hl), BF16),
         out_lanes((8, tokens), F32)],
        [],
        False,
        "fwd2",
        18,
    )
    scal = gather_stat(nrow, count, stat)

    dy, dg, leaving, prodb, first, gout, sums, root = call(
        bwd1_kernel,
        steps,
        [sublanes(gate), sublanes(uv), sublanes(bc), lanes(rows), lanes(tok), sublanes(scan), sublanes(dn),
         lanes(scal), cot_in, whole(post), whole(skip), whole(spread)],
        [out_sub((tokens, hl), BF16), out_sub((tokens, hl), BF16), out_each((steps, NSTATE, hl), BF16),
         out_each((steps, 8, hl), F32), out_whole((NSTATE, hl), F32), out_whole((width, hl), BF16),
         out_whole((16, hl), F32), out_lanes((8, tokens), F32)],
        [pltpu.VMEM((NSTATE, hl), F32), pltpu.VMEM((8, hl), F32), pltpu.VMEM((width, hl), F32)],
        True,
        "bwd1",
        15,
    )
    din = shift(ncol, -1, first.astype(BF16), 4).astype(F32)
    for _ in range(hops - 1):
        din = shift(ncol, -1, (first + total * din).astype(BF16), 4).astype(F32)

    hs = sub // 2
    home, ghout, gin, ginh, gw, gs, gr, gk, gh, gp = call(
        functools.partial(bwd2_kernel, (nrow, ncol, ndp, fold)),
        steps,
        [x_in, xh_in, whole(gain), wmain, whole(wstate), whole(wrate), lanes(tok), whole(head),
         whole(hmask), whole(rinvh), whole(iconv), whole(sconv), whole(triangle), whole(spread), whole(skip),
         sublanes(pre), sublanes(st), whole(preh), whole(sth), sublanes(uv), sublanes(us), sublanes(bc), lanes(rows),
         each(states), each(prod), whole(sin), sublanes(scan), sublanes(dy), sublanes(dg),
         each(leaving), each(prodb), whole(din), lanes(root), whole(scal),
         raw(out.reshape(nrow, ncol, own, tokens)), raw(gout.reshape(ncol, 2, hs, hl))],
        [((own, length), BF16, None, None), ((fold, sub, sh), BF16, None, None),
         out_lanes((nrow, depth, tokens), BF16), out_whole((nrow, depth, 128), BF16), out_whole((width, 2 * hl), BF16),
         out_whole((width, ns2), BF16), out_whole((16, width), F32), out_whole((40, hl + ns2), F32),
         out_whole((2 * heads, GROUP), F32), out_whole((width, 128), F32)],
        [pltpu.VMEM((GROUP + 8, hl + ns2), F32), pltpu.VMEM((width, 2 * hl + ns2), F32)]
        + delivery_scratch(nrow, ncol, ndp, fold, own, tokens, hs, hl),
        True,
        "bwd2",
        50,
        5,
    )

    gk = jnp.sum(gk.reshape(5, 8, -1), 1)
    gh = jnp.sum(gh, 1).reshape(2, heads)
    sums = jnp.sum(sums.reshape(2, 8, hl), 1)
    gskip = jnp.sum(sums[1].reshape(1, heads, HEADP), 2)
    small = [
        jnp.sum(gp, 1),
        gr[:heads],
        gk[:, :hl],
        gk[:, hl:],
        jnp.concatenate([gh, gskip]),
        sums[0],
    ]
    flat = jnp.concatenate([a.reshape(-1) for a in small])
    flat = jnp.pad(flat, (0, -flat.size % 1024)).reshape(-1, 128)
    gin, edge, ghome, gstate, flat = leave(
        nrow, ncol, ndp, fold,
        gin.reshape(nrow, ncol, own, tokens), ginh.reshape(nrow, ncol, own, 128),
        gw.reshape(ncol, 2, hs, 2 * hl), gs.reshape(nrow, depth, ns2), flat,
    )
    edge = jnp.concatenate([edge[1:], edge[:1]], 0)
    result, grad_input = call(
        finish_kernel,
        ncol,
        [(a, (own, tokens), 1) for a in (xs, cs, home, gin)] + [each(edge)],
        [((own, length), F32, (own, tokens), 1)] * 2,
        [],
        False,
        "finish",
        5,
    )
    result, grad_input = result.T[None], grad_input.T[None]

    ghome = ghome.reshape(2, depth, stored, HEADP)
    ginner = jnp.concatenate([ghome[0], ghome[1]], 2)
    gout = ghout.reshape(depth, sh).T.reshape(stored, HEADP, depth)
    updated = adam(
        [(ginner, moments[2], moments[3], innerweight), (gout, moments[16], moments[17], outweight)], 4
    )
    flat = flat.reshape(nrow, -1)
    parts, at = [], 0
    for array in small:
        parts.append(flat[:, at : at + array.size].reshape((nrow,) + array.shape))
        at += array.size
    feature = (row * ncol + col) * own
    block = col * nrow + row
    gpre = lax.dynamic_slice_in_dim(jnp.sum(parts[0], 0).reshape(-1), feature, own, 0)
    grate = lax.dynamic_slice(
        parts[1], (col // fold, (col % fold) * stored, row * depth), (1, stored, depth)
    )[0].T
    giconv = parts[2].transpose(1, 0, 2).reshape(5, count)
    wide = block_heads * HEADP
    giconv = lax.dynamic_slice_in_dim(giconv, block * wide, wide, 1)
    giconv = giconv.reshape(5, block_heads, HEADP)
    gsconv = jnp.sum(parts[3], 0)
    ghead = parts[4].transpose(1, 0, 2).reshape(3, total_heads)
    ghead = lax.dynamic_slice_in_dim(ghead, block * block_heads, block_heads, 1)
    gpost = lax.dynamic_slice_in_dim(parts[5].reshape(count), block * wide, wide, 0)
    gpost = gpost.reshape(block_heads, HEADP)

    grads = (gpre, None, grate, gstate, giconv, gsconv, ghead, gpost, None)
    params = (
        pregain, innerweight, rateweight, stateweight, innerconv, stateconv, headparams, postgain, outweight,
    )
    ready = {1: updated[:4], 8: updated[4:]}
    outputs = [result, grad_input]
    for i, (grad, param) in enumerate(zip(grads, params)):
        if i in ready:
            outputs.extend(ready[i])
            continue
        outputs.append(grad)
        outputs.extend(adamw_step(grad, moments[2 * i], moments[2 * i + 1], param.astype(F32)))
    return tuple(outputs)


def solution(mesh):
    tokens = P("dp", None, ("row", "col"))
    weights = (
        P(("row", "col")),
        P("row", "col", None),
        P("row", "col"),
        P(("row", "col"), None),
        P(None, ("col", "row"), None),
        P(),
        P(None, ("col", "row")),
        P(("col", "row"), None),
        P("col", None, "row"),
    )
    return jax.shard_map(
        local,
        mesh=mesh,
        in_specs=(tokens, P("dp", None), tokens)
        + weights
        + tuple(w for w in weights for _ in range(2)),
        out_specs=(tokens, tokens) + tuple(w for w in weights for _ in range(4)),
        check_vma=False,
    )
```

time: 806 us -> 427 us (0.53)
  waiting for transfers between devices: 359 us -> 0 us
  Pallas kernels: 107 us -> 379 us
  blocking collectives: 187 us -> 0 us
  local copies, waits for them, and re-layouts: 80.7 us -> 24.1 us
  starting transfers between devices: 23.5 us -> 0 us
  between operations: 14.7 us -> 1.36 us
  other arithmetic: 30 us -> 21.6 us
    pallas_call x4 -> x11, Pallas kernels: 107 us -> 379 us  [the longest x6 137 us: call(): pl.pallas_call(kernel, grid=(steps,), in_specs=[spec(*item[1:]) for item...]
    reduce_scatter x5 -> x0, waiting for transfers between devices: 169 us -> none  [the longest x2 74.4 us: home(): lax.psum_scatter(grad.astype(BF16), 'col', scatter_dimension=0, tiled=True)]
    psum x1 -> x0, waiting for transfers between devices: 106 us -> none  [local(): lax.psum(jnp.pad(flat, (0, pad)).reshape(-1, 128), ('dp', 'row', 'col'))]
    all_to_all x2 -> x0, blocking collectives: 96.4 us -> none  [the longest x1 55.1 us: local(): lax.all_to_all(pieces, 'col', 0, 0).transpose(1, 0, 2)]
    ppermute x5 -> x0, waiting for transfers between devices: 66.3 us -> none  [the longest x1 36 us: local(): came.append(lax.ppermute(piece, ('row', 'col'), perm))]
    psum x2 -> x0, blocking collectives: 52 us -> none  [the longest x1 41.9 us: home(): grad = lax.psum(grad.astype(F32), 'dp').astype(BF16)]
    all_gather x1 -> x0, blocking collectives: 38.8 us -> none  [local(): lax.all_gather(packed, ('row', 'col'), axis=0).reshape(nrow, ncol, -1)]
    slice x24 -> x16, local copies, waits for them, and re-layouts: 24.8 us -> 2.16 us  [the longest x3 1.33 us: local(): ginner = jnp.concatenate([ghome[0], ghome[1]], 2)]
  transfers between devices with their start and end apart: 16 -> 0, of which waited for: 10 -> 0; matrix products, arithmetic and copies ran while one was open for 11% -> 0% of each run, Pallas kernels for 3% -> 0%
where the time goes in v2:
time: 427 us; the launch traced here: 426 us
  Pallas kernels  379 us (89%)
  local copies, waits for them, and re-layouts  24.1 us (6%)
  other arithmetic  21.6 us (5%)
    pallas_call x6, Pallas kernels, call(): pl.pallas_call(kernel, grid=(steps,), in_specs=[spec(*item[1:]) for item...  137 us
    pallas_call x1, Pallas kernels, leave(): pl.pallas_call(functools.partial(leave_kernel, nrow, ncol, ndp, fold), ou...  110 us
    pallas_call x1, Pallas kernels, enter(): pl.pallas_call(functools.partial(enter_kernel, nrow, ncol, ndp, fold), ou...  109 us
    pallas_call x2, Pallas kernels, shift(): pl.pallas_call(functools.partial(shift_kernel, ncol, by), out_shape=jax.S...  15.8 us

profile of v2, /device:TPU:6, one launch (start us, length us, event | category | flops | bytes accessed | tf_op | source)
XLA Modules:
  0.0 425.7 jit_solution(12409594530653654390)
XLA Ops:
  1.7 1.6 compare_convert_fusion
  4.9 1.3 copy.122
  9.1 109.1 %enter.1 = (bf16[4,4,64,2048]{3,2,1,0:T(8,128)(2,1)}, bf16[4,4,64,128]{3,2,1,0:T(8,128)(2,1)}, bf16[4,4,64,2048]{3,2,1,0:T(8,128)(2,1)}, bf16[4,1,256,1536]{3,2,1,0:T(8,128)(2,1)}, bf16[4,4,160,128]{3,2,1,0:T(8,128)(2,1)}) custom-call(bf16[64,8192]{1,0:T(8,128)(2,1)} %bitcast.123, bf16[64,8192]{1,0:T(8,128)(2,1)} %bitcast.125, ...), custom_call_target="tpu_custom_call" | custom-call | tf_op jit(solution)/shard_map/enter/pallas_call | solution.py:902
  118.2 1.7 reshape.258
  121.4 1.2 reshape.261
  124.8 1.2 reshape.260.wstate_ref
  126.1 1.0 broadcast_in_dim.33.gain_ref
  128.6 23.2 %fwd1.1 = (f32[2048,512]{1,0:T(8,128)}, f32[2048,512]{1,0:T(8,128)}, bf16[2048,256]{1,0:T(8,128)(2,1)}, f32[2048,512]{1,0:T(8,128)}, f32[2048,256]{1,0:T(8,128)}...) custom-call(bf16[1024,2048]{1,0:T(8,128)(2,1)} %bitcast.166, ...), custom_call_target="tpu_custom_call" | custom-call | flops 22000001024 | bytes 22000000 | tf_op jit(solution)/shard_map/fwd1/pallas_call | solution.py:1313
  151.8 1.6 convert_element_type.94.src
  153.5 7.4 %shift3.1 = bf16[128,512]{1,0:T(8,128)(2,1)} custom-call(bf16[128,512]{1,0:T(8,128)(2,1)} %convert_element_type.94.src), custom_call_target="tpu_custom_call" | custom-call | tf_op jit(solution)/shard_map/shift3/pallas_call | solution.py:966
  160.8 1.6 convert_element_type.95.sin_ref
  163.9 17.9 %fwd2.1 = (f32[2048,512]{1,0:T(8,128)}, bf16[4,256,2048]{2,1,0:T(8,128)(2,1)}, bf16[2048,512]{1,0:T(8,128)(2,1)}, f32[8,2048]{1,0:T(8,128)}) custom-call(f32[2048,512]{1,0:T(8,128)} %get-tuple-element.109.gate_ref, f32[2048,512]{1,0:T(8,128)} %get-tuple-element.102.uv_ref, bf16[2048,256]{1,0:T(8,128)(2,1)} %get-tuple-element.104.bc_ref, ...), custom_call_target="tpu_custom_call" | custom-call | flops 17999998976 | bytes 18000000 | tf_op jit(solution)/shard_map/fwd2/pallas_call | solution.py:1313
  181.8 6.6 %stat.1.scal_ref = f32[8,2048]{1,0:T(8,128)} custom-call(f32[8,2048]{1,0:T(8,128)} %get-tuple-element.113.stat), custom_call_target="tpu_custom_call" | custom-call | tf_op jit(solution)/shard_map/stat/pallas_call | solution.py:1003
  188.4 15.9 %bwd1.1 = (bf16[2048,512]{1,0:T(8,128)(2,1)}, bf16[2048,512]{1,0:T(8,128)(2,1)}, bf16[8,128,512]{2,1,0:T(8,128)(2,1)}, f32[8,8,512]{2,1,0:T(8,128)}, f32[128,512...) custom-call(f32[2048,512]{1,0:T(8,128)} %get-tuple-element.109.gate_ref, ...), custom_call_target="tpu_custom_call" | custom-call | flops 15000000512 | bytes 15000000 | tf_op jit(solution)/shard_map/bwd1/pallas_call | solution.py:1313
  204.3 1.6 convert_element_type.97.src
  206.0 8.4 %shift4.1 = bf16[128,512]{1,0:T(8,128)(2,1)} custom-call(bf16[128,512]{1,0:T(8,128)(2,1)} %convert_element_type.97.src), custom_call_target="tpu_custom_call" | custom-call | tf_op jit(solution)/shard_map/shift4/pallas_call | solution.py:966
  214.4 1.6 convert_element_type.98.din_ref
  217.5 69.4 %bwd2.1 = (bf16[64,8192]{1,0:T(8,128)(2,1)}, bf16[1,256,512]{2,1,0:T(8,128)(2,1)}, bf16[4,256,2048]{2,1,0:T(8,128)(2,1)}, bf16[4,256,128]{2,1,0:T(8,128)(2,1)}, ...) custom-call(bf16[1024,2048]{1,0:T(8,128)(2,1)} %bitcast.167, ...), custom_call_target="tpu_custom_call" | custom-call | flops 49999998976 | bytes 50000000 | tf_op jit(solution)/shard_map/bwd2/pallas_call | solution.py:1313
  289.9 1.2 reduce_sum.67
  291.9 110.1 %leave.1 = (bf16[64,8192]{1,0:T(8,128)(2,1)}, bf16[4,64,128]{2,1,0:T(8,128)(2,1)}, bf16[2,1,256,512]{3,2,1,0:T(8,128)(2,1)}, f32[64,256]{1,0:T(8,128)}, f32[4,112,128]{2,1,0:T(8,128)}) custom-call(bf16[4,4,64,2048]{3,2,1,0:T(8,128)(2,1)} %bitcast.114, bf16[4,4,64,128]{3,2,1,0:T(8,128)(2,1)} %bitcast.140, bf16[4,2,128,1024]{3,2,1,0:T(8,128)(2,1)} %bitcast.117, ...), custom_call_target="tpu_custom_call" | custom-call | tf_op jit(solution)/shard_map/leave/pallas_call | solution.py:1223
  402.0 1.1 fusion.37
  404.0 1.1 pad_maximum_fusion.refs_0_
  405.9 5.9 %adam.1 = (f32[256,8,128]{2,1,0:T(8,128)}, f32[256,8,128]{2,1,0:T(8,128)}, f32[256,8,128]{2,1,0:T(8,128)}, f32[256,8,128]{2,1,0:T(8,128)}, f32[8,64,256]{2,1,0:T...) custom-call(bf16[256,8,128]{2,1,0:T(8,128)(2,1)} %pad_maximum_fusion.refs_0_, ...), custom_call_target="tpu_custom_call" | custom-call | flops 5000000000 | bytes 5000000 | tf_op jit(solution)/shard_map/adam/pallas_call | solution.py:1313
  412.6 4.9 %finish.1 = (f32[64,8192]{1,0:T(8,128)}, f32[64,8192]{1,0:T(8,128)}) custom-call(bf16[64,8192]{1,0:T(8,128)(2,1)} %bitcast.124, bf16[64,8192]{1,0:T(8,128)(2,1)} %bitcast.126, bf16[64,8192]{1,0:T(8,128)(2,1)} %get-tuple-element.122.r_ref, bf16[64,8192]{1,0:T(8,128)(2,1)} %get-tuple-element.132.g_ref, bf16[4,64,128]{2,1,0:T(8,128)(2,1)} %pad_maximum_fusion.1.h_ref), custom_call_target="tpu_custom_call" | custom-call | flops 5000000000 | bytes 5000000 | tf_op jit(solution)/shard_map/finish/pallas_call | solution.py:1313
  (187 shorter events, 27.7 us)
Async XLA Ops:
  0.7 5.9 %copy-start.1 = (bf16[8,64,256]{2,1,0:T(8,128)(2,1)S(1)}, bf16[8,64,256]{2,1,0:T(8,128)(2,1)}, u32[]{:S(2)}) copy-start(bf16[8,64,256]{2,1,0:T(8,128)(2,1)} %refs_7_.1) | copy-start | bytes 786436
  122.6 5.5 %copy-start.12 = (bf16[5,256]{1,0:T(8,128)(2,1)S(1)}, bf16[5,256]{1,0:T(8,128)(2,1)}, u32[]{:S(2)}) copy-start(bf16[5,256]{1,0:T(8,128)(2,1)} %param.38) | copy-start | bytes 7684
  188.4 27.6 %copy-start = (s32[1,8192]{1,0:T(1,128)S(1)}, s32[1,8192]{1,0:T(1,128)}, u32[]{:S(2)}) copy-start(s32[1,8192]{1,0:T(1,128)} %param.31) | copy-start | bytes 98308
  217.5 70.3 %copy-start.9 = (f32[16,512]{1,0:T(8,128)S(1)}, f32[16,512]{1,0:T(8,128)}, u32[]{:S(2)}) copy-start(f32[16,512]{1,0:T(8,128)} %get-tuple-element.131) | copy-start | bytes 98308
  405.9 5.9 %copy-start.6 = (bf16[4,64,128]{2,1,0:T(8,128)(2,1)S(1)}, bf16[4,64,128]{2,1,0:T(8,128)(2,1)}, u32[]{:S(2)}) copy-start(bf16[4,64,128]{2,1,0:T(8,128)(2,1)} %get-tuple-element.133) | copy-start | bytes 196612
  412.5 5.1 %copy-start.4 = (f32[4,112,128]{2,1,0:T(8,128)S(1)}, f32[4,112,128]{2,1,0:T(8,128)}, u32[]{:S(2)}) copy-start(f32[4,112,128]{2,1,0:T(8,128)} %get-tuple-element.136) | copy-start | bytes 688132
  412.5 5.3 %copy-start.15 = (f32[256,8]{0,1:T(8,128)S(1)}, f32[256,8]{0,1:T(8,128)}, u32[]{:S(2)}) copy-start(f32[256,8]{0,1:T(8,128)} %param.47) | copy-start | bytes 24580
  412.5 5.3 %copy-start.16 = (f32[256,8]{0,1:T(8,128)S(1)}, f32[256,8]{0,1:T(8,128)}, u32[]{:S(2)}) copy-start(f32[256,8]{0,1:T(8,128)} %param.46) | copy-start | bytes 24580
  412.5 6.1 %copy-start.19 = (f32[5,2,64]{2,1,0:T(2,128)S(1)}, f32[5,2,64]{2,1,0:T(2,128)}, u32[]{:S(2)}) copy-start(f32[5,2,64]{2,1,0:T(2,128)} %param.51) | copy-start | bytes 7684
  412.5 6.1 %copy-start.20 = (f32[5,2,64]{2,1,0:T(2,128)S(1)}, f32[5,2,64]{2,1,0:T(2,128)}, u32[]{:S(2)}) copy-start(f32[5,2,64]{2,1,0:T(2,128)} %param.50) | copy-start | bytes 7684
  412.5 6.9 %copy-start.23 = (f32[3,2]{0,1:T(2,128)S(1)}, f32[3,2]{0,1:T(2,128)}, u32[]{:S(2)}) copy-start(f32[3,2]{0,1:T(2,128)} %param.54) | copy-start | bytes 76
  412.5 6.9 %copy-start.24 = (f32[3,2]{0,1:T(2,128)S(1)}, f32[3,2]{0,1:T(2,128)}, u32[]{:S(2)}) copy-start(f32[3,2]{0,1:T(2,128)} %param.55) | copy-start | bytes 76
  412.5 9.8 %copy-start.17 = (f32[5,256]{1,0:T(8,128)S(1)}, f32[5,256]{1,0:T(8,128)}, u32[]{:S(2)}) copy-start(f32[5,256]{1,0:T(8,128)} %param.53) | copy-start | bytes 15364
  412.5 9.7 %copy-start.18 = (f32[5,256]{1,0:T(8,128)S(1)}, f32[5,256]{1,0:T(8,128)}, u32[]{:S(2)}) copy-start(f32[5,256]{1,0:T(8,128)} %param.52) | copy-start | bytes 15364
  412.5 10.6 %copy-start.25 = (f32[2,64]{1,0:T(2,128)S(1)}, f32[2,64]{1,0:T(2,128)}, u32[]{:S(2)}) copy-start(f32[2,64]{1,0:T(2,128)} %param.57) | copy-start | bytes 1540
  412.5 10.6 %copy-start.26 = (f32[2,64]{1,0:T(2,128)S(1)}, f32[2,64]{1,0:T(2,128)}, u32[]{:S(2)}) copy-start(f32[2,64]{1,0:T(2,128)} %param.56) | copy-start | bytes 1540
  412.6 11.2 %copy-start.28 = (f32[64]{0:T(128)S(1)}, f32[64]{0:T(128)}, u32[]{:S(2)}) copy-start(f32[64]{0:T(128)} %param.43) | copy-start | bytes 772
  412.6 11.2 %copy-start.29 = (f32[64]{0:T(128)S(1)}, f32[64]{0:T(128)}, u32[]{:S(2)}) copy-start(f32[64]{0:T(128)} %param.42) | copy-start | bytes 772
  412.6 11.8 %copy-start.3 = (f32[64,256]{1,0:T(8,128)S(1)}, f32[64,256]{1,0:T(8,128)}, u32[]{:S(2)}) copy-start(f32[64,256]{1,0:T(8,128)} %get-tuple-element.362) | copy-start | bytes 196612
  412.6 11.8 %copy-start.7 = (f32[64,256]{1,0:T(8,128)S(1)}, f32[64,256]{1,0:T(8,128)}, u32[]{:S(2)}) copy-start(f32[64,256]{1,0:T(8,128)} %param.49) | copy-start | bytes 196612
  412.6 11.8 %copy-start.8 = (f32[64,256]{1,0:T(8,128)S(1)}, f32[64,256]{1,0:T(8,128)}, u32[]{:S(2)}) copy-start(f32[64,256]{1,0:T(8,128)} %param.48) | copy-start | bytes 196612
  418.5 7.2 %copy-start.11 = (f32[5,2,64]{2,1,0:T(2,128)}, f32[5,2,64]{2,1,0:T(2,128)S(1)}, u32[]{:S(2)}) copy-start(f32[5,2,64]{2,1,0:T(2,128)S(1)} %reshape.290) | copy-start | bytes 7684
  422.3 3.5 copy-start.10
  423.2 2.6 copy-start.27
  (8 other events, 14.7 us)

commit v3 on v2

--- a/solution.py
+++ b/solution.py
@@ -174,7 +174,7 @@
     prod_ref[0] = prod[...]
     state[...] = state[...] * carry[0:1] + mm_tn(bc[:, :NSTATE], scaled)
     prod[...] = prod[...] * carry
-    fin_ref[...] = state[...]
+    fin_ref[...] = state[...].astype(BF16)
     total_ref[...] = prod[...]
 
 
@@ -210,7 +210,7 @@
     u = uv_ref[...].astype(F32)
     values = u * sigmoid(u)
     scaled = (values * expand(rates, spread)).astype(BF16)
-    entering = (sent_ref[0].astype(F32) + prod_ref[0, 0:1] * sin_ref[...]).astype(BF16)
+    entering = (sent_ref[0].astype(F32) + prod_ref[0, 0:1] * sin_ref[...].astype(F32)).astype(BF16)
     outer = mm(cm, entering) * expand(enter, spread)
     first = pair_lanes((GROUP, 128))
     pieces = []
@@ -297,7 +297,7 @@
     prodb_ref[0] = prod[...]
     adj[...] = adj[...] * carry[0:1] + mm_tn(cm, weighted)
     prod[...] = prod[...] * carry
-    first_ref[...] = adj[...]
+    first_ref[...] = adj[...].astype(BF16)
 
 
 class Delivery:
@@ -414,6 +414,8 @@
 
             @pl.when(step == jnp.minimum(2 + i, last - 1))
             def _():
+                if i == 0:
+                    self.weights()
                 self.come("a0", d)
                 self.come("b", d)
                 total = self.own[0, self.cols[d]].astype(F32) + self.ra[0, d].astype(F32) + self.rb[d].astype(F32)
@@ -423,18 +425,22 @@
                 else:
                     self.stays.start()
 
-        @pl.when(step == jnp.minimum(3, last - 1))
+        @pl.when(step == jnp.minimum(6, last))
         def _():
-            for d in plan:
+            self.homeward()
+
+    def weights(self):
+        if True:
+            for d in self.plan:
                 self.come("y", d)
                 self.sy[d] = (self.gv[self.cols[d]].astype(F32) + self.ry[d].astype(F32)).astype(BF16)
                 if d:
                     self.go("z", d)
 
-        @pl.when(step == last)
-        def _():
+    def homeward(self):
+        if True:
             total = self.sy[0].astype(F32)
-            for d in range(1, ncol):
+            for d in range(1, self.dims[1]):
                 self.come("z", d)
                 total = total + self.rz[d].astype(F32)
             for i, hop in enumerate(self.hops):
@@ -529,8 +535,8 @@
     rexp = expand(rates, spread)
     scaled = (values * rexp).astype(BF16)
     dyb = dy_ref[...]
-    entering = (sent_ref[0].astype(F32) + prod_ref[0, 0:1] * sin_ref[...]).astype(BF16)
-    leaving = (leave_ref[0].astype(F32) + prodb_ref[0, 0:1] * din_ref[...]).astype(BF16)
+    entering = (sent_ref[0].astype(F32) + prod_ref[0, 0:1] * sin_ref[...].astype(F32)).astype(BF16)
+    leaving = (leave_ref[0].astype(F32) + prodb_ref[0, 0:1] * din_ref[...].astype(F32)).astype(BF16)
 
     first = pair_lanes((GROUP, 128))
     dscores = jnp.zeros((GROUP, GROUP), F32)
@@ -783,7 +789,7 @@
     pltpu.make_async_copy(mid, dst, sem).start()
 
 
-def enter_kernel(nrow, ncol, ndp, fold, xs, cs, ws, ss, xo, ho, co, wo, so, xv, hv, cv, wv, sv, send, recv, local):
+def enter_kernel(nrow, ncol, ndp, fold, xs, cs, ws, ss, ts, xo, ho, co, wo, so, to_, xv, hv, cv, wv, sv, tv, send, recv, local):
     row, col, dp = (lax.axis_index(a) for a in ("row", "col", "dp"))
     w = Wires(send, recv)
     greet(nrow, ncol, ndp)
@@ -798,6 +804,7 @@
 
     spreads = [
         Spread(w, ncol, lambda to: ss, so),
+        Spread(w, ncol, lambda to: ts, to_),
         Spread(w, ncol, lambda to: before(xs, to), ho),
         Spread(w, ncol, lambda to: tokens_of(xs, to), xo),
         Spread(w, ncol, lambda to: tokens_of(cs, to), co),
@@ -828,6 +835,7 @@
     for s in spreads:
         s.begin()
     moved(ss, sv, so.at[row, col], local.at[1])
+    moved(ts, tv, to_.at[row, col], local.at[5])
     moved(tokens_of(xs, col), xv, xo.at[row, col], local.at[2])
     moved(tokens_of(cs, col), cv, co.at[row, col], local.at[3])
     moved(before(xs, col), hv, ho.at[row, col], local.at[4])
@@ -847,7 +855,7 @@
     w.start(left[1], own, own, {"col": col + 1}, col + 1 < ncol)
     w.start(right[1], own, own, {"col": col - 1}, col >= 1)
     w.start(cross[0], own, own, {"dp": other})
-    steps = order(ncol)
+    steps = [0] + order(ncol)[:0:-1]
     for at in range(1, ncol):
         d = steps[at]
         for s in spreads:
@@ -886,6 +894,7 @@
     for s in spreads:
         s.end()
     pltpu.make_async_copy(sv, so.at[row, col], local.at[1]).wait()
+    pltpu.make_async_copy(tv, to_.at[row, col], local.at[5]).wait()
     pltpu.make_async_copy(xv, xo.at[row, col], local.at[2]).wait()
     pltpu.make_async_copy(cv, co.at[row, col], local.at[3]).wait()
     pltpu.make_async_copy(hv, ho.at[row, col], local.at[4]).wait()
@@ -896,9 +905,9 @@
 ONCHIP = pl.BlockSpec(memory_space=pltpu.VMEM)
 
 
-def enter(nrow, ncol, ndp, fold, xs, cs, ws, ss):
+def enter(nrow, ncol, ndp, fold, xs, cs, ws, ss, ts):
     own, tokens = xs.shape[0], xs.shape[1] // ncol
-    slots = 16 * ncol + fold + 4 * ncol
+    slots = 20 * ncol + fold + 4 * ncol
     return pl.pallas_call(
         functools.partial(enter_kernel, nrow, ncol, ndp, fold),
         out_shape=[
@@ -907,22 +916,24 @@
             jax.ShapeDtypeStruct((nrow, ncol, own, tokens), BF16),
             jax.ShapeDtypeStruct((ncol,) + ws.shape, BF16),
             jax.ShapeDtypeStruct((nrow, ncol) + ss.shape, BF16),
+            jax.ShapeDtypeStruct((nrow, ncol) + ts.shape, BF16),
         ],
-        in_specs=[ANYWHERE] * 4,
-        out_specs=[ANYWHERE] * 5,
+        in_specs=[ANYWHERE] * 5,
+        out_specs=[ANYWHERE] * 6,
         scratch_shapes=[
             pltpu.VMEM((own, tokens), BF16),
             pltpu.VMEM((own, 128), BF16),
             pltpu.VMEM((own, tokens), BF16),
             pltpu.VMEM((ws.shape[1] // 2, ws.shape[2]), BF16),
             pltpu.VMEM(ss.shape, BF16),
-            pltpu.SemaphoreType.DMA((20 * ncol + 8 + fold * fold,)),
+            pltpu.VMEM(ts.shape, BF16),
+            pltpu.SemaphoreType.DMA((24 * ncol + 8 + fold * fold,)),
             pltpu.SemaphoreType.DMA((slots,)),
-            pltpu.SemaphoreType.DMA((5,)),
+            pltpu.SemaphoreType.DMA((6,)),
         ],
         compiler_params=pltpu.CompilerParams(collective_id=0, has_side_effects=True),
         name="enter",
-    )(xs, cs, ws, ss)
+    )(xs, cs, ws, ss, ts)
 
 
 def shift_kernel(ncol, by, src, dst, buf, send, recv, local):
@@ -1183,7 +1194,6 @@
                 this = lax.rem(col, fold) == j
                 dst = ho.at[p, j, mine]
                 w.start(h1[p][j], src, dst, {"row": orow, "col": ocol}, away & this)
-                w.start(h2[p][j], src, dst, {"row": orow, "col": ocol, "dp": other}, this)
 
                 @pl.when(~away & this)
                 def _():
@@ -1194,12 +1204,16 @@
     for j in range(fold):
         srow, scol = col // fold, row * fold + j
         for p in range(count):
+            got = ho.at[p, j, mine]
 
             @pl.when((srow != row) | (scol != col))
             def _():
-                w.arrived(h1[p][j], ho.at[p, j, mine], {"row": srow, "col": scol})
-
-            w.arrived(h2[p][j], ho.at[p, j, theirs], {"row": srow, "col": scol, "dp": other})
+                w.arrived(h1[p][j], got, {"row": srow, "col": scol})
+
+            w.start(h2[p][j], got, got, {"dp": other})
+    for j in range(fold):
+        for p in range(count):
+            w.arrived(h2[p][j], ho.at[p, j, theirs], {"dp": other})
     for d in range(1, ncol):
         came = pl.ds(pl.multiple_of(from_col[d] * tokens, 128), tokens)
         w.arrived(c_[d], go.at[:, came], {"col": from_col[d]})
@@ -1415,7 +1429,7 @@
 
     block_heads = headparams.shape[1]
     xs, cs = inputs[0].T, cotangent[0].T
-    smalls = [pregain, innerconv, headparams, postgain, rateweight, stateweight]
+    smalls = [pregain, innerconv, headparams, postgain, rateweight]
     flat = jnp.concatenate([a.reshape(-1) for a in smalls])
     ss = jnp.pad(flat, (0, -flat.size % 2048)).reshape(-1, 128)
     sub = depth // fold
@@ -1430,7 +1444,7 @@
         1,
     ).reshape(fold, sub, 3 * sh)
 
-    x, xh, cot, weights, gathered = enter(nrow, ncol, ndp, fold, xs, cs, ws, ss)
+    x, xh, cot, weights, gathered, wstate = enter(nrow, ncol, ndp, fold, xs, cs, ws, ss, stateweight)
 
     if fold > 1:
         weights = weights.reshape(ncol, fold, sub, 3, sh).transpose(0, 2, 3, 1, 4)
@@ -1452,7 +1466,7 @@
     wrate = wrate.transpose(1, 3, 0, 2).reshape(total_heads, width)
     wrate = lax.dynamic_slice_in_dim(wrate, row * heads, heads, 0)
     wrate = jnp.pad(wrate, ((0, 16 - heads), (0, 0)))
-    wstate = parts[5].reshape(width, 2 * NSTATE)
+    wstate = wstate.reshape(width, 2 * NSTATE)
     sconv = stateconv.astype(F32)
     head = jnp.broadcast_to(
         jnp.concatenate([-jnp.exp(hp[0]), hp[1]])[:, None], (2 * heads, 128)
@@ -1476,7 +1490,7 @@
          out_sub((tokens, hl), F32), out_sub((tokens, ns2), F32), out_sub((tokens, ns2), BF16),
          out_lanes((4 * heads, tokens), F32),
          out_each((steps, NSTATE, hl), BF16), out_each((steps, 8, hl), F32),
-         out_whole((NSTATE, hl), F32), out_whole((8, hl), F32), out_whole((HALO, hl), BF16),
+         out_whole((NSTATE, hl), BF16), out_whole((8, hl), F32), out_whole((HALO, hl), BF16),
          out_whole((HALO, ns2), BF16), out_whole((HALO, 128), F32)],
         [pltpu.VMEM((GROUP + 8, hl + ns2), F32), pltpu.VMEM((NSTATE, hl), F32), pltpu.VMEM((8, hl), F32)],
         False,
@@ -1484,9 +1498,9 @@
         22,
     )
     total = total[0:1]
-    sin = shift(ncol, 1, fin.astype(BF16), 3).astype(F32)
+    sin = shift(ncol, 1, fin, 3)
     for _ in range(hops - 1):
-        sin = shift(ncol, 1, (fin + total * sin).astype(BF16), 3).astype(F32)
+        sin = shift(ncol, 1, (fin.astype(F32) + total * sin.astype(F32)).astype(BF16), 3)
 
     scan, out, dn, stat = call(
         fwd2_kernel,
@@ -1508,16 +1522,16 @@
         [sublanes(gate), sublanes(uv), sublanes(bc), lanes(rows), lanes(tok), sublanes(scan), sublanes(dn),
          lanes(scal), cot_in, whole(post), whole(skip), whole(spread)],
         [out_sub((tokens, hl), BF16), out_sub((tokens, hl), BF16), out_each((steps, NSTATE, hl), BF16),
-         out_each((steps, 8, hl), F32), out_whole((NSTATE, hl), F32), out_whole((width, hl), BF16),
+         out_each((steps, 8, hl), F32), out_whole((NSTATE, hl), BF16), out_whole((width, hl), BF16),
          out_whole((16, hl), F32), out_lanes((8, tokens), F32)],
         [pltpu.VMEM((NSTATE, hl), F32), pltpu.VMEM((8, hl), F32), pltpu.VMEM((width, hl), F32)],
         True,
         "bwd1",
         15,
     )
-    din = shift(ncol, -1, first.astype(BF16), 4).astype(F32)
+    din = shift(ncol, -1, first, 4)
     for _ in range(hops - 1):
-        din = shift(ncol, -1, (first + total * din).astype(BF16), 4).astype(F32)
+        din = shift(ncol, -1, (first.astype(F32) + total * din.astype(F32)).astype(BF16), 4)
 
     hs = sub // 2
     home, ghout, gin, ginh, gw, gs, gr, gk, gh, gp = call(

time: 427 us -> 411 us (0.963)
  Pallas kernels: 379 us -> 371 us
  other arithmetic: 21.6 us -> 15.1 us
    pallas_call x1, Pallas kernels: 110 us -> 102 us  [leave(): pl.pallas_call(functools.partial(leave_kernel, nrow, ncol, ndp, fold), ou...]
    convert_element_type x4 -> x0, other arithmetic: 6.51 us -> none  [the longest x2 3.26 us: local(): sin = shift(ncol, 1, fin.astype(BF16), 3).astype(F32)]
where the time goes in v3:
time: 411 us; the launch traced here: 409 us
  Pallas kernels  371 us (90%)
  local copies, waits for them, and re-layouts  21.7 us (5%)
  other arithmetic  15.1 us (4%)
    pallas_call x6, Pallas kernels, call(): pl.pallas_call(kernel, grid=(steps,), in_specs=[spec(*item[1:]) for item...  137 us
    pallas_call x1, Pallas kernels, enter(): pl.pallas_call(functools.partial(enter_kernel, nrow, ncol, ndp, fold), ou...  109 us
    pallas_call x1, Pallas kernels, leave(): pl.pallas_call(functools.partial(leave_kernel, nrow, ncol, ndp, fold), ou...  102 us
    pallas_call x2, Pallas kernels, shift(): pl.pallas_call(functools.partial(shift_kernel, ncol, by), out_shape=jax.S...  15.7 us

profile of v3, /device:TPU:6, one launch (start us, length us, event | category | flops | bytes accessed | tf_op | source)
XLA Modules:
  0.0 409.3 jit_solution(11119369632872340558)
XLA Ops:
  0.7 0.8 pad_dynamic-slice_fusion.15
  1.7 1.6 compare_convert_fusion
  4.9 1.3 copy.122
  6.7 0.9 maximum_bitcast_fusion.ws
  9.0 109.4 %enter.1 = (bf16[4,4,64,2048]{3,2,1,0:T(8,128)(2,1)}, bf16[4,4,64,128]{3,2,1,0:T(8,128)(2,1)}, bf16[4,4,64,2048]{3,2,1,0:T(8,128)(2,1)}, bf16[4,1,256,1536]{3,2,...) custom-call(bf16[64,8192]{1,0:T(8,128)(2,1)} %bitcast.122, ...), custom_call_target="tpu_custom_call" | custom-call | tf_op jit(solution)/shard_map/enter/pallas_call | solution.py:911
  118.4 0.9 reshape.254
  120.8 1.2 reshape.257
  124.0 1.0 broadcast_in_dim.33.gain_ref
  126.6 23.8 %fwd1.1 = (f32[2048,512]{1,0:T(8,128)}, f32[2048,512]{1,0:T(8,128)}, bf16[2048,256]{1,0:T(8,128)(2,1)}, f32[2048,512]{1,0:T(8,128)}, f32[2048,256]{1,0:T(8,128)}...) custom-call(bf16[1024,2048]{1,0:T(8,128)(2,1)} %bitcast.163, ...), custom_call_target="tpu_custom_call" | custom-call | flops 22000001024 | bytes 22000000 | tf_op jit(solution)/shard_map/fwd1/pallas_call | solution.py:1327
  150.4 7.3 %shift3.1.sin_ref = bf16[128,512]{1,0:T(8,128)(2,1)} custom-call(bf16[128,512]{1,0:T(8,128)(2,1)} %get-tuple-element.110.src), custom_call_target="tpu_custom_call" | custom-call | tf_op jit(solution)/shard_map/shift3/pallas_call | solution.py:977
  159.1 18.0 %fwd2.1 = (f32[2048,512]{1,0:T(8,128)}, bf16[4,256,2048]{2,1,0:T(8,128)(2,1)}, bf16[2048,512]{1,0:T(8,128)(2,1)}, f32[8,2048]{1,0:T(8,128)}) custom-call(f32[2048,512]{1,0:T(8,128)} %get-tuple-element.111.gate_ref, f32[2048,512]{1,0:T(8,128)} %get-tuple-element.104.uv_ref, bf16[2048,256]{1,0:T(8,128)(2,1)} %get-tuple-element.106.bc_ref, ...), custom_call_target="tpu_custom_call" | custom-call | flops 17999998976 | bytes 18000000 | tf_op jit(solution)/shard_map/fwd2/pallas_call | solution.py:1327
  177.1 6.6 %stat.1.scal_ref = f32[8,2048]{1,0:T(8,128)} custom-call(f32[8,2048]{1,0:T(8,128)} %get-tuple-element.115.stat), custom_call_target="tpu_custom_call" | custom-call | tf_op jit(solution)/shard_map/stat/pallas_call | solution.py:1014
  183.7 15.9 %bwd1.1 = (bf16[2048,512]{1,0:T(8,128)(2,1)}, bf16[2048,512]{1,0:T(8,128)(2,1)}, bf16[8,128,512]{2,1,0:T(8,128)(2,1)}, f32[8,8,512]{2,1,0:T(8,128)}, bf16[128,51...) custom-call(f32[2048,512]{1,0:T(8,128)} %get-tuple-element.111.gate_ref, ...), custom_call_target="tpu_custom_call" | custom-call | flops 15000000512 | bytes 15000000 | tf_op jit(solution)/shard_map/bwd1/pallas_call | solution.py:1327
  199.5 8.4 %shift4.1.din_ref = bf16[128,512]{1,0:T(8,128)(2,1)} custom-call(bf16[128,512]{1,0:T(8,128)(2,1)} %get-tuple-element.120.src), custom_call_target="tpu_custom_call" | custom-call | tf_op jit(solution)/shard_map/shift4/pallas_call | solution.py:977
  209.4 68.9 %bwd2.1 = (bf16[64,8192]{1,0:T(8,128)(2,1)}, bf16[1,256,512]{2,1,0:T(8,128)(2,1)}, bf16[4,256,2048]{2,1,0:T(8,128)(2,1)}, bf16[4,256,128]{2,1,0:T(8,128)(2,1)}, ...) custom-call(bf16[1024,2048]{1,0:T(8,128)(2,1)} %bitcast.164, ...), custom_call_target="tpu_custom_call" | custom-call | flops 49999998976 | bytes 50000000 | tf_op jit(solution)/shard_map/bwd2/pallas_call | solution.py:1327
  278.4 0.8 reduce_sum.69
  280.4 0.9 bitcast_reduce_fusion
  281.4 1.2 reduce_sum.67
  283.4 102.2 %leave.1 = (bf16[64,8192]{1,0:T(8,128)(2,1)}, bf16[4,64,128]{2,1,0:T(8,128)(2,1)}, bf16[2,1,256,512]{3,2,1,0:T(8,128)(2,1)}, f32[64,256]{1,0:T(8,128)}, f32[4,112,128]{2,1,0:T(8,128)}) custom-call(bf16[4,4,64,2048]{3,2,1,0:T(8,128)(2,1)} %bitcast.113, bf16[4,4,64,128]{3,2,1,0:T(8,128)(2,1)} %bitcast.139, bf16[4,2,128,1024]{3,2,1,0:T(8,128)(2,1)} %bitcast.116, ...), custom_call_target="tpu_custom_call" | custom-call | tf_op jit(solution)/shard_map/leave/pallas_call | solution.py:1237
  385.5 1.1 fusion.37
  387.5 1.1 pad_maximum_fusion.refs_0_
  388.6 0.8 copy.144
  389.5 5.9 %adam.1 = (f32[256,8,128]{2,1,0:T(8,128)}, f32[256,8,128]{2,1,0:T(8,128)}, f32[256,8,128]{2,1,0:T(8,128)}, f32[256,8,128]{2,1,0:T(8,128)}, f32[8,64,256]{2,1,0:T...) custom-call(bf16[256,8,128]{2,1,0:T(8,128)(2,1)} %pad_maximum_fusion.refs_0_, ...), custom_call_target="tpu_custom_call" | custom-call | flops 5000000000 | bytes 5000000 | tf_op jit(solution)/shard_map/adam/pallas_call | solution.py:1327
  396.2 4.9 %finish.1 = (f32[64,8192]{1,0:T(8,128)}, f32[64,8192]{1,0:T(8,128)}) custom-call(bf16[64,8192]{1,0:T(8,128)(2,1)} %bitcast.123, bf16[64,8192]{1,0:T(8,128)(2,1)} %bitcast.125, bf16[64,8192]{1,0:T(8,128)(2,1)} %get-tuple-element.124.r_ref, bf16[64,8192]{1,0:T(8,128)(2,1)} %get-tuple-element.134.g_ref, bf16[4,64,128]{2,1,0:T(8,128)(2,1)} %pad_maximum_fusion.1.h_ref), custom_call_target="tpu_custom_call" | custom-call | flops 5000000000 | bytes 5000000 | tf_op jit(solution)/shard_map/finish/pallas_call | solution.py:1327
  (180 shorter events, 22.9 us)
Async XLA Ops:
  0.7 5.9 %copy-start.1 = (bf16[8,64,256]{2,1,0:T(8,128)(2,1)S(1)}, bf16[8,64,256]{2,1,0:T(8,128)(2,1)}, u32[]{:S(2)}) copy-start(bf16[8,64,256]{2,1,0:T(8,128)(2,1)} %refs_7_.1) | copy-start | bytes 786436
  118.4 7.5 %copy-start.12 = (bf16[5,256]{1,0:T(8,128)(2,1)S(1)}, bf16[5,256]{1,0:T(8,128)(2,1)}, u32[]{:S(2)}) copy-start(bf16[5,256]{1,0:T(8,128)(2,1)} %param.38) | copy-start | bytes 7684
  183.7 24.3 %copy-start = (s32[1,8192]{1,0:T(1,128)S(1)}, s32[1,8192]{1,0:T(1,128)}, u32[]{:S(2)}) copy-start(s32[1,8192]{1,0:T(1,128)} %param.31) | copy-start | bytes 98308
  209.4 69.9 %copy-start.9 = (f32[16,512]{1,0:T(8,128)S(1)}, f32[16,512]{1,0:T(8,128)}, u32[]{:S(2)}) copy-start(f32[16,512]{1,0:T(8,128)} %get-tuple-element.133) | copy-start | bytes 98308
  389.5 5.9 %copy-start.6 = (bf16[4,64,128]{2,1,0:T(8,128)(2,1)S(1)}, bf16[4,64,128]{2,1,0:T(8,128)(2,1)}, u32[]{:S(2)}) copy-start(bf16[4,64,128]{2,1,0:T(8,128)(2,1)} %get-tuple-element.135) | copy-start | bytes 196612
  396.0 5.1 %copy-start.4 = (f32[4,112,128]{2,1,0:T(8,128)S(1)}, f32[4,112,128]{2,1,0:T(8,128)}, u32[]{:S(2)}) copy-start(f32[4,112,128]{2,1,0:T(8,128)} %get-tuple-element.138) | copy-start | bytes 688132
  396.0 5.3 %copy-start.15 = (f32[256,8]{0,1:T(8,128)S(1)}, f32[256,8]{0,1:T(8,128)}, u32[]{:S(2)}) copy-start(f32[256,8]{0,1:T(8,128)} %param.47) | copy-start | bytes 24580
  396.0 5.3 %copy-start.16 = (f32[256,8]{0,1:T(8,128)S(1)}, f32[256,8]{0,1:T(8,128)}, u32[]{:S(2)}) copy-start(f32[256,8]{0,1:T(8,128)} %param.46) | copy-start | bytes 24580
  396.0 6.1 %copy-start.19 = (f32[5,2,64]{2,1,0:T(2,128)S(1)}, f32[5,2,64]{2,1,0:T(2,128)}, u32[]{:S(2)}) copy-start(f32[5,2,64]{2,1,0:T(2,128)} %param.51) | copy-start | bytes 7684
  396.0 6.1 %copy-start.20 = (f32[5,2,64]{2,1,0:T(2,128)S(1)}, f32[5,2,64]{2,1,0:T(2,128)}, u32[]{:S(2)}) copy-start(f32[5,2,64]{2,1,0:T(2,128)} %param.50) | copy-start | bytes 7684
  396.0 6.9 %copy-start.23 = (f32[3,2]{0,1:T(2,128)S(1)}, f32[3,2]{0,1:T(2,128)}, u32[]{:S(2)}) copy-start(f32[3,2]{0,1:T(2,128)} %param.54) | copy-start | bytes 76
  396.0 7.0 %copy-start.24 = (f32[3,2]{0,1:T(2,128)S(1)}, f32[3,2]{0,1:T(2,128)}, u32[]{:S(2)}) copy-start(f32[3,2]{0,1:T(2,128)} %param.55) | copy-start | bytes 76
  396.1 9.8 %copy-start.17 = (f32[5,256]{1,0:T(8,128)S(1)}, f32[5,256]{1,0:T(8,128)}, u32[]{:S(2)}) copy-start(f32[5,256]{1,0:T(8,128)} %param.53) | copy-start | bytes 15364
  396.1 9.8 %copy-start.18 = (f32[5,256]{1,0:T(8,128)S(1)}, f32[5,256]{1,0:T(8,128)}, u32[]{:S(2)}) copy-start(f32[5,256]{1,0:T(8,128)} %param.52) | copy-start | bytes 15364
  396.1 10.6 %copy-start.25 = (f32[2,64]{1,0:T(2,128)S(1)}, f32[2,64]{1,0:T(2,128)}, u32[]{:S(2)}) copy-start(f32[2,64]{1,0:T(2,128)} %param.57) | copy-start | bytes 1540
  396.1 10.6 %copy-start.26 = (f32[2,64]{1,0:T(2,128)S(1)}, f32[2,64]{1,0:T(2,128)}, u32[]{:S(2)}) copy-start(f32[2,64]{1,0:T(2,128)} %param.56) | copy-start | bytes 1540
  396.1 11.2 %copy-start.28 = (f32[64]{0:T(128)S(1)}, f32[64]{0:T(128)}, u32[]{:S(2)}) copy-start(f32[64]{0:T(128)} %param.43) | copy-start | bytes 772
  396.1 11.2 %copy-start.29 = (f32[64]{0:T(128)S(1)}, f32[64]{0:T(128)}, u32[]{:S(2)}) copy-start(f32[64]{0:T(128)} %param.42) | copy-start | bytes 772
  396.1 11.8 %copy-start.3 = (f32[64,256]{1,0:T(8,128)S(1)}, f32[64,256]{1,0:T(8,128)}, u32[]{:S(2)}) copy-start(f32[64,256]{1,0:T(8,128)} %get-tuple-element.364) | copy-start | bytes 196612
  396.1 11.8 %copy-start.5 = (bf16[64,256]{1,0:T(8,128)(2,1)S(1)}, bf16[64,256]{1,0:T(8,128)(2,1)}, u32[]{:S(2)}) copy-start(bf16[64,256]{1,0:T(8,128)(2,1)} %ts.1) | copy-start | bytes 98308
  396.2 11.8 %copy-start.7 = (f32[64,256]{1,0:T(8,128)S(1)}, f32[64,256]{1,0:T(8,128)}, u32[]{:S(2)}) copy-start(f32[64,256]{1,0:T(8,128)} %param.49) | copy-start | bytes 196612
  396.2 11.8 %copy-start.8 = (f32[64,256]{1,0:T(8,128)S(1)}, f32[64,256]{1,0:T(8,128)}, u32[]{:S(2)}) copy-start(f32[64,256]{1,0:T(8,128)} %param.48) | copy-start | bytes 196612
  402.1 7.2 %copy-start.11 = (f32[5,2,64]{2,1,0:T(2,128)}, f32[5,2,64]{2,1,0:T(2,128)S(1)}, u32[]{:S(2)}) copy-start(f32[5,2,64]{2,1,0:T(2,128)S(1)} %reshape.286) | copy-start | bytes 7684
  405.8 3.5 copy-start.10
  (8 other events, 15.2 us)
